TPU v7x, 128 devices: a whole 4x4x4 slice. The times are simulated.
128 devices in a mesh: dp: 16 (over y, x), expert: 8 (over z, core).
Axes of the slice: x: 4, y: 4, z: 4, core: 2. Of those that a mesh axis runs over, the one named last changes fastest.
Arguments:
- tokens: bfloat16 [16384, 4096], P(('dp', 'expert')), may hold values from -6 to 6
- probs: bfloat16 [16384, 1], P(('dp', 'expert')), may hold values from 0.19921875 to 1
- routes: int32 [16384, 1], P(('dp', 'expert')), may hold values from 0 to 7; in each aligned block of 128 rows (0 to 127, 128 to 255, ...) at most 17 rows name the same one
- w_gate: bfloat16 [8, 4096, 1024], P('expert', 'dp'), may hold values from -0.09375 to 0.09375
- w_up: bfloat16 [8, 4096, 1024], P('expert', 'dp'), may hold values from -0.09375 to 0.09375
- w_down: bfloat16 [8, 1024, 4096], P('expert', None, 'dp'), may hold values from -0.1875 to 0.1875
- cotangent: bfloat16 [16384, 4096], P(('dp', 'expert')), may hold values from -6 to 6
Outputs:
- mixed: bfloat16 [16384, 4096], P(('dp', 'expert'))
- input_grad: bfloat16 [16384, 4096], P(('dp', 'expert'))
- grad_gate: bfloat16 [8, 4096, 1024], P('expert', 'dp')
- grad_up: bfloat16 [8, 4096, 1024], P('expert', 'dp')
- grad_down: bfloat16 [8, 1024, 4096], P('expert', None, 'dp')
Inputs may be any that keep to these rules, and one draw needn't show every extreme that they name: `routes`: each row names exactly one expert. Among the 128 rows of one device (aligned blocks), no expert is named more than 17 times, a bound that some block reaches.
All inputs are finite; a program needn't handle non-finite values.
Results may differ from a plain program's by a relative error of at most 0.025.
Values may be sent and summed in bfloat16 or wider, within the bound.
No kernel may reach another device: no remote copies, remote signals or barrier semaphores. Data moves between devices by JAX's collectives and lax.ppermute only.
A program may use at most 128 MiB of HBM per device.

v0:
```python
import jax
import jax.numpy as jnp
from jax import lax
from jax.sharding import Mesh
from jax.sharding import PartitionSpec as P

DP = ("dp_0", "dp_1")
DP_EXPERT = ("dp_0", "dp_1", "expert")


def cut_along(value, dim, devices):
    before, after = (value.shape[:dim], value.shape[dim + 1 :])
    return jnp.moveaxis(value.reshape(*before, devices, -1, *after), dim, 0)


def laid_out(tiles, dim):
    tiles = jnp.moveaxis(tiles, 0, dim)
    dims = tiles.shape
    return tiles.reshape(*dims[:dim], dims[dim] * dims[dim + 1], *dims[dim + 2 :])


def exchange_both(value, axis, axes, splits, concats):
    sizes = [lax.axis_size(a) for a in axes]
    tiles = cut_along(value, splits[0], sizes[0])
    tiles = jnp.moveaxis(cut_along(tiles, splits[1] + 1, sizes[1]), 0, 1)
    inside = tiles.shape[2:]
    tiles = tiles.reshape(-1, *inside)
    tiles = lax.all_to_all(tiles, axis, split_axis=0, concat_axis=0, tiled=True)
    tiles = laid_out(tiles.reshape(*sizes, *inside), concats[0] + 1)
    return laid_out(tiles, concats[1])


def summed_rows_2(terms, axes):
    total = terms.astype(jnp.bfloat16)
    for axis in axes:
        total = lax.psum_scatter(total, axis, scatter_dimension=0, tiled=True)
    return total.astype(jnp.float32)


def side_by_side(arrays, axis, dim, along):
    ends, at = ([], 0)
    for a in arrays[:-1]:
        at += a.shape[along]
        ends.append(at)
    both = jnp.concatenate(arrays, axis=along)
    return tuple(jnp.split(lax.all_gather(both, axis, axis=dim, tiled=True), ends, axis=along))


def slot_table(routes, experts_all, capacity):
    flat = routes.reshape(-1)
    hits = (flat[:, None] == jnp.arange(experts_all, dtype=jnp.int32)[None, :]).astype(jnp.int32)
    before = jnp.cumsum(hits, axis=0) - hits
    place = jnp.sum(before * hits, axis=1)
    target = flat * capacity + place
    table = jnp.arange(experts_all * capacity, dtype=jnp.int32)[:, None] == target[None, :]
    return table.astype(jnp.bfloat16)


def spread_rows(table, values, slices):
    shaped = values.reshape(values.shape[0], slices, values.shape[1] // slices)
    return jnp.einsum("st,tnk->nsk", table, shaped, preferred_element_type=jnp.float32).astype(
        jnp.bfloat16
    )


def to_rows(received, local_count):
    sources, slots, width = received.shape
    shaped = received.reshape(sources, local_count, slots // local_count, width)
    shaped = jnp.swapaxes(shaped, 1, 2)
    return shaped.reshape(sources * (slots // local_count), local_count, width)


def to_sources(rowwise, capacity):
    total, local_count, width = rowwise.shape
    shaped = rowwise.reshape(total // capacity, capacity, local_count, width)
    shaped = jnp.swapaxes(shaped, 1, 2)
    return shaped.reshape(total // capacity, local_count * capacity, width)


def collect(table, back, tok_rows, top):
    picked = jnp.einsum("st,nsk->tnk", table, back, preferred_element_type=jnp.float32)
    return picked.reshape(tok_rows, top, -1)


def per_device(tokens, probs, routes, w_gate, w_up, w_down, cotangent):
    local_count = w_gate.shape[0]
    n_dp = lax.axis_size(DP)
    n_exp = lax.axis_size("expert")
    experts_all = local_count * n_exp
    tok_rows, width = tokens.shape
    top = routes.shape[1]
    capacity = max(2, 17 * tok_rows * top // (16 * experts_all))
    blocks = n_dp * n_exp
    slot_width = width // n_dp
    table = slot_table(routes, experts_all, capacity)
    x_send = spread_rows(table, jnp.repeat(tokens, top, axis=0), n_dp)
    x_send = x_send.reshape(blocks, local_count * capacity, slot_width)
    weight = probs.astype(jnp.float32)
    scaled = (jnp.repeat(cotangent, top, axis=0).astype(jnp.float32) * weight).astype(jnp.bfloat16)
    x_got = lax.all_to_all(x_send, DP_EXPERT, split_axis=0, concat_axis=0, tiled=True)
    rows = to_rows(x_got, local_count)
    part = rows
    gate = jnp.einsum("red,edf->ref", part, w_gate, preferred_element_type=jnp.float32)
    upper = jnp.einsum("red,edf->ref", part, w_up, preferred_element_type=jnp.float32)
    summed = lax.psum_scatter(
        jnp.stack([gate, upper], axis=2).astype(jnp.bfloat16), DP, scatter_dimension=0, tiled=True
    ).astype(jnp.float32)
    gate_pre = summed[:, :, 0]
    up_value = summed[:, :, 1]
    sig = jax.nn.sigmoid(gate_pre)
    act = (gate_pre * sig * up_value).astype(jnp.bfloat16)
    act_all = lax.all_gather(act, DP, axis=0, tiled=True)
    result = jnp.einsum("ref,efd->red", act_all, w_down, preferred_element_type=jnp.float32).astype(
        jnp.bfloat16
    )
    outgoing = to_sources(result, capacity)
    sectioned = outgoing.reshape(n_dp, n_exp, local_count * capacity, slot_width)
    back = exchange_both(sectioned, DP_EXPERT, (DP, "expert"), (0, 1), (0, 1))
    back = back.reshape(n_dp, experts_all * capacity, slot_width)
    picked = collect(table, back, tok_rows, top)
    mixed = jnp.sum(picked * weight[..., None], axis=1).astype(jnp.bfloat16)
    dy_send = spread_rows(table, scaled, n_dp).reshape(blocks, local_count * capacity, slot_width)
    dy_got = lax.all_to_all(dy_send, DP_EXPERT, split_axis=0, concat_axis=0, tiled=True)
    dout = to_rows(dy_got, local_count)
    grad_down = jnp.einsum("ref,red->efd", act_all, dout, preferred_element_type=jnp.float32)
    part = dout
    dact = summed_rows_2(
        jnp.einsum("red,efd->ref", part, w_down, preferred_element_type=jnp.float32), DP
    )
    dgate = (dact * up_value * sig * (1.0 + gate_pre * (1.0 - sig))).astype(jnp.bfloat16)
    dup = (dact * gate_pre * sig).astype(jnp.bfloat16)
    dgate_all, dup_all = side_by_side((dgate, dup), DP, 0, 1)
    grad_gate = jnp.einsum("red,ref->edf", rows, dgate_all, preferred_element_type=jnp.float32)
    grad_up = jnp.einsum("red,ref->edf", rows, dup_all, preferred_element_type=jnp.float32)
    slot_grad = jnp.einsum(
        "ref,edf->red", dgate_all, w_gate, preferred_element_type=jnp.float32
    ) + jnp.einsum("ref,edf->red", dup_all, w_up, preferred_element_type=jnp.float32)
    slot_grad = slot_grad.astype(jnp.bfloat16)
    returned = lax.all_to_all(
        to_sources(slot_grad, capacity), DP_EXPERT, split_axis=0, concat_axis=0, tiled=True
    )
    returned = returned.reshape(n_dp, experts_all * capacity, slot_width)
    input_grad = jnp.sum(collect(table, returned, tok_rows, top), axis=1).astype(jnp.bfloat16)
    return (
        mixed,
        input_grad,
        grad_gate.astype(jnp.bfloat16),
        grad_up.astype(jnp.bfloat16),
        grad_down.astype(jnp.bfloat16),
    )


def solution(mesh):
    finer = Mesh(mesh.devices.reshape(4, 4, mesh.shape["expert"]), ("dp_0", "dp_1", "expert"))
    return jax.shard_map(
        per_device,
        mesh=finer,
        in_specs=(
            P(DP_EXPERT, None),
            P(DP_EXPERT, None),
            P(DP_EXPERT, None),
            P("expert", DP, None),
            P("expert", DP, None),
            P("expert", None, DP),
            P(DP_EXPERT, None),
        ),
        out_specs=(
            P(DP_EXPERT, None),
            P(DP_EXPERT, None),
            P("expert", DP, None),
            P("expert", DP, None),
            P("expert", None, DP),
        ),
        check_vma=False,
    )
```

profile of v0, /device:TPU:1, one launch (start us, length us, event | category | flops | bytes accessed | tf_op | source)
XLA Modules:
  0.0 452.7 jit_solution(14067609955037086214)
XLA Ops:
  11.2 1.5 multiply_convert_fusion
  13.6 35.9 %all_to_all.20 = bf16[128,17,256]{2,1,0:T(8,128)(2,1)} all-to-all(bf16[128,17,256]{2,1,0:T(8,128)(2,1)S(1)} %reshape.244), channel_id=1, replica_groups=mesh['dp_0'=4,'dp_1'=4,'expert'=8] {'dp_0','dp_1','expert'}, dimensions={0} | all-to-all | bytes 2228224 | tf_op jit(solution)/shard_map/all_to_all | solution.py:123
  49.5 2.3 reshape.245
  51.8 3.4 fusion.2
  55.4 1.1 copy-done.3
  57.4 30.8 %all_to_all.21 = bf16[128,17,256]{2,1,0:T(8,128)(2,1)} all-to-all(bf16[128,17,256]{2,1,0:T(8,128)(2,1)S(1)} %reshape.235), channel_id=1, replica_groups=mesh['dp_0'=4,'dp_1'=4,'expert'=8] {'dp_0','dp_1','expert'}, dimensions={0} | all-to-all | bytes 2228224 | tf_op jit(solution)/shard_map/all_to_all | solution.py:100
  88.2 2.4 reshape.236
  90.6 3.4 fusion
  94.0 3.5 fusion.1
  97.5 8.0 %pad_maximum_fusion = bf16[2176,1,2,1024]{3,0,2,1:T(8,128)(2,1)} fusion(bf16[2176,1,1,1024]{3,0,2,1:T(8,128)(2,1)} %fusion.1, bf16[2176,1,1,1024]{3,0,2,1:T(8,128)(2,1)} %fusion), kind=kLoop, calls=%fused_computation | loop fusion | flops 4456448 | bytes 17825792 | tf_op jit(solution)/shard_map/stack | solution.py:106
  105.5 11.9 %reduce-scatter.4.cloned.1.call-done = bf16[544,1,1024]{2,0,1:T(8,128)(2,1)} async-done(((bf16[2176,1,1024]{2,0,1:T(8,128)(2,1)}), bf16[544,1,1024]{2,0,1:T(8,128)(2,1)}) %reduce-scatter.4.cloned.1.call-update) | async-done | bytes 1114128 | tf_op jit(solution)/shard_map/reduce_scatter | solution.py:36
  118.7 139.2 %all-reduce.3.cloned.1.call-done = bf16[2176,1,2,1024]{3,0,2,1:T(8,128)(2,1)} async-done(((bf16[2176,1,2,1024]{3,0,2,1:T(8,128)(2,1)}), bf16[2176,1,2,1024]{3,0,2,1:T(8,128)(2,1)}) %all-reduce.3.cloned.1.call-update) | async-done | bytes 8912912
  257.9 1.2 dynamic-slice_convert_fusion
  259.1 2.0 fusion.37
  262.1 51.1 %all-gather.3.cloned.1.call-done = bf16[2176,1,1024]{2,0,1:T(8,128)(2,1)} async-done(((bf16[136,1,1024]{2,0,1:T(8,128)(2,1)}), bf16[2176,1,1024]{2,0,1:T(8,128)(2,1)}) %all-gather.3.cloned.1.call-update) | async-done | bytes 4456464 | tf_op jit(solution)/shard_map/all_gather | solution.py:112
  313.2 3.6 fusion.15
  316.7 1.4 reshape_transpose_transpose_reshape_reshape_reshape_reshape_transpose_reshape.3
  318.1 8.2 %all-to-all-start.1 = ((bf16[128,1,1,17,256]{4,3,2,1,0:T(8,128)(2,1)}), bf16[128,1,1,17,256]{4,3,2,1,0:T(8,128)(2,1)S(1)}, u32[]{:S(2)}, u32[]{:S(2)}) async-start(bf16[128,1,1,17,256]{4,3,2,1,0:T(8,128)(2,1)} %bitcast.158), calls=%async_computation.1 | async-start | bytes 3145728 | tf_op jit(solution)/shard_map/all_to_all | solution.py:28
  326.4 5.0 %fusion.26 = bf16[1,1024,256]{2,1,0:T(8,128)(2,1)} fusion(bf16[2176,256]{1,0:T(8,128)(2,1)} %copy-done.2, bf16[2176,1,1024]{2,0,1:T(8,128)(2,1)} %all-gather.3.cloned.1.call-done), kind=kOutput, calls=%fused_computation.32 | convolution fusion | flops 1141112832 | bytes 6094848 | tf_op jit(solution)/shard_map/ref,red->efd/dot_general | solution.py:125
  331.3 28.7 %all-to-all-done.1 = bf16[128,1,1,17,256]{4,3,2,1,0:T(8,128)(2,1)S(1)} async-done(((bf16[128,1,1,17,256]{4,3,2,1,0:T(8,128)(2,1)}), bf16[128,1,1,17,256]{4,3,2,1,0:T(8,128)(2,1)S(1)}, u32[]{:S(2)}, u32[]{:S(2)}) %all-to-all-start.1) | async-done | bytes 1114144 | tf_op jit(solution)/shard_map/all_to_all | solution.py:28
  360.5 1.5 copy.33
  362.0 40.7 %all-gather.5.cloned.1.call-done = bf16[2176,2,1024]{2,0,1:T(8,128)(2,1)} async-done(((bf16[136,2,1024]{2,0,1:T(8,128)(2,1)}), bf16[2176,2,1024]{2,0,1:T(8,128)(2,1)}) %all-gather.5.cloned.1.call-update) | async-done | bytes 8912912 | tf_op jit(solution)/shard_map/all_gather | solution.py:46
  402.7 3.8 fusion.9
  406.5 1.1 copy-done.8
  407.6 1.4 fusion.18
  408.9 1.4 reshape_transpose_reshape.2
  410.3 8.2 %all-to-all-start.3 = ((bf16[128,17,256]{2,1,0:T(8,128)(2,1)}), bf16[128,17,256]{2,1,0:T(8,128)(2,1)S(1)}, u32[]{:S(2)}, u32[]{:S(2)}) async-start(bf16[128,17,256]{2,1,0:T(8,128)(2,1)} %reshape_transpose_reshape.2), calls=%async_computation.5 | async-start | bytes 3145728 | tf_op jit(solution)/shard_map/all_to_all | solution.py:139
  418.5 2.7 fusion.3
  421.3 4.5 fusion.29
  425.7 4.5 fusion.30
  430.2 12.9 %all-to-all-done.3 = bf16[128,17,256]{2,1,0:T(8,128)(2,1)S(1)} async-done(((bf16[128,17,256]{2,1,0:T(8,128)(2,1)}), bf16[128,17,256]{2,1,0:T(8,128)(2,1)S(1)}, u32[]{:S(2)}, u32[]{:S(2)}) %all-to-all-start.3) | async-done | bytes 1114144 | tf_op jit(solution)/shard_map/all_to_all | solution.py:139
  443.7 1.5 convolution_convert_fusion.3
  (44 shorter events, 7.7 us)
Async XLA Ops:
  8.0 43.8 %copy-start = (bf16[1,1024,256]{2,1,0:T(8,128)(2,1)S(1)}, bf16[1,1024,256]{2,1,0:T(8,128)(2,1)}, u32[]{:S(2)}) copy-start(bf16[1,1024,256]{2,1,0:T(8,128)(2,1)} %param.12) | copy-start | bytes 1572868
  8.0 109.4 %reduce-scatter.4.cloned.1.call-start = ((), (), s32[]{:S(2)}) async-start(), calls=%async_computation.7 | async-start | bytes 5570560 | tf_op jit(solution)/shard_map/reduce_scatter | solution.py:36
  51.8 3.5 copy-start.2
  55.3 1.2 copy-start.3
  55.3 202.6 %all-reduce.3.cloned.1.call-start = ((), (), s32[]{:S(2)}) async-start(), calls=%async_computation.10 | async-start | bytes 17825792
  88.2 2.4 copy-start.4
  90.6 3.4 copy-start.6
  105.4 12.1 %copy-start.9 = (u32[128]{0:T(128)S(1)}, u32[128]{0:T(128)}, u32[]{:S(2)}) copy-start(u32[128]{0:T(128)} %constant.16) | copy-start | bytes 1540
  105.5 153.6 %reduce-scatter.6.cloned.1.call-start = ((), (), s32[]{:S(2)}) async-start(), calls=%async_computation.8 | async-start | bytes 1392640 | tf_op jit(solution)/shard_map/reduce_scatter | solution.py:36
  117.4 195.7 %all-gather.3.cloned.1.call-start = ((), (), s32[]{:S(2)}) async-start(), calls=%async_computation.6 | async-start | bytes 4734976 | tf_op jit(solution)/shard_map/all_gather | solution.py:112
  261.1 141.6 %all-gather.5.cloned.1.call-start = ((), (), s32[]{:S(2)}) async-start(), calls=%async_computation.9 | async-start | bytes 9469952 | tf_op jit(solution)/shard_map/all_gather | solution.py:46
  318.1 41.9 %all-to-all-start.1 = ((bf16[128,1,1,17,256]{4,3,2,1,0:T(8,128)(2,1)}), bf16[128,1,1,17,256]{4,3,2,1,0:T(8,128)(2,1)S(1)}, u32[]{:S(2)}, u32[]{:S(2)}) async-start(bf16[128,1,1,17,256]{4,3,2,1,0:T(8,128)(2,1)} %bitcast.158), calls=%async_computation.1 | async-start | bytes 3145728 | tf_op jit(solution)/shard_map/all_to_all | solution.py:28
  360.3 42.4 %copy-start.5 = (bf16[1,256,1024]{2,1,0:T(8,128)(2,1)S(1)}, bf16[1,256,1024]{2,1,0:T(8,128)(2,1)}, u32[]{:S(2)}) copy-start(bf16[1,256,1024]{2,1,0:T(8,128)(2,1)} %param.10) | copy-start | bytes 1572868
  362.0 44.5 %copy-start.7 = (bf16[1,256,1024]{2,1,0:T(8,128)(2,1)S(1)}, bf16[1,256,1024]{2,1,0:T(8,128)(2,1)}, u32[]{:S(2)}) copy-start(bf16[1,256,1024]{2,1,0:T(8,128)(2,1)} %param.11) | copy-start | bytes 1572868
  402.7 4.9 %copy-start.8 = (bf16[2176,2,1024]{2,0,1:T(8,128)(2,1)S(1)}, bf16[2176,2,1024]{2,0,1:T(8,128)(2,1)}, u32[]{:S(2)}) copy-start(bf16[2176,2,1024]{2,0,1:T(8,128)(2,1)} %all-gather.5.cloned.1.call-done) | copy-start | bytes 26738692
  410.3 32.8 %all-to-all-start.3 = ((bf16[128,17,256]{2,1,0:T(8,128)(2,1)}), bf16[128,17,256]{2,1,0:T(8,128)(2,1)S(1)}, u32[]{:S(2)}, u32[]{:S(2)}) async-start(bf16[128,17,256]{2,1,0:T(8,128)(2,1)} %reshape_transpose_reshape.2), calls=%async_computation.5 | async-start | bytes 3145728 | tf_op jit(solution)/shard_map/all_to_all | solution.py:139
  443.5 1.6 copy-start.1
Sparse Core Ops, SparseCore 0:
  55.4 61.9 reduce-scatter.3
  119.8 34.0 reduce-scatter.5
Sparse Core Ops, SparseCore 1:
  105.5 152.3 all-reduce.2
  261.2 51.9 all-gather.2
  315.8 86.9 all-gather.4
where the time goes:
time: 453 us
  waiting for transfers between devices  285 us (63%)
  blocking collectives  66.8 us (15%)
  matrix products  38 us (8%)
  starting transfers between devices  16.7 us (4%)
  other arithmetic  16.6 us (4%)
  between operations  16.6 us (4%)
  local copies, waits for them, and re-layouts  13.6 us (3%)
    unnamed x6, waiting for transfers between devices  139 us
    all_gather x1, waiting for transfers between devices, per_device(): act_all = lax.all_gather(act, DP, axis=0, tiled=True)  51.1 us
    all_gather x1, waiting for transfers between devices, side_by_side(): lax.all_gather(both, axis, axis=dim, tiled=True)  40.7 us
    all_to_all x1, blocking collectives, per_device(): lax.all_to_all(dy_send, DP_EXPERT, split_axis=0, concat_axis=0, tiled=True)  35.9 us
    all_to_all x1, blocking collectives, per_device(): lax.all_to_all(x_send, DP_EXPERT, split_axis=0, concat_axis=0, tiled=True)  30.8 us
    all_to_all x1, waiting for transfers between devices, exchange_both(): tiles = lax.all_to_all(tiles, axis, split_axis=0, concat_axis=0, tiled=True)  28.7 us
    all_to_all x1, waiting for transfers between devices, per_device(): lax.all_to_all(to_sources(slot_grad, capacity), DP_EXPERT, split_axis=0,...  12.9 us
    reduce_scatter x2, waiting for transfers between devices, summed_rows_2(): total = lax.psum_scatter(total, axis, scatter_dimension=0, tiled=True)  11.9 us
  transfers between devices with their start and end apart: 7, of which 6 were waited for; matrix products, arithmetic and copies ran while one was open for 10% of the time, Pallas kernels for 0%

commit v1 on v0

v1 whole, which is shorter than its diff:
```python
import jax
import jax.numpy as jnp
from jax import lax
from jax.experimental import pallas as pl
from jax.experimental.pallas import tpu as pltpu
from jax.sharding import Mesh
from jax.sharding import PartitionSpec as P

AXES = ("y", "x", "z", "c")
BF = jnp.bfloat16
F32 = jnp.float32
SIDE = 4
TOK = 128
BLK = 256
FF = 1024
SLOT = 36
PAIR = 2 * SLOT
SHARE = SIDE * SLOT
SENT = SIDE * PAIR
ROWS = SIDE * SHARE
WIDE = SIDE * BLK


def place(y, x, z, c):
    return ((y * SIDE + x) * SIDE + z) * 2 + c


def groups():
    n = range(SIDE)
    feature, copies, spread = [], [], []
    for k in n:
        for z in n:
            feature.append([place(k, x, z, 0) for x in n])
            feature.append([place(y, k, z, 1) for y in n])
            copies.append([place(y, k, z, 0) for y in n])
            copies.append([place(k, x, z, 1) for x in n])
        spread.append([place(k, x, z, 0) for x in n for z in n])
        spread.append([place(y, k, z, 1) for y in n for z in n])
    return feature, copies, spread


FEATURE, COPIES, SPREAD = groups()


def shifted(value, rings, step):
    pairs = [(g[(i + step) % SIDE], g[i]) for g in rings for i in range(SIDE)]
    return lax.ppermute(value, AXES, pairs)


def grouped(value, rings):
    return lax.all_to_all(value, AXES, 0, 0, axis_index_groups=rings, tiled=True)


def other_core(value):
    return lax.ppermute(value, "c", [(0, 1), (1, 0)])


def iota(shape, dim):
    return lax.broadcasted_iota(jnp.int32, shape, dim)


def dot(a, b):
    return jnp.dot(a, b, preferred_element_type=F32)


def dot_nt(a, b):
    return lax.dot_general(a, b, (((1,), (1,)), ((), ())), preferred_element_type=F32)


def dot_tn(a, b):
    return lax.dot_general(a, b, (((0,), (0,)), ((), ())), preferred_element_type=F32)


def call(body, outs, scratch=(), smem=1, n_in=0):
    specs = [pl.BlockSpec(memory_space=pltpu.SMEM)] * smem + [pl.BlockSpec(memory_space=pltpu.VMEM)] * n_in
    return pl.pallas_call(
        body,
        out_shape=outs,
        in_specs=specs,
        out_specs=jax.tree.map(lambda _: pl.BlockSpec(memory_space=pltpu.VMEM), outs),
        scratch_shapes=list(scratch),
        compiler_params=pltpu.CompilerParams(vmem_limit_bytes=56 * 2**20),
    )


def column(kind, near, group, k):
    turned = (near + k) % SIDE
    return jnp.where(kind == 0, turned * SIDE + group, group * SIDE + turned)


def row_targets(route_row, kind):
    count = route_row.shape[1]
    hits = (iota((8, count), 0) == route_row).astype(F32)
    earlier = (iota((count, count), 0) < iota((count, count), 1)).astype(BF)
    before = dot(hits.astype(BF), earlier)
    slot = jnp.sum(before * hits, axis=0, keepdims=True).astype(jnp.int32)
    return jnp.where(route_row % 2 == kind, (route_row // 2) * PAIR + slot, -PAIR)


def row_targets_t(route_col, kind):
    count = route_col.shape[0]
    hits = (iota((count, 8), 1) == route_col).astype(F32)
    earlier = (iota((count, count), 1) < iota((count, count), 0)).astype(BF)
    before = dot(earlier, hits.astype(BF))
    slot = jnp.sum(before * hits, axis=1, keepdims=True).astype(jnp.int32)
    return jnp.where(route_col % 2 == kind, (route_col // 2) * PAIR + slot, -PAIR)


def pack_body(pos, route, prob, tok_a, tok_b, cot_a, cot_b, out):
    kind, near = pos[0], pos[1]
    target = row_targets(route[...], kind)
    rows = iota((SENT, 2 * TOK), 0)
    pick_x = (rows == target).astype(BF)
    pick_y = (rows == target + SLOT).astype(BF)
    weight = prob[...]
    for d in range(SIDE):
        for k in range(SIDE):
            at = pl.ds(pl.multiple_of(column(kind, near, d, k) * BLK, BLK), BLK)
            x = jnp.concatenate([tok_a[:, at], tok_b[:, at]], axis=0)
            y = jnp.concatenate([cot_a[:, at], cot_b[:, at]], axis=0).astype(F32)
            y = (y * weight).astype(BF)
            out[d, :, k * BLK : (k + 1) * BLK] = (dot(pick_x, x) + dot(pick_y, y)).astype(BF)


def project_body(pos, got, w0, w1, w2, w3, part, x_out, y_out):
    at = pos[2]
    q, r = iota((SHARE, SENT), 0), iota((SHARE, SENT), 1)
    home = q + (q // SLOT) * SLOT
    take_x = (r == home).astype(BF)
    take_y = (r == home + SLOT).astype(BF)
    for k in range(SIDE):
        rows = got[(at + k) % SIDE]
        x_out[k * SHARE : (k + 1) * SHARE, :] = dot(take_x, rows).astype(BF)
        y_out[k * SHARE : (k + 1) * SHARE, :] = dot(take_y, rows).astype(BF)
    for t, left in enumerate((x_out, x_out, y_out)):
        for n in range(FF // BLK):
            cols = slice(n * BLK, (n + 1) * BLK)
            total = None
            for k, w in enumerate((w0, w1, w2, w3)):
                term = dot(left[:, k * BLK : (k + 1) * BLK], w[t * BLK : (t + 1) * BLK, cols])
                total = term if total is None else total + term
            total = total.astype(BF)
            for k in range(SIDE):
                part[(at + k) % SIDE, :, t * FF + n * BLK : t * FF + (n + 1) * BLK] = total[
                    k * SHARE : (k + 1) * SHARE
                ]


def activate_body(terms, out):
    for n in range(FF // BLK):
        def summed(t):
            cols = slice(t * FF + n * BLK, t * FF + (n + 1) * BLK)
            return sum(terms[s, :, cols].astype(F32) for s in range(SIDE))

        gate, upper, dact = summed(0), summed(1), summed(2)
        sig = jax.nn.sigmoid(gate)
        act = gate * sig * upper
        dgate = dact * upper * sig * (1.0 + gate * (1.0 - sig))
        dup = dact * gate * sig
        for t, v in enumerate((act, dgate, dup)):
            out[:, t * FF + n * BLK : t * FF + (n + 1) * BLK] = v.astype(BF)


def return_body(pos, a0, a1, a2, a3, w0, w1, w2, w3, back, acts, res, slot):
    at = pos[2]
    for k, a in enumerate((a0, a1, a2, a3)):
        acts[k * SHARE : (k + 1) * SHARE, :] = a[...]
    for k, w in enumerate((w0, w1, w2, w3)):
        cols = slice(k * BLK, (k + 1) * BLK)
        res[:, cols] = dot_nt(acts[:, 0:FF], w[2 * BLK : 3 * BLK, :]).astype(BF)
        grad = dot_nt(acts[:, FF : 2 * FF], w[0:BLK, :]) + dot_nt(acts[:, 2 * FF : 3 * FF], w[BLK : 2 * BLK, :])
        slot[:, cols] = grad.astype(BF)
    r, q = iota((SENT, SHARE), 0), iota((SENT, SHARE), 1)
    home = q + (q // SLOT) * SLOT
    give_m = (r == home).astype(BF)
    give_s = (r == home + SLOT).astype(BF)
    for k in range(SIDE):
        rows = slice(k * SHARE, (k + 1) * SHARE)
        back[(at + k) % SIDE] = (dot(give_m, res[rows, :]) + dot(give_s, slot[rows, :])).astype(BF)


def grads_body(x, y, acts, g0, g1, g2, g3):
    for k, g in enumerate((g0, g1, g2, g3)):
        cols = slice(k * BLK, (k + 1) * BLK)
        g[0:BLK, :] = dot_tn(x[:, cols], acts[:, FF : 2 * FF]).astype(BF)
        g[BLK : 2 * BLK, :] = dot_tn(x[:, cols], acts[:, 2 * FF : 3 * FF]).astype(BF)
        g[2 * BLK : 3 * BLK, :] = dot_tn(y[:, cols], acts[:, 0:FF]).astype(BF)


def unpack_body(pos, route_a, route_b, prob, own, oth, mixed, grad):
    kind, near, across = pos[0], pos[1], pos[2]
    mine = row_targets_t(jnp.concatenate([route_a[...], route_b[...]], axis=0), kind)[0:TOK]
    theirs = row_targets_t(jnp.concatenate([route_b[...], route_a[...]], axis=0), 1 - kind)[TOK:]
    rows = iota((TOK, SENT), 1)
    own_m, own_s = (rows == mine).astype(BF), (rows == mine + SLOT).astype(BF)
    oth_m, oth_s = (rows == theirs).astype(BF), (rows == theirs + SLOT).astype(BF)
    weight = prob[...]
    for b in range(SIDE * SIDE):
        major, minor = b // SIDE, b % SIDE
        own_d = jnp.where(kind == 0, minor, major)
        own_k = (jnp.where(kind == 0, major, minor) - near + SIDE) % SIDE
        oth_d = jnp.where(kind == 0, major, minor)
        oth_k = (jnp.where(kind == 0, minor, major) - across + SIDE) % SIDE
        o = own[own_d, :, pl.ds(pl.multiple_of(own_k * BLK, BLK), BLK)]
        t = oth[oth_d, :, pl.ds(pl.multiple_of(oth_k * BLK, BLK), BLK)]
        cols = slice(b * BLK, (b + 1) * BLK)
        mixed[:, cols] = ((dot(own_m, o) + dot(oth_m, t)) * weight).astype(BF)
        grad[:, cols] = (dot(own_s, o) + dot(oth_s, t)).astype(BF)


def total_body(g0, g1, g2, g3, gate, upper, down):
    def total(t):
        rows = slice(t * BLK, (t + 1) * BLK)
        return sum(g[rows, :].astype(F32) for g in (g0, g1, g2, g3))

    gate[...] = total(0).astype(BF)
    upper[...] = total(1).astype(BF)
    down[...] = jnp.transpose(total(2)).astype(BF)


def per_device(tokens, probs, routes, w_gate, w_up, w_down, cotangent):
    shape = lambda *dims: jax.ShapeDtypeStruct(dims, BF)
    y, x, c = lax.axis_index("y"), lax.axis_index("x"), lax.axis_index("c")
    pos = jnp.stack([c, jnp.where(c == 0, y, x), jnp.where(c == 0, x, y)]).astype(jnp.int32)
    weights = jnp.concatenate([w_gate[0], w_up[0], w_down[0].T], axis=0)
    ws = [weights] + [shifted(weights, COPIES, k) for k in (1, 2, 3)]
    prob = probs.astype(F32)
    tok_b, cot_b = other_core(tokens), other_core(cotangent)
    route_b, prob_b = other_core(routes), other_core(probs).astype(F32)
    route_row = jnp.concatenate([routes, route_b], axis=0).reshape(1, 2 * TOK)
    sent = call(pack_body, shape(SIDE, SENT, WIDE), n_in=6)(
        pos, route_row, jnp.concatenate([prob, prob_b], axis=0), tokens, tok_b, cotangent, cot_b
    )
    got = grouped(sent.reshape(SIDE * SIDE, PAIR, WIDE), SPREAD).reshape(SIDE, SENT, WIDE)
    part, rows_x, rows_y = call(
        project_body, [shape(SIDE, SHARE, 3 * FF), shape(ROWS, WIDE), shape(ROWS, WIDE)], n_in=5
    )(pos, got, *ws)
    terms = grouped(part, FEATURE)
    acts = call(activate_body, shape(SHARE, 3 * FF), smem=0, n_in=1)(terms)
    act_s = [acts] + [shifted(acts, FEATURE, k) for k in (1, 2, 3)]
    back, acts_all = call(
        return_body,
        [shape(SIDE, SENT, WIDE), shape(ROWS, 3 * FF)],
        scratch=[pltpu.VMEM((ROWS, WIDE), BF), pltpu.VMEM((ROWS, WIDE), BF)],
        n_in=8,
    )(pos, *act_s, *ws)
    own = grouped(back.reshape(SIDE * SIDE, PAIR, WIDE), SPREAD).reshape(SIDE, SENT, WIDE)
    gs = call(grads_body, [shape(3 * BLK, FF)] * SIDE, smem=0, n_in=3)(rows_x, rows_y, acts_all)
    gs = [gs[0]] + [shifted(gs[k], COPIES, -k) for k in (1, 2, 3)]
    oth = other_core(own)
    mixed, grad = call(unpack_body, [shape(TOK, SIDE * WIDE), shape(TOK, SIDE * WIDE)], n_in=5)(
        pos, routes, route_b, prob, own, oth
    )
    gate, upper, down = call(
        total_body, [shape(BLK, FF), shape(BLK, FF), shape(FF, BLK)], smem=0, n_in=4
    )(*gs)
    return mixed, grad, gate[None], upper[None], down[None]


def solution(mesh):
    finer = Mesh(mesh.devices.reshape(SIDE, SIDE, SIDE, 2), AXES)
    rows = P(AXES, None)
    wide = P(("z", "c"), ("y", "x"), None)
    tall = P(("z", "c"), None, ("y", "x"))
    return jax.shard_map(
        per_device,
        mesh=finer,
        in_specs=(rows, rows, rows, wide, wide, tall, rows),
        out_specs=(rows, rows, wide, wide, tall),
        check_vma=False,
    )
```

time: 453 us -> 253 us (0.56)
  waiting for transfers between devices: 285 us -> 103 us
  Pallas kernels: 0 us -> 51.4 us
  matrix products: 38 us -> 0 us
  between operations: 16.6 us -> 0.76 us
  other arithmetic: 16.6 us -> 2.65 us
  starting transfers between devices: 16.7 us -> 25.2 us
  blocking collectives: 66.8 us -> 60.5 us
  local copies, waits for them, and re-layouts: 13.6 us -> 9.06 us
    unnamed x6 -> x0, waiting for transfers between devices: 139 us -> none
    ppermute x0 -> x14, waiting for transfers between devices: none -> 103 us  [the longest x9 102 us: shifted(): return lax.ppermute(value, AXES, pairs)]
    all_gather x2 -> x0, waiting for transfers between devices: 91.8 us -> none  [the longest x1 51.1 us: per_device(): act_all = lax.all_gather(act, DP, axis=0, tiled=True)]
    pallas_call x0 -> x7, Pallas kernels: none -> 51.4 us  [the longest x1 11.4 us: per_device(): call(return_body, [shape(SIDE, SENT, WIDE), shape(ROWS, 3 * FF)], scratch...]
    all_to_all x2 -> x1, waiting for transfers between devices: 41.5 us -> 0.01 us  [grouped(): lax.all_to_all(value, AXES, 0, 0, axis_index_groups=rings, tiled=True)]
    dot_general x13 -> x0, matrix products: 38 us -> none  [the longest x1 4.99 us: per_device(): jnp.einsum('ref,red->efd', act_all, dout, preferred_element_type=jnp.floa...]
    ppermute x0 -> x14, starting transfers between devices: none -> 17.2 us  [the longest x9 12.1 us: shifted(): return lax.ppermute(value, AXES, pairs)]
    reduce_scatter x2 -> x0, waiting for transfers between devices: 11.9 us -> none  [summed_rows_2(): total = lax.psum_scatter(total, axis, scatter_dimension=0, tiled=True)]
  transfers between devices with their start and end apart: 7 -> 15, of which waited for: 6 -> 7; matrix products, arithmetic and copies ran while one was open for 10% -> 2% of each run, Pallas kernels for 0% -> 6%
where the time goes in v1:
time: 253 us; the launch traced here: 252 us
  waiting for transfers between devices  103 us (41%)
  blocking collectives  60.5 us (24%)
  Pallas kernels  51.4 us (20%)
  starting transfers between devices  25.2 us (10%)
  local copies, waits for them, and re-layouts  9.06 us (4%)
  other arithmetic  2.65 us (1%)
    ppermute x9, waiting for transfers between devices, shifted(): return lax.ppermute(value, AXES, pairs)  102 us
    all_to_all x2, blocking collectives, grouped(): lax.all_to_all(value, AXES, 0, 0, axis_index_groups=rings, tiled=True)  60.5 us
    ppermute x9, starting transfers between devices, shifted(): return lax.ppermute(value, AXES, pairs)  12.1 us
    pallas_call x1, Pallas kernels, per_device(): call(return_body, [shape(SIDE, SENT, WIDE), shape(ROWS, 3 * FF)], scratch...  11.4 us
    pallas_call x1, Pallas kernels, per_device(): call(project_body, [shape(SIDE, SHARE, 3 * FF), shape(ROWS, WIDE), shape(...  10.6 us
    pallas_call x1, Pallas kernels, per_device(): call(grads_body, [shape(3 * BLK, FF)] * SIDE, smem=0, n_in=3)  9.06 us
    unnamed x39, local copies, waits for them, and re-layouts  9.01 us
    all_to_all x1, starting transfers between devices, grouped(): lax.all_to_all(value, AXES, 0, 0, axis_index_groups=rings, tiled=True)  8.07 us
  transfers between devices with their start and end apart: 15, of which 7 were waited for; matrix products, arithmetic and copies ran while one was open for 2% of the time, Pallas kernels for 6%

profile of v1, /device:TPU:1, one launch (start us, length us, event | category | flops | bytes accessed | tf_op | source)
XLA Modules:
  0.0 252.4 jit_solution(6129968152391359728)
XLA Ops:
  0.6 1.5 collective-permute-start.2
  2.2 0.8 copy.32
  3.5 0.8 copy.36.route_a
  5.0 1.1 collective-permute-done.1
  6.9 1.2 add_bitcast_fusion.route
  8.1 1.0 copy-done.7
  9.1 1.0 copy-done.8
  10.1 5.3 %shard_map.110 = bf16[4,288,1024]{2,1,0:T(8,128)(2,1)} custom-call(s32[3]{0:T(128)} %pad_add_fusion.pos, s32[1,256]{1,0:T(1,128)} %add_bitcast_fusion.route, f32[256,1]{1,0:T(8,128)} %pad_maximum_fusion.1.prob, bf16[128,4096]{1,0:T(8,128)(2,1)} %tok_a.1, bf16[128,4096]{1,0:T(8,128)(2,1)} %copy-done.7, bf16[128,4096]{1,0:T(8,128)(2,1)} %cot_a.1, ...), custom_call_target="tpu_custom_call" | custom-call | tf_op jit(solution)/shard_map/pallas_call | solution.py:231
  15.4 8.1 %all-to-all-start = ((bf16[16,72,1024]{2,1,0:T(8,128)(2,1)}), bf16[16,72,1024]{2,1,0:T(8,128)(2,1)}, u32[]{:S(2)}, u32[]{:S(2)}) async-start(bf16[16,72,1024]{2,1,0:T(8,128)(2,1)} %bitcast.19), calls=%async_computation | async-start | bytes 4718592 | tf_op jit(solution)/shard_map/all_to_all | solution.py:51
  23.9 1.3 collective-permute-start.6
  25.2 2.4 collective-permute-start.5
  27.6 1.2 collective-permute-start.4
  28.8 46.7 %collective-permute-done.6.w3 = bf16[768,1024]{1,0:T(8,128)(2,1)S(1)} collective-permute-done((bf16[768,1024]{1,0:T(8,128)(2,1)S(1)}, bf16[768,1024]{1,0:T(8,128)(2,1)S(1)}, u32[]{:S(2)}, u32[]{:S(2)}) %collective-permute-start.6) | collective-permute-done | bytes 1572896 | tf_op jit(solution)/shard_map/ppermute | solution.py:47
  75.4 1.2 copy-done.3
  77.2 10.6 %shard_map.111 = (bf16[4,144,3072]{2,1,0:T(8,128)(2,1)}, bf16[576,1024]{1,0:T(8,128)(2,1)}, bf16[576,1024]{1,0:T(8,128)(2,1)}) custom-call(s32[3]{0:T(128)} %pad_add_fusion.pos, bf16[4,288,1024]{2,1,0:T(8,128)(2,1)} %bitcast.5.got, bf16[768,1024]{1,0:T(8,128)(2,1)} %copy-done, bf16[768,1024]{1,0:T(8,128)(2,1)} %collective-permute-done.4.w1, ...), custom_call_target="tpu_custom_call" | custom-call | tf_op jit(solution)/shard_map/pallas_call | solution.py:235
  87.8 28.9 %all_to_all.15.terms = bf16[4,144,3072]{2,1,0:T(8,128)(2,1)} all-to-all(bf16[4,144,3072]{2,1,0:T(8,128)(2,1)} %get-tuple-element.19), channel_id=1, replica_groups={{0,8,16,24},{1,33,65,97},{2,10,18,26},{3,35,67,99},{4,12,20,28},{5,37,6..., dimensions={0} | all-to-all | bytes 7077888 | tf_op jit(solution)/shard_map/all_to_all | solution.py:51
  116.7 3.6 %shard_map.112.a0 = bf16[144,3072]{1,0:T(8,128)(2,1)} custom-call(bf16[4,144,3072]{2,1,0:T(8,128)(2,1)} %all_to_all.15.terms), custom_call_target="tpu_custom_call" | custom-call | tf_op jit(solution)/shard_map/pallas_call | solution.py:239
  120.3 1.8 collective-permute-start.8
  122.1 0.9 collective-permute-start.7
  123.0 20.4 %collective-permute-done.9.a3 = bf16[144,3072]{1,0:T(8,128)(2,1)S(1)} collective-permute-done((bf16[144,3072]{1,0:T(8,128)(2,1)}, bf16[144,3072]{1,0:T(8,128)(2,1)S(1)}, u32[]{:S(2)}, u32[]{:S(2)}) %collective-permute-start.9) | collective-permute-done | bytes 884768 | tf_op jit(solution)/shard_map/ppermute | solution.py:47
  144.7 0.9 copy-done.11
  145.6 11.4 %shard_map.113 = (bf16[4,288,1024]{2,1,0:T(8,128)(2,1)}, bf16[576,3072]{1,0:T(8,128)(2,1)}) custom-call(s32[3]{0:T(128)} %pad_add_fusion.pos, bf16[144,3072]{1,0:T(8,128)(2,1)} %shard_map.112.a0, bf16[144,3072]{1,0:T(8,128)(2,1)} %copy-done.11, bf16[144,3072]{1,0:T(8,128)(2,1)} %copy-done.10, bf16[144,3072]{1,0:T(8,128)(2,1)} %copy-done.9, ...), custom_call_target="tpu_custom_call" | custom-call | tf_op jit(solution)/shard_map/pallas_call | solution.py:241
  157.0 31.5 %all_to_all.16 = bf16[16,72,1024]{2,1,0:T(8,128)(2,1)S(1)} all-to-all(bf16[16,72,1024]{2,1,0:T(8,128)(2,1)} %bitcast.20), channel_id=1, replica_groups={{0,2,4,6,8,10,12,14,16,18,20,22,24,26,28,30},{1,3,5,7,33,35,37,39,65,67..., dimensions={0} | all-to-all | bytes 4718592 | tf_op jit(solution)/shard_map/all_to_all | solution.py:51
  188.5 2.8 %collective-permute-start.10 = (bf16[4,288,1024]{2,1,0:T(8,128)(2,1)S(1)}, bf16[4,288,1024]{2,1,0:T(8,128)(2,1)S(1)}, u32[]{:S(2)}, u32[]{:S(2)}) collective-permute-start(bf16[4,288,1024]{2,1,0:T(8,128)(2,1)S(1)} %bitcast.17), channel_id=1, source_target_pairs={{0,1},{1,0},{2,3},{3,2},{4,5},{5,4},{6,7},{7,6},{8,9},{9,8},{10,11... | collective-permute-start | bytes 7077896 | tf_op jit(solution)/shard_map/ppermute | solution.py:55
  191.3 9.1 %shard_map.115 = (bf16[768,1024]{1,0:T(8,128)(2,1)}, bf16[768,1024]{1,0:T(8,128)(2,1)}, bf16[768,1024]{1,0:T(8,128)(2,1)}, bf16[768,1024]{1,0:T(8,128)(2,1)}) custom-call(bf16[576,1024]{1,0:T(8,128)(2,1)} %get-tuple-element.23.x, bf16[576,1024]{1,0:T(8,128)(2,1)} %get-tuple-element.24.y, bf16[576,3072]{1,0:T(8,128)(2,1)} %get-tuple-element.25.acts), custom_call_target="tpu_custom_call" | custom-call | tf_op jit(solution)/shard_map/pallas_call | solution.py:248
  200.4 2.8 %collective-permute-start.12 = (bf16[768,1024]{1,0:T(8,128)(2,1)}, bf16[768,1024]{1,0:T(8,128)(2,1)S(1)}, u32[]{:S(2)}, u32[]{:S(2)}) collective-permute-start(bf16[768,1024]{1,0:T(8,128)(2,1)} %get-tuple-element.28), channel_id=1, source_target_pairs={{64,0},{96,32},{0,64},{32,96},{17,1},{25,9},{1,17},{9,25},{66,2},{... | collective-permute-start | bytes 4718600 | tf_op jit(solution)/shard_map/ppermute | solution.py:47
  203.2 1.8 collective-permute-start.13
  205.0 16.4 %collective-permute-done.11.g1 = bf16[768,1024]{1,0:T(8,128)(2,1)S(1)} collective-permute-done((bf16[768,1024]{1,0:T(8,128)(2,1)}, bf16[768,1024]{1,0:T(8,128)(2,1)S(1)}, u32[]{:S(2)}, u32[]{:S(2)}) %collective-permute-start.11) | collective-permute-done | bytes 1572896 | tf_op jit(solution)/shard_map/ppermute | solution.py:47
  221.4 17.0 %collective-permute-done.12.g2 = bf16[768,1024]{1,0:T(8,128)(2,1)S(1)} collective-permute-done((bf16[768,1024]{1,0:T(8,128)(2,1)}, bf16[768,1024]{1,0:T(8,128)(2,1)S(1)}, u32[]{:S(2)}, u32[]{:S(2)}) %collective-permute-start.12) | collective-permute-done | bytes 1572896 | tf_op jit(solution)/shard_map/ppermute | solution.py:47
  239.5 4.9 %shard_map.116 = (bf16[256,1024]{1,0:T(8,128)(2,1)}, bf16[256,1024]{1,0:T(8,128)(2,1)}, bf16[1024,256]{1,0:T(8,128)(2,1)}) custom-call(bf16[768,1024]{1,0:T(8,128)(2,1)} %get-tuple-element.26.g0, bf16[768,1024]{1,0:T(8,128)(2,1)} %copy-done.5, bf16[768,1024]{1,0:T(8,128)(2,1)} %copy-done.6, bf16[768,1024]{1,0:T(8,128)(2,1)} %collective-permute-done.13.g3), custom_call_target="tpu_custom_call" | custom-call | tf_op jit(solution)/shard_map/pallas_call | solution.py:254
  244.4 1.4 copy-done.4
  245.8 6.6 %shard_map.114 = (bf16[128,4096]{1,0:T(8,128)(2,1)}, bf16[128,4096]{1,0:T(8,128)(2,1)}) custom-call(s32[3]{0:T(128)} %pad_add_fusion.pos, s32[128,1]{1,0:T(8,128)} %copy-done.16, s32[128,1]{1,0:T(8,128)} %copy-done.17, f32[128,1]{1,0:T(8,128)} %copy-done.12, bf16[4,288,1024]{2,1,0:T(8,128)(2,1)} %bitcast.18, bf16[4,288,1024]{2,1,0:T(8,128)(2,1)} %copy-done.4), custom_call_target="tpu_custom_call" | custom-call | tf_op jit(solution)/shard_map/pallas_call | solution.py:251
  (53 shorter events, 5.5 us)
Async XLA Ops:
  0.6 7.5 %collective-permute-start.2 = (bf16[128,4096]{1,0:T(8,128)(2,1)}, bf16[128,4096]{1,0:T(8,128)(2,1)S(1)}, u32[]{:S(2)}, u32[]{:S(2)}) collective-permute-start(bf16[128,4096]{1,0:T(8,128)(2,1)} %tok_a.1), channel_id=1, source_target_pairs={{0,1},{1,0},{2,3},{3,2},{4,5},{5,4},{6,7},{7,6},{8,9},{9,8},{10,11... | collective-permute-start | bytes 3145736 | tf_op jit(solution)/shard_map/ppermute | solution.py:55
  2.1 6.0 %collective-permute-start.3 = (bf16[128,4096]{1,0:T(8,128)(2,1)}, bf16[128,4096]{1,0:T(8,128)(2,1)S(1)}, u32[]{:S(2)}, u32[]{:S(2)}) collective-permute-start(bf16[128,4096]{1,0:T(8,128)(2,1)} %cot_a.1), channel_id=1, source_target_pairs={{0,1},{1,0},{2,3},{3,2},{4,5},{5,4},{6,7},{7,6},{8,9},{9,8},{10,11... | collective-permute-start | bytes 3145736 | tf_op jit(solution)/shard_map/ppermute | solution.py:55
  3.0 3.2 %collective-permute-start.1 = (bf16[128,1]{1,0:T(8,128)(2,1)S(1)}, bf16[128,1]{1,0:T(8,128)(2,1)S(1)}, u32[]{:S(2)}, u32[]{:S(2)}) collective-permute-start(bf16[128,1]{1,0:T(8,128)(2,1)S(1)} %copy.32), channel_id=1, source_target_pairs={{0,1},{1,0},{2,3},{3,2},{4,5},{5,4},{6,7},{7,6},{8,9},{9,8},{10,11... | collective-permute-start | bytes 776 | tf_op jit(solution)/shard_map/ppermute | solution.py:55
  4.2 11.2 %copy-start.16 = (s32[128,1]{1,0:T(8,128)}, s32[128,1]{1,0:T(8,128)S(1)}, u32[]{:S(2)}) copy-start(s32[128,1]{1,0:T(8,128)S(1)} %copy.36.route_a) | copy-start | bytes 1540
  4.2 2.6 %collective-permute-start = (s32[128,1]{1,0:T(8,128)S(1)}, s32[128,1]{1,0:T(8,128)S(1)}, u32[]{:S(2)}, u32[]{:S(2)}) collective-permute-start(s32[128,1]{1,0:T(8,128)S(1)} %copy.36.route_a), channel_id=1, source_target_pairs={{0,1},{1,0},{2,3},{3,2},{4,5},{5,4},{6,7},{7,6},{8,9},{9,8},{10,11... | collective-permute-start | bytes 1544 | tf_op jit(solution)/shard_map/ppermute | solution.py:55
  5.0 10.4 %copy-start.12 = (f32[128,1]{1,0:T(8,128)}, f32[128,1]{1,0:T(8,128)S(1)}, u32[]{:S(2)}) copy-start(f32[128,1]{1,0:T(8,128)S(1)} %convert_element_type.6.prob) | copy-start | bytes 1540
  6.8 8.6 %copy-start.17 = (s32[128,1]{1,0:T(8,128)}, s32[128,1]{1,0:T(8,128)S(1)}, u32[]{:S(2)}) copy-start(s32[128,1]{1,0:T(8,128)S(1)} %collective-permute-done.route_b) | copy-start | bytes 1540
  8.1 1.0 copy-start.7
  9.1 1.0 copy-start.8
  15.4 8.1 %copy-start.13 = (bf16[1,1024,256]{2,1,0:T(8,128)(2,1)S(1)}, bf16[1,1024,256]{2,1,0:T(8,128)(2,1)}, u32[]{:S(2)}) copy-start(bf16[1,1024,256]{2,1,0:T(8,128)(2,1)} %param.12) | copy-start | bytes 1572868
  15.4 8.3 %copy-start.14 = (bf16[1,256,1024]{2,1,0:T(8,128)(2,1)S(1)}, bf16[1,256,1024]{2,1,0:T(8,128)(2,1)}, u32[]{:S(2)}) copy-start(bf16[1,256,1024]{2,1,0:T(8,128)(2,1)} %param.11) | copy-start | bytes 1572868
  15.4 8.3 %copy-start.15 = (bf16[1,256,1024]{2,1,0:T(8,128)(2,1)S(1)}, bf16[1,256,1024]{2,1,0:T(8,128)(2,1)}, u32[]{:S(2)}) copy-start(bf16[1,256,1024]{2,1,0:T(8,128)(2,1)} %param.10) | copy-start | bytes 1572868
  15.4 61.2 %all-to-all-start = ((bf16[16,72,1024]{2,1,0:T(8,128)(2,1)}), bf16[16,72,1024]{2,1,0:T(8,128)(2,1)}, u32[]{:S(2)}, u32[]{:S(2)}) async-start(bf16[16,72,1024]{2,1,0:T(8,128)(2,1)} %bitcast.19), calls=%async_computation | async-start | bytes 4718592 | tf_op jit(solution)/shard_map/all_to_all | solution.py:51
  23.9 52.7 %copy-start = (bf16[768,1024]{1,0:T(8,128)(2,1)}, bf16[768,1024]{1,0:T(8,128)(2,1)S(1)}, u32[]{:S(2)}) copy-start(bf16[768,1024]{1,0:T(8,128)(2,1)S(1)} %pad_maximum_fusion.w0) | copy-start | bytes 4718596
  23.9 51.5 %collective-permute-start.6 = (bf16[768,1024]{1,0:T(8,128)(2,1)S(1)}, bf16[768,1024]{1,0:T(8,128)(2,1)S(1)}, u32[]{:S(2)}, u32[]{:S(2)}) collective-permute-start(bf16[768,1024]{1,0:T(8,128)(2,1)S(1)} %pad_maximum_fusion.w0), channel_id=1, source_target_pairs={{96,0},{0,32},{32,64},{64,96},{25,1},{1,9},{9,17},{17,25},{98,2},{... | collective-permute-start | bytes 4718600 | tf_op jit(solution)/shard_map/ppermute | solution.py:47
  25.2 50.3 %collective-permute-start.5 = (bf16[768,1024]{1,0:T(8,128)(2,1)S(1)}, bf16[768,1024]{1,0:T(8,128)(2,1)S(1)}, u32[]{:S(2)}, u32[]{:S(2)}) collective-permute-start(bf16[768,1024]{1,0:T(8,128)(2,1)S(1)} %pad_maximum_fusion.w0), channel_id=1, source_target_pairs={{64,0},{96,32},{0,64},{32,96},{17,1},{25,9},{1,17},{9,25},{66,2},{... | collective-permute-start | bytes 4718600 | tf_op jit(solution)/shard_map/ppermute | solution.py:47
  27.6 49.0 %collective-permute-start.4 = (bf16[768,1024]{1,0:T(8,128)(2,1)S(1)}, bf16[768,1024]{1,0:T(8,128)(2,1)}, u32[]{:S(2)}, u32[]{:S(2)}) collective-permute-start(bf16[768,1024]{1,0:T(8,128)(2,1)S(1)} %pad_maximum_fusion.w0), channel_id=1, source_target_pairs={{32,0},{64,32},{96,64},{0,96},{9,1},{17,9},{25,17},{1,25},{34,2},{... | collective-permute-start | bytes 4718600 | tf_op jit(solution)/shard_map/ppermute | solution.py:47
  75.4 1.8 copy-start.2
  75.4 1.2 copy-start.3
  120.3 23.1 %collective-permute-start.9 = (bf16[144,3072]{1,0:T(8,128)(2,1)}, bf16[144,3072]{1,0:T(8,128)(2,1)S(1)}, u32[]{:S(2)}, u32[]{:S(2)}) collective-permute-start(bf16[144,3072]{1,0:T(8,128)(2,1)} %shard_map.112.a0), channel_id=1, source_target_pairs={{24,0},{0,8},{8,16},{16,24},{97,1},{1,33},{33,65},{65,97},{26,2},{... | collective-permute-start | bytes 2654216 | tf_op jit(solution)/shard_map/ppermute | solution.py:47
  120.3 23.1 %collective-permute-start.8 = (bf16[144,3072]{1,0:T(8,128)(2,1)}, bf16[144,3072]{1,0:T(8,128)(2,1)S(1)}, u32[]{:S(2)}, u32[]{:S(2)}) collective-permute-start(bf16[144,3072]{1,0:T(8,128)(2,1)} %shard_map.112.a0), channel_id=1, source_target_pairs={{16,0},{24,8},{0,16},{8,24},{65,1},{97,33},{1,65},{33,97},{18,2},{... | collective-permute-start | bytes 2654216 | tf_op jit(solution)/shard_map/ppermute | solution.py:47
  122.1 21.9 %collective-permute-start.7 = (bf16[144,3072]{1,0:T(8,128)(2,1)}, bf16[144,3072]{1,0:T(8,128)(2,1)S(1)}, u32[]{:S(2)}, u32[]{:S(2)}) collective-permute-start(bf16[144,3072]{1,0:T(8,128)(2,1)} %shard_map.112.a0), channel_id=1, source_target_pairs={{8,0},{16,8},{24,16},{0,24},{33,1},{65,33},{97,65},{1,97},{10,2},{... | collective-permute-start | bytes 2654216 | tf_op jit(solution)/shard_map/ppermute | solution.py:47
  143.4 0.9 copy-start.9
  143.4 1.3 copy-start.10
  188.5 11.9 %copy-start.1 = (bf16[16,72,1024]{2,1,0:T(8,128)(2,1)}, bf16[16,72,1024]{2,1,0:T(8,128)(2,1)S(1)}, u32[]{:S(2)}) copy-start(bf16[16,72,1024]{2,1,0:T(8,128)(2,1)S(1)} %all_to_all.16) | copy-start | bytes 7077892
  188.5 55.9 %collective-permute-start.10 = (bf16[4,288,1024]{2,1,0:T(8,128)(2,1)S(1)}, bf16[4,288,1024]{2,1,0:T(8,128)(2,1)S(1)}, u32[]{:S(2)}, u32[]{:S(2)}) collective-permute-start(bf16[4,288,1024]{2,1,0:T(8,128)(2,1)S(1)} %bitcast.17), channel_id=1, source_target_pairs={{0,1},{1,0},{2,3},{3,2},{4,5},{5,4},{6,7},{7,6},{8,9},{9,8},{10,11... | collective-permute-start | bytes 7077896 | tf_op jit(solution)/shard_map/ppermute | solution.py:55
  200.4 21.0 %collective-permute-start.11 = (bf16[768,1024]{1,0:T(8,128)(2,1)}, bf16[768,1024]{1,0:T(8,128)(2,1)S(1)}, u32[]{:S(2)}, u32[]{:S(2)}) collective-permute-start(bf16[768,1024]{1,0:T(8,128)(2,1)} %get-tuple-element.27), channel_id=1, source_target_pairs={{96,0},{0,32},{32,64},{64,96},{25,1},{1,9},{9,17},{17,25},{98,2},{... | collective-permute-start | bytes 4718600 | tf_op jit(solution)/shard_map/ppermute | solution.py:47
  200.4 38.0 %collective-permute-start.12 = (bf16[768,1024]{1,0:T(8,128)(2,1)}, bf16[768,1024]{1,0:T(8,128)(2,1)S(1)}, u32[]{:S(2)}, u32[]{:S(2)}) collective-permute-start(bf16[768,1024]{1,0:T(8,128)(2,1)} %get-tuple-element.28), channel_id=1, source_target_pairs={{64,0},{96,32},{0,64},{32,96},{17,1},{25,9},{1,17},{9,25},{66,2},{... | collective-permute-start | bytes 4718600 | tf_op jit(solution)/shard_map/ppermute | solution.py:47
  203.2 35.8 %collective-permute-start.13 = (bf16[768,1024]{1,0:T(8,128)(2,1)}, bf16[768,1024]{1,0:T(8,128)(2,1)}, u32[]{:S(2)}, u32[]{:S(2)}) collective-permute-start(bf16[768,1024]{1,0:T(8,128)(2,1)} %get-tuple-element.29), channel_id=1, source_target_pairs={{32,0},{64,32},{96,64},{0,96},{9,1},{17,9},{25,17},{1,25},{34,2},{... | collective-permute-start | bytes 4718600 | tf_op jit(solution)/shard_map/ppermute | solution.py:47
  221.4 17.6 %copy-start.5 = (bf16[768,1024]{1,0:T(8,128)(2,1)}, bf16[768,1024]{1,0:T(8,128)(2,1)S(1)}, u32[]{:S(2)}) copy-start(bf16[768,1024]{1,0:T(8,128)(2,1)S(1)} %collective-permute-done.11.g1) | copy-start | bytes 4718596
  238.3 1.1 copy-start.6
  244.4 1.4 copy-start.4
  (1 other events, 0.9 us)

commit v2 on v1

v2 whole, which is shorter than its diff:
```python
import jax
import jax.numpy as jnp
from jax import lax
from jax.experimental import pallas as pl
from jax.experimental.pallas import tpu as pltpu
from jax.sharding import Mesh
from jax.sharding import PartitionSpec as P


AXES = ("y", "x", "z", "c")
BF = jnp.bfloat16
F32 = jnp.float32
SIDE = 4
TOK = 128
BLK = 256
FF = 1024
SLOT = 36
PAIR = 2 * SLOT
SHARE = SIDE * SLOT
SENT = SIDE * PAIR
ROWS = SIDE * SHARE
WIDE = SIDE * BLK


def place(y, x, z, c):
    return ((y * SIDE + x) * SIDE + z) * 2 + c


def groups():
    n = range(SIDE)
    feature, copies, spread = [], [], []
    for k in n:
        for z in n:
            feature.append([place(k, x, z, 0) for x in n])
            feature.append([place(y, k, z, 1) for y in n])
            copies.append([place(y, k, z, 0) for y in n])
            copies.append([place(k, x, z, 1) for x in n])
        spread.append([place(k, x, z, 0) for x in n for z in n])
        spread.append([place(y, k, z, 1) for y in n for z in n])
    return feature, copies, spread


FEATURE, COPIES, SPREAD = groups()


def shifted(value, rings, step):
    pairs = [(g[(i + step) % SIDE], g[i]) for g in rings for i in range(SIDE)]
    return lax.ppermute(value, AXES, pairs)


def grouped(value, rings):
    return lax.all_to_all(value, AXES, 0, 0, axis_index_groups=rings, tiled=True)


def other_core(value):
    return lax.ppermute(value, "c", [(0, 1), (1, 0)])


def iota(shape, dim):
    return lax.broadcasted_iota(jnp.int32, shape, dim)


def dot(a, b):
    return jnp.dot(a, b, preferred_element_type=F32)


def dot_nt(a, b):
    return lax.dot_general(a, b, (((1,), (1,)), ((), ())), preferred_element_type=F32)


def call(body, outs, args, scratch=(), smem=1, limit=16, hbm=False):
    near = pl.BlockSpec(memory_space=pltpu.VMEM)
    small, large = args[:smem], args[smem:]
    large = [pltpu.with_memory_space_constraint(a, pltpu.VMEM) for a in large]
    place_out = jax.ShapeDtypeStruct if hbm else pltpu.VMEM
    return pl.pallas_call(
        body,
        out_shape=[place_out(dims, BF) for dims in outs],
        in_specs=[pl.BlockSpec(memory_space=pltpu.SMEM)] * smem + [near] * len(large),
        out_specs=[near] * len(outs),
        scratch_shapes=[pltpu.VMEM(dims, BF) for dims in scratch],
        compiler_params=pltpu.CompilerParams(vmem_limit_bytes=limit * 2**20),
    )(*small, *large)


def column(kind, near, group, k):
    turned = (near + k) % SIDE
    return jnp.where(kind == 0, turned * SIDE + group, group * SIDE + turned)


def row_targets(route, kind):
    count = route.shape[0]
    hits = (iota((count, 8), 1) == route).astype(F32)
    earlier = (iota((count, count), 1) < iota((count, count), 0)).astype(BF)
    slot = jnp.sum(dot(earlier, hits.astype(BF)) * hits, axis=1, keepdims=True).astype(jnp.int32)
    return jnp.where(route % 2 == kind, (route // 2) * PAIR + slot, -PAIR)


def routes_of(*metas):
    return jnp.concatenate([m[:, 0:1] for m in metas], axis=0).astype(F32).astype(jnp.int32)


def pack_body(pos, meta_a, meta_b, tok_a, tok_b, cot_a, cot_b, out):
    kind, near = pos[0], pos[1]
    target = row_targets(routes_of(meta_a, meta_b), kind)
    rows = iota((2 * TOK, SENT), 1)
    pick_x = jnp.transpose((rows == target).astype(F32)).astype(BF)
    pick_y = jnp.transpose((rows == target + SLOT).astype(F32)).astype(BF)
    weight = jnp.concatenate([meta_a[:, 1:2], meta_b[:, 1:2]], axis=0).astype(F32)
    for d in range(SIDE):
        for k in range(SIDE):
            at = pl.ds(pl.multiple_of(column(kind, near, d, k) * BLK, BLK), BLK)
            x = jnp.concatenate([tok_a[:, at], tok_b[:, at]], axis=0)
            y = jnp.concatenate([cot_a[:, at], cot_b[:, at]], axis=0).astype(F32)
            y = (y * weight).astype(BF)
            out[d, :, k * BLK : (k + 1) * BLK] = (dot(pick_x, x) + dot(pick_y, y)).astype(BF)


def project_body(pos, got, w0, w1, w2a, w2b, w3, part, x_out, y_out, w2):
    at = pos[2]
    half = w2a.shape[0]
    w2[0:half, :] = w2a[...]
    w2[half:, :] = w2b[...]
    q, r = iota((SHARE, SENT), 0), iota((SHARE, SENT), 1)
    home = q + (q // SLOT) * SLOT
    take_x = (r == home).astype(BF)
    take_y = (r == home + SLOT).astype(BF)
    for k in range(SIDE):
        rows = got[(at + k) % SIDE]
        x_out[k * SHARE : (k + 1) * SHARE, :] = dot(take_x, rows).astype(BF)
        y_out[k * SHARE : (k + 1) * SHARE, :] = dot(take_y, rows).astype(BF)
    for t, left in enumerate((x_out, x_out, y_out)):
        for n in range(FF // BLK):
            cols = slice(n * BLK, (n + 1) * BLK)
            total = sum(
                dot(left[:, k * BLK : (k + 1) * BLK], w[t * BLK : (t + 1) * BLK, cols])
                for k, w in enumerate((w0, w1, w2, w3))
            ).astype(BF)
            for k in range(SIDE):
                part[(at + k) % SIDE, :, t * FF + n * BLK : t * FF + (n + 1) * BLK] = total[
                    k * SHARE : (k + 1) * SHARE
                ]


def activate_body(terms, out):
    for n in range(FF // BLK):
        def summed(t):
            cols = slice(t * FF + n * BLK, t * FF + (n + 1) * BLK)
            return sum(terms[s, :, cols].astype(F32) for s in range(SIDE))

        gate, upper, dact = summed(0), summed(1), summed(2)
        sig = jax.nn.sigmoid(gate)
        act = gate * sig * upper
        dgate = dact * upper * sig * (1.0 + gate * (1.0 - sig))
        dup = dact * gate * sig
        for t, v in enumerate((act, dgate, dup)):
            out[:, t * FF + n * BLK : t * FF + (n + 1) * BLK] = v.astype(BF)


def turn_body(x, y, xt, yt):
    for src, dst in ((x, xt), (y, yt)):
        for k in range(SIDE):
            cols = slice(k * BLK, (k + 1) * BLK)
            dst[cols, :] = jnp.transpose(src[:, cols].astype(F32)).astype(BF)


def block_grads(k, xt, yt, acts):
    cols = slice(k * BLK, (k + 1) * BLK)
    return (
        dot(xt[cols, :], acts[:, FF : 2 * FF]),
        dot(xt[cols, :], acts[:, 2 * FF : 3 * FF]),
        dot(yt[cols, :], acts[:, 0:FF]),
    )


def far_grads_body(xt, yt, a0, a1, a2, a3, acts, top, low):
    for k, a in enumerate((a0, a1, a2, a3)):
        acts[k * SHARE : (k + 1) * SHARE, :] = a[...]
    gate, upper, down = block_grads(2, xt, yt, acts)
    half = BLK // 2
    top[0:BLK, :] = gate.astype(BF)
    top[BLK : BLK + half, :] = upper[0:half].astype(BF)
    low[0:half, :] = upper[half:].astype(BF)
    low[half:, :] = down.astype(BF)


def near_grads_body(xt, yt, acts, top, low, g0, g1, g3):
    half = BLK // 2
    for t, v in enumerate(block_grads(0, xt, yt, acts)):
        g0[t * BLK : (t + 1) * BLK, :] = v.astype(BF)
    gate, upper, down = block_grads(1, xt, yt, acts)
    g1[0:BLK, :] = (gate + top[0:BLK, :].astype(F32)).astype(BF)
    g1[BLK : BLK + half, :] = (upper[0:half] + top[BLK:, :].astype(F32)).astype(BF)
    g1[BLK + half : 2 * BLK, :] = upper[half:].astype(BF)
    g1[2 * BLK :, :] = down.astype(BF)
    gate, upper, down = block_grads(3, xt, yt, acts)
    g3[0:BLK, :] = gate.astype(BF)
    g3[BLK : BLK + half, :] = upper[0:half].astype(BF)
    g3[BLK + half : 2 * BLK, :] = (upper[half:] + low[0:half, :].astype(F32)).astype(BF)
    g3[2 * BLK :, :] = (down + low[half:, :].astype(F32)).astype(BF)


def return_body(pos, acts, w0, w1, w2, w3, back, res, slot):
    at = pos[2]
    for k, w in enumerate((w0, w1, w2, w3)):
        cols = slice(k * BLK, (k + 1) * BLK)
        res[:, cols] = dot_nt(acts[:, 0:FF], w[2 * BLK : 3 * BLK, :]).astype(BF)
        grad = dot_nt(acts[:, FF : 2 * FF], w[0:BLK, :]) + dot_nt(acts[:, 2 * FF : 3 * FF], w[BLK : 2 * BLK, :])
        slot[:, cols] = grad.astype(BF)
    r, q = iota((SENT, SHARE), 0), iota((SENT, SHARE), 1)
    home = q + (q // SLOT) * SLOT
    give_m = (r == home).astype(BF)
    give_s = (r == home + SLOT).astype(BF)
    for k in range(SIDE):
        rows = slice(k * SHARE, (k + 1) * SHARE)
        back[(at + k) % SIDE] = (dot(give_m, res[rows, :]) + dot(give_s, slot[rows, :])).astype(BF)


def unpack_body(pos, meta_a, meta_b, own, oth, mixed, grad):
    kind, near, across = pos[0], pos[1], pos[2]
    mine = row_targets(routes_of(meta_a, meta_b), kind)[0:TOK]
    theirs = row_targets(routes_of(meta_b, meta_a), 1 - kind)[TOK:]
    rows = iota((TOK, SENT), 1)
    own_m, own_s = (rows == mine).astype(BF), (rows == mine + SLOT).astype(BF)
    oth_m, oth_s = (rows == theirs).astype(BF), (rows == theirs + SLOT).astype(BF)
    weight = meta_a[:, 1:2].astype(F32)
    for b in range(SIDE * SIDE):
        major, minor = b // SIDE, b % SIDE
        own_d = jnp.where(kind == 0, minor, major)
        own_k = (jnp.where(kind == 0, major, minor) - near + SIDE) % SIDE
        oth_d = jnp.where(kind == 0, major, minor)
        oth_k = (jnp.where(kind == 0, minor, major) - across + SIDE) % SIDE
        o = own[own_d, :, pl.ds(pl.multiple_of(own_k * BLK, BLK), BLK)]
        t = oth[oth_d, :, pl.ds(pl.multiple_of(oth_k * BLK, BLK), BLK)]
        cols = slice(b * BLK, (b + 1) * BLK)
        mixed[:, cols] = ((dot(own_m, o) + dot(oth_m, t)) * weight).astype(BF)
        grad[:, cols] = (dot(own_s, o) + dot(oth_s, t)).astype(BF)


def total_body(g0, g1, g3, gate, upper, down):
    def total(t):
        rows = slice(t * BLK, (t + 1) * BLK)
        return sum(g[rows, :].astype(F32) for g in (g0, g1, g3))

    gate[...] = total(0).astype(BF)
    upper[...] = total(1).astype(BF)
    down[...] = jnp.transpose(total(2)).astype(BF)


def layer(tokens, probs, routes, w_gate, w_up, w_down, cotangent):
    y, x, c = lax.axis_index("y"), lax.axis_index("x"), lax.axis_index("c")
    pos = jnp.stack([c, jnp.where(c == 0, y, x), jnp.where(c == 0, x, y)]).astype(jnp.int32)
    meta = jnp.concatenate([routes.astype(BF), probs], axis=1)
    meta_b, tok_b, cot_b = other_core(meta), other_core(tokens), other_core(cotangent)
    w0 = jnp.concatenate([w_gate[0], w_up[0], w_down[0].T], axis=0)
    half = w0.shape[0] // 2
    w1, w3 = shifted(w0, COPIES, 1), shifted(w0, COPIES, -1)
    (sent,) = call(pack_body, [(SIDE, SENT, WIDE)], [pos, meta, meta_b, tokens, tok_b, cotangent, cot_b])
    w2a, w2b = shifted(w1[:half], COPIES, 1), shifted(w3[half:], COPIES, -1)
    got = grouped(sent.reshape(SIDE * SIDE, PAIR, WIDE), SPREAD).reshape(SIDE, SENT, WIDE)
    part, rows_x, rows_y, w2 = call(
        project_body,
        [(SIDE, SHARE, 3 * FF), (ROWS, WIDE), (ROWS, WIDE), (3 * BLK, FF)],
        [pos, got, w0, w1, w2a, w2b, w3],
    )
    terms = grouped(part, FEATURE)
    (a0,) = call(activate_body, [(SHARE, 3 * FF)], [terms], smem=0)
    a1, a2, a3 = [shifted(a0, FEATURE, k) for k in (1, 2, -1)]
    xt, yt = call(turn_body, [(WIDE, ROWS), (WIDE, ROWS)], [rows_x, rows_y], smem=0)
    acts, top, low = call(
        far_grads_body,
        [(ROWS, 3 * FF), (half, FF), (half, FF)],
        [xt, yt, a0, a1, a2, a3],
        smem=0,
    )
    top, low = shifted(top, COPIES, -1), shifted(low, COPIES, 1)
    (back,) = call(
        return_body,
        [(SIDE, SENT, WIDE)],
        [pos, acts, w0, w1, w2, w3],
        scratch=[(ROWS, WIDE), (ROWS, WIDE)],
    )
    own = grouped(back.reshape(SIDE * SIDE, PAIR, WIDE), SPREAD).reshape(SIDE, SENT, WIDE)
    g0, g1, g3 = call(near_grads_body, [(3 * BLK, FF)] * 3, [xt, yt, acts, top, low], smem=0)
    g1, g3 = shifted(g1, COPIES, -1), shifted(g3, COPIES, 1)
    oth = other_core(own)
    mixed, grad = call(
        unpack_body, [(TOK, SIDE * WIDE)] * 2, [pos, meta, meta_b, own, oth], hbm=True
    )
    gate, upper, down = call(
        total_body, [(BLK, FF), (BLK, FF), (FF, BLK)], [g0, g1, g3], smem=0, hbm=True
    )
    return mixed, grad, gate[None], upper[None], down[None]


def solution(mesh):
    finer = Mesh(mesh.devices.reshape(SIDE, SIDE, SIDE, 2), AXES)
    rows = P(AXES, None)
    wide = P(("z", "c"), ("y", "x"), None)
    tall = P(("z", "c"), None, ("y", "x"))
    return jax.shard_map(
        layer,
        mesh=finer,
        in_specs=(rows, rows, rows, wide, wide, tall, rows),
        out_specs=(rows, rows, wide, wide, tall),
        check_vma=False,
    )
```

time: 253 us -> 199 us (0.79)
  blocking collectives: 60.5 us -> 27.2 us
  waiting for transfers between devices: 103 us -> 83.4 us
  Pallas kernels: 51.4 us -> 34.2 us
  starting transfers between devices: 25.2 us -> 36.1 us
  local copies, waits for them, and re-layouts: 9.06 us -> 15.4 us
    ppermute x9 -> x11, waiting for transfers between devices: 102 us -> 57.3 us  [shifted(): return lax.ppermute(value, AXES, pairs)]
    all_to_all x2 -> x1, blocking collectives: 60.5 us -> 27.2 us  [grouped(): lax.all_to_all(value, AXES, 0, 0, axis_index_groups=rings, tiled=True)]
    all_to_all x1 -> x2, waiting for transfers between devices: 0.01 us -> 25.3 us  [grouped(): lax.all_to_all(value, AXES, 0, 0, axis_index_groups=rings, tiled=True)]
    pallas_call x7 -> x9, Pallas kernels: 51.4 us -> 34.2 us  [call(): pl.pallas_call(body, out_shape=[place_out(dims, BF) for dims in outs], in...]
    all_to_all x1 -> x2, starting transfers between devices: 8.07 us -> 13.5 us  [grouped(): lax.all_to_all(value, AXES, 0, 0, axis_index_groups=rings, tiled=True)]
    unnamed x39 -> x49, local copies, waits for them, and re-layouts: 9.01 us -> 13.8 us
    ppermute x5 -> x4, starting transfers between devices: 5.03 us -> 8.87 us  [other_core(): return lax.ppermute(value, 'c', [(0, 1), (1, 0)])]
    ppermute x9 -> x11, starting transfers between devices: 12.1 us -> 13.7 us  [shifted(): return lax.ppermute(value, AXES, pairs)]
  transfers between devices with their start and end apart: 15 -> 17, of which waited for: 7 -> 8; matrix products, arithmetic and copies ran while one was open for 2% -> 2% of each run, Pallas kernels for 6% -> 6%
where the time goes in v2:
time: 199 us
  waiting for transfers between devices  83.4 us (42%)
  starting transfers between devices  36.1 us (18%)
  Pallas kernels  34.2 us (17%)
  blocking collectives  27.2 us (14%)
  local copies, waits for them, and re-layouts  15.4 us (8%)
    ppermute x11, waiting for transfers between devices, shifted(): return lax.ppermute(value, AXES, pairs)  57.3 us
    pallas_call x9, Pallas kernels, call(): pl.pallas_call(body, out_shape=[place_out(dims, BF) for dims in outs], in...  34.2 us
    all_to_all x1, blocking collectives, grouped(): lax.all_to_all(value, AXES, 0, 0, axis_index_groups=rings, tiled=True)  27.2 us
    all_to_all x2, waiting for transfers between devices, grouped(): lax.all_to_all(value, AXES, 0, 0, axis_index_groups=rings, tiled=True)  25.3 us
    unnamed x49, local copies, waits for them, and re-layouts  13.8 us
    ppermute x11, starting transfers between devices, shifted(): return lax.ppermute(value, AXES, pairs)  13.7 us
    all_to_all x2, starting transfers between devices, grouped(): lax.all_to_all(value, AXES, 0, 0, axis_index_groups=rings, tiled=True)  13.5 us
    ppermute x4, starting transfers between devices, other_core(): return lax.ppermute(value, 'c', [(0, 1), (1, 0)])  8.87 us
  transfers between devices with their start and end apart: 17, of which 8 were waited for; matrix products, arithmetic and copies ran while one was open for 2% of the time, Pallas kernels for 6%

profile of v2, /device:TPU:1, one launch (start us, length us, event | category | flops | bytes accessed | tf_op | source)
XLA Modules:
  0.0 198.6 jit_solution(11503085658471856138)
XLA Ops:
  0.6 1.5 collective-permute-start.1
  2.2 1.2 copy.17
  3.5 1.4 pad_maximum_fusion.w0
  4.9 1.4 collective-permute-start.5
  6.3 1.4 collective-permute-start.3
  9.7 1.2 copy-done.10
  12.2 3.5 %shard_map.110 = bf16[4,288,1024]{2,1,0:T(8,128)(2,1)S(1)} custom-call(s32[3]{0:T(128)S(1)} %pad_add_fusion.pos, bf16[128,2]{1,0:T(8,128)(2,1)S(1)} %copy.18.meta_a, bf16[128,2]{1,0:T(8,128)(2,1)S(1)} %collective-permute-done.meta_b, bf16[128,4096]{1,0:T(8,128)(2,1)S(1)} %copy-done.10, bf16[128,4096]{1,0:T(8,128)(2,1)} %collective-permute-done.1.tok_b, ...), custom_call_target="tpu_custom_call" | custom-call | tf_op jit(solution)/shard_map/pallas_call | solution.py:76
  15.7 1.5 copy-done.4
  17.1 7.3 %all-to-all-start = ((bf16[16,72,1024]{2,1,0:T(8,128)(2,1)}), bf16[16,72,1024]{2,1,0:T(8,128)(2,1)}, u32[]{:S(2)}, u32[]{:S(2)}) async-start(bf16[16,72,1024]{2,1,0:T(8,128)(2,1)} %bitcast.15), calls=%async_computation | async-start | bytes 4718592 | tf_op jit(solution)/shard_map/all_to_all | solution.py:52
  24.5 1.2 collective-permute-done.5.w3
  26.1 1.4 slice.8
  27.4 2.3 %collective-permute-start.4 = (bf16[384,1024]{1,0:T(8,128)(2,1)S(1)}, bf16[384,1024]{1,0:T(8,128)(2,1)S(1)}, u32[]{:S(2)}, u32[]{:S(2)}) collective-permute-start(bf16[384,1024]{1,0:T(8,128)(2,1)S(1)} %slice.8), channel_id=1, source_target_pairs={{32,0},{64,32},{96,64},{0,96},{9,1},{17,9},{25,17},{1,25},{34,2},{... | collective-permute-start | bytes 2359304 | tf_op jit(solution)/shard_map/ppermute | solution.py:48
  29.8 18.0 %collective-permute-done.6.w2b = bf16[384,1024]{1,0:T(8,128)(2,1)S(1)} collective-permute-done((bf16[384,1024]{1,0:T(8,128)(2,1)S(1)}, bf16[384,1024]{1,0:T(8,128)(2,1)S(1)}, u32[]{:S(2)}, u32[]{:S(2)}) %collective-permute-start.6) | collective-permute-done | bytes 786464 | tf_op jit(solution)/shard_map/ppermute | solution.py:48
  49.5 3.8 %all-to-all-done = bf16[16,72,1024]{2,1,0:T(8,128)(2,1)} async-done(((bf16[16,72,1024]{2,1,0:T(8,128)(2,1)}), bf16[16,72,1024]{2,1,0:T(8,128)(2,1)}, u32[]{:S(2)}, u32[]{:S(2)}) %all-to-all-start) | async-done | bytes 2359328 | tf_op jit(solution)/shard_map/all_to_all | solution.py:52
  55.6 7.5 %shard_map.111 = (bf16[4,144,3072]{2,1,0:T(8,128)(2,1)S(1)}, bf16[576,1024]{1,0:T(8,128)(2,1)S(1)}, bf16[576,1024]{1,0:T(8,128)(2,1)S(1)}, bf16[768,1024]{1,0:T(8,128)(2,1)S(1)}) custom-call(s32[3]{0:T(128)S(1)} %pad_add_fusion.pos, bf16[4,288,1024]{2,1,0:T(8,128)(2,1)} %bitcast.4.got, bf16[768,1024]{1,0:T(8,128)(2,1)S(1)} %pad_maximum_fusion.w0, ...), custom_call_target="tpu_custom_call" | custom-call | tf_op jit(solution)/shard_map/pallas_call | solution.py:76
  63.1 27.2 %all_to_all.15.terms = bf16[4,144,3072]{2,1,0:T(8,128)(2,1)S(1)} all-to-all(bf16[4,144,3072]{2,1,0:T(8,128)(2,1)S(1)} %get-tuple-element.26), channel_id=1, replica_groups={{0,8,16,24},{1,33,65,97},{2,10,18,26},{3,35,67,99},{4,12,20,28},{5,37,6..., dimensions={0} | all-to-all | bytes 7077888 | tf_op jit(solution)/shard_map/all_to_all | solution.py:52
  91.4 1.8 collective-permute-start.8
  94.7 19.3 %collective-permute-done.9.a3 = bf16[144,3072]{1,0:T(8,128)(2,1)S(1)} collective-permute-done((bf16[144,3072]{1,0:T(8,128)(2,1)S(1)}, bf16[144,3072]{1,0:T(8,128)(2,1)S(1)}, u32[]{:S(2)}, u32[]{:S(2)}) %collective-permute-start.9) | collective-permute-done | bytes 884768 | tf_op jit(solution)/shard_map/ppermute | solution.py:48
  114.6 1.4 shard_map.114
  116.5 7.6 %shard_map.115 = bf16[4,288,1024]{2,1,0:T(8,128)(2,1)S(1)} custom-call(s32[3]{0:T(128)S(1)} %pad_add_fusion.pos, bf16[576,3072]{1,0:T(8,128)(2,1)S(1)} %get-tuple-element.27.acts, bf16[768,1024]{1,0:T(8,128)(2,1)S(1)} %copy-done.1, bf16[768,1024]{1,0:T(8,128)(2,1)} %collective-permute-done.3.w1, bf16[768,1024]{1,0:T(8,128)(2,1)S(1)} %get-tuple-element.28.w2, ...), custom_call_target="tpu_custom_call" | custom-call | tf_op jit(solution)/shard_map/pallas_call | solution.py:76
  124.2 1.5 copy-done.5
  125.6 6.2 %all-to-all-start.2 = ((bf16[16,72,1024]{2,1,0:T(8,128)(2,1)}), bf16[16,72,1024]{2,1,0:T(8,128)(2,1)}, u32[]{:S(2)}, u32[]{:S(2)}) async-start(bf16[16,72,1024]{2,1,0:T(8,128)(2,1)} %bitcast.16), calls=%async_computation.2 | async-start | bytes 4718592 | tf_op jit(solution)/shard_map/all_to_all | solution.py:52
  132.0 2.7 %collective-permute-start.12 = (bf16[384,1024]{1,0:T(8,128)(2,1)}, bf16[384,1024]{1,0:T(8,128)(2,1)}, u32[]{:S(2)}, u32[]{:S(2)}) collective-permute-start(bf16[384,1024]{1,0:T(8,128)(2,1)} %copy-done.20), channel_id=1, source_target_pairs={{32,0},{64,32},{96,64},{0,96},{9,1},{17,9},{25,17},{1,25},{34,2},{... | collective-permute-start | bytes 2359304 | tf_op jit(solution)/shard_map/ppermute | solution.py:48
  134.6 21.4 %all-to-all-done.2 = bf16[16,72,1024]{2,1,0:T(8,128)(2,1)} async-done(((bf16[16,72,1024]{2,1,0:T(8,128)(2,1)}), bf16[16,72,1024]{2,1,0:T(8,128)(2,1)}, u32[]{:S(2)}, u32[]{:S(2)}) %all-to-all-start.2) | async-done | bytes 2359328 | tf_op jit(solution)/shard_map/all_to_all | solution.py:52
  156.1 6.3 %collective-permute-start.10 = (bf16[4,288,1024]{2,1,0:T(8,128)(2,1)}, bf16[4,288,1024]{2,1,0:T(8,128)(2,1)S(1)}, u32[]{:S(2)}, u32[]{:S(2)}) collective-permute-start(bf16[4,288,1024]{2,1,0:T(8,128)(2,1)} %bitcast.10.own), channel_id=1, source_target_pairs={{0,1},{1,0},{2,3},{3,2},{4,5},{5,4},{6,7},{7,6},{8,9},{9,8},{10,11... | collective-permute-start | bytes 7077896 | tf_op jit(solution)/shard_map/ppermute | solution.py:56
  162.3 1.3 copy-done.7
  163.7 1.3 copy-done.9
  165.0 5.2 %shard_map.117 = (bf16[768,1024]{1,0:T(8,128)(2,1)S(1)}, bf16[768,1024]{1,0:T(8,128)(2,1)S(1)}, bf16[768,1024]{1,0:T(8,128)(2,1)S(1)}) custom-call(bf16[1024,576]{1,0:T(8,128)(2,1)S(1)} %copy-done.7, bf16[1024,576]{1,0:T(8,128)(2,1)S(1)} %copy-done.9, bf16[576,3072]{1,0:T(8,128)(2,1)S(1)} %get-tuple-element.27.acts, ...), custom_call_target="tpu_custom_call" | custom-call | tf_op jit(solution)/shard_map/pallas_call | solution.py:76
  170.3 2.7 %collective-permute-start.14 = (bf16[768,1024]{1,0:T(8,128)(2,1)S(1)}, bf16[768,1024]{1,0:T(8,128)(2,1)S(1)}, u32[]{:S(2)}, u32[]{:S(2)}) collective-permute-start(bf16[768,1024]{1,0:T(8,128)(2,1)S(1)} %get-tuple-element.35), channel_id=1, source_target_pairs={{32,0},{64,32},{96,64},{0,96},{9,1},{17,9},{25,17},{1,25},{34,2},{... | collective-permute-start | bytes 4718600 | tf_op jit(solution)/shard_map/ppermute | solution.py:48
  173.0 18.1 %collective-permute-done.13.g1 = bf16[768,1024]{1,0:T(8,128)(2,1)S(1)} collective-permute-done((bf16[768,1024]{1,0:T(8,128)(2,1)S(1)}, bf16[768,1024]{1,0:T(8,128)(2,1)S(1)}, u32[]{:S(2)}, u32[]{:S(2)}) %collective-permute-start.13) | collective-permute-done | bytes 1572896 | tf_op jit(solution)/shard_map/ppermute | solution.py:48
  191.1 1.8 shard_map.118
  192.9 5.8 %shard_map.116 = (bf16[128,4096]{1,0:T(8,128)(2,1)}, bf16[128,4096]{1,0:T(8,128)(2,1)}) custom-call(s32[3]{0:T(128)S(1)} %pad_add_fusion.pos, bf16[128,2]{1,0:T(8,128)(2,1)S(1)} %copy-done.17, bf16[128,2]{1,0:T(8,128)(2,1)S(1)} %copy-done.19, bf16[4,288,1024]{2,1,0:T(8,128)(2,1)} %bitcast.10.own, bf16[4,288,1024]{2,1,0:T(8,128)(2,1)S(1)} %collective-permute-done.10.oth), custom_call_target="tpu_custom_call" | custom-call | tf_op jit(solution)/shard_map/pallas_call | solution.py:76
  (68 shorter events, 11.6 us)
Async XLA Ops:
  0.6 9.1 %collective-permute-start.1 = (bf16[128,4096]{1,0:T(8,128)(2,1)}, bf16[128,4096]{1,0:T(8,128)(2,1)}, u32[]{:S(2)}, u32[]{:S(2)}) collective-permute-start(bf16[128,4096]{1,0:T(8,128)(2,1)} %tok_a.1), channel_id=1, source_target_pairs={{0,1},{1,0},{2,3},{3,2},{4,5},{5,4},{6,7},{7,6},{8,9},{9,8},{10,11... | collective-permute-start | bytes 3145736 | tf_op jit(solution)/shard_map/ppermute | solution.py:56
  2.1 7.6 %collective-permute-start.2 = (bf16[128,4096]{1,0:T(8,128)(2,1)}, bf16[128,4096]{1,0:T(8,128)(2,1)}, u32[]{:S(2)}, u32[]{:S(2)}) collective-permute-start(bf16[128,4096]{1,0:T(8,128)(2,1)} %cot_a.1), channel_id=1, source_target_pairs={{0,1},{1,0},{2,3},{3,2},{4,5},{5,4},{6,7},{7,6},{8,9},{9,8},{10,11... | collective-permute-start | bytes 3145736 | tf_op jit(solution)/shard_map/ppermute | solution.py:56
  3.4 4.2 %copy-start.22 = (s32[128,1]{0,1:T(1,128)S(1)}, s32[128,1]{0,1:T(1,128)}, u32[]{:S(2)}) copy-start(s32[128,1]{0,1:T(1,128)} %param.9) | copy-start | bytes 1540
  3.5 4.2 %copy-start.23 = (bf16[128,1]{0,1:T(2,128)(2,1)S(1)}, bf16[128,1]{0,1:T(2,128)(2,1)}, u32[]{:S(2)}) copy-start(bf16[128,1]{0,1:T(2,128)(2,1)} %param.8) | copy-start | bytes 772
  4.9 48.5 %copy-start = (bf16[768,1024]{1,0:T(8,128)(2,1)}, bf16[768,1024]{1,0:T(8,128)(2,1)S(1)}, u32[]{:S(2)}) copy-start(bf16[768,1024]{1,0:T(8,128)(2,1)S(1)} %pad_maximum_fusion.w0) | copy-start | bytes 4718596
  4.9 20.8 %collective-permute-start.5 = (bf16[768,1024]{1,0:T(8,128)(2,1)S(1)}, bf16[768,1024]{1,0:T(8,128)(2,1)S(1)}, u32[]{:S(2)}, u32[]{:S(2)}) collective-permute-start(bf16[768,1024]{1,0:T(8,128)(2,1)S(1)} %pad_maximum_fusion.w0), channel_id=1, source_target_pairs={{96,0},{0,32},{32,64},{64,96},{25,1},{1,9},{9,17},{17,25},{98,2},{... | collective-permute-start | bytes 4718600 | tf_op jit(solution)/shard_map/ppermute | solution.py:48
  6.3 19.8 %collective-permute-start.3 = (bf16[768,1024]{1,0:T(8,128)(2,1)S(1)}, bf16[768,1024]{1,0:T(8,128)(2,1)}, u32[]{:S(2)}, u32[]{:S(2)}) collective-permute-start(bf16[768,1024]{1,0:T(8,128)(2,1)S(1)} %pad_maximum_fusion.w0), channel_id=1, source_target_pairs={{32,0},{64,32},{96,64},{0,96},{9,1},{17,9},{25,17},{1,25},{34,2},{... | collective-permute-start | bytes 4718600 | tf_op jit(solution)/shard_map/ppermute | solution.py:48
  7.8 7.9 %copy-start.16 = (bf16[128,2]{1,0:T(8,128)(2,1)}, bf16[128,2]{1,0:T(8,128)(2,1)S(1)}, u32[]{:S(2)}) copy-start(bf16[128,2]{1,0:T(8,128)(2,1)S(1)} %copy.18.meta_a) | copy-start | bytes 1540
  7.8 1.9 collective-permute-start
  9.7 6.0 %copy-start.18 = (bf16[128,2]{1,0:T(8,128)(2,1)}, bf16[128,2]{1,0:T(8,128)(2,1)S(1)}, u32[]{:S(2)}) copy-start(bf16[128,2]{1,0:T(8,128)(2,1)S(1)} %collective-permute-done.meta_b) | copy-start | bytes 1540
  15.7 1.5 copy-start.4
  17.1 36.2 %all-to-all-start = ((bf16[16,72,1024]{2,1,0:T(8,128)(2,1)}), bf16[16,72,1024]{2,1,0:T(8,128)(2,1)}, u32[]{:S(2)}, u32[]{:S(2)}) async-start(bf16[16,72,1024]{2,1,0:T(8,128)(2,1)} %bitcast.15), calls=%async_computation | async-start | bytes 4718592 | tf_op jit(solution)/shard_map/all_to_all | solution.py:52
  25.7 27.7 %copy-start.2 = (bf16[768,1024]{1,0:T(8,128)(2,1)}, bf16[768,1024]{1,0:T(8,128)(2,1)S(1)}, u32[]{:S(2)}) copy-start(bf16[768,1024]{1,0:T(8,128)(2,1)S(1)} %collective-permute-done.5.w3) | copy-start | bytes 4718596
  25.8 22.0 %collective-permute-start.6 = (bf16[384,1024]{1,0:T(8,128)(2,1)S(1)}, bf16[384,1024]{1,0:T(8,128)(2,1)S(1)}, u32[]{:S(2)}, u32[]{:S(2)}) collective-permute-start(bf16[384,1024]{1,0:T(8,128)(2,1)S(1)} %slice.9), channel_id=1, source_target_pairs={{96,0},{0,32},{32,64},{64,96},{25,1},{1,9},{9,17},{17,25},{98,2},{... | collective-permute-start | bytes 2359304 | tf_op jit(solution)/shard_map/ppermute | solution.py:48
  27.4 21.2 %collective-permute-start.4 = (bf16[384,1024]{1,0:T(8,128)(2,1)S(1)}, bf16[384,1024]{1,0:T(8,128)(2,1)S(1)}, u32[]{:S(2)}, u32[]{:S(2)}) collective-permute-start(bf16[384,1024]{1,0:T(8,128)(2,1)S(1)} %slice.8), channel_id=1, source_target_pairs={{32,0},{64,32},{96,64},{0,96},{9,1},{17,9},{25,17},{1,25},{34,2},{... | collective-permute-start | bytes 2359304 | tf_op jit(solution)/shard_map/ppermute | solution.py:48
  91.1 22.9 %collective-permute-start.9 = (bf16[144,3072]{1,0:T(8,128)(2,1)S(1)}, bf16[144,3072]{1,0:T(8,128)(2,1)S(1)}, u32[]{:S(2)}, u32[]{:S(2)}) collective-permute-start(bf16[144,3072]{1,0:T(8,128)(2,1)S(1)} %shard_map.113.a0), channel_id=1, source_target_pairs={{24,0},{0,8},{8,16},{16,24},{97,1},{1,33},{33,65},{65,97},{26,2},{... | collective-permute-start | bytes 2654216 | tf_op jit(solution)/shard_map/ppermute | solution.py:48
  91.4 22.6 %collective-permute-start.8 = (bf16[144,3072]{1,0:T(8,128)(2,1)S(1)}, bf16[144,3072]{1,0:T(8,128)(2,1)S(1)}, u32[]{:S(2)}, u32[]{:S(2)}) collective-permute-start(bf16[144,3072]{1,0:T(8,128)(2,1)S(1)} %shard_map.113.a0), channel_id=1, source_target_pairs={{16,0},{24,8},{0,16},{8,24},{65,1},{97,33},{1,65},{33,97},{18,2},{... | collective-permute-start | bytes 2654216 | tf_op jit(solution)/shard_map/ppermute | solution.py:48
  93.2 21.4 %collective-permute-start.7 = (bf16[144,3072]{1,0:T(8,128)(2,1)S(1)}, bf16[144,3072]{1,0:T(8,128)(2,1)S(1)}, u32[]{:S(2)}, u32[]{:S(2)}) collective-permute-start(bf16[144,3072]{1,0:T(8,128)(2,1)S(1)} %shard_map.113.a0), channel_id=1, source_target_pairs={{8,0},{16,8},{24,16},{0,24},{33,1},{65,33},{97,65},{1,97},{10,2},{... | collective-permute-start | bytes 2654216 | tf_op jit(solution)/shard_map/ppermute | solution.py:48
  94.7 21.4 %copy-start.6 = (bf16[1024,576]{1,0:T(8,128)(2,1)}, bf16[1024,576]{1,0:T(8,128)(2,1)S(1)}, u32[]{:S(2)}) copy-start(bf16[1024,576]{1,0:T(8,128)(2,1)S(1)} %get-tuple-element.24.xt) | copy-start | bytes 3538948
  94.7 21.4 %copy-start.8 = (bf16[1024,576]{1,0:T(8,128)(2,1)}, bf16[1024,576]{1,0:T(8,128)(2,1)S(1)}, u32[]{:S(2)}) copy-start(bf16[1024,576]{1,0:T(8,128)(2,1)S(1)} %get-tuple-element.25.yt) | copy-start | bytes 3538948
  114.6 1.9 copy-start.3
  116.1 8.1 %copy-start.20 = (bf16[384,1024]{1,0:T(8,128)(2,1)}, bf16[384,1024]{1,0:T(8,128)(2,1)S(1)}, u32[]{:S(2)}) copy-start(bf16[384,1024]{1,0:T(8,128)(2,1)S(1)} %get-tuple-element.32) | copy-start | bytes 2359300
  116.1 8.1 %copy-start.21 = (bf16[384,1024]{1,0:T(8,128)(2,1)}, bf16[384,1024]{1,0:T(8,128)(2,1)S(1)}, u32[]{:S(2)}) copy-start(bf16[384,1024]{1,0:T(8,128)(2,1)S(1)} %get-tuple-element.31) | copy-start | bytes 2359300
  124.2 1.5 copy-start.5
  125.6 30.4 %all-to-all-start.2 = ((bf16[16,72,1024]{2,1,0:T(8,128)(2,1)}), bf16[16,72,1024]{2,1,0:T(8,128)(2,1)}, u32[]{:S(2)}, u32[]{:S(2)}) async-start(bf16[16,72,1024]{2,1,0:T(8,128)(2,1)} %bitcast.16), calls=%async_computation.2 | async-start | bytes 4718592 | tf_op jit(solution)/shard_map/all_to_all | solution.py:52
  131.9 30.5 %collective-permute-start.11 = (bf16[384,1024]{1,0:T(8,128)(2,1)}, bf16[384,1024]{1,0:T(8,128)(2,1)}, u32[]{:S(2)}, u32[]{:S(2)}) collective-permute-start(bf16[384,1024]{1,0:T(8,128)(2,1)} %copy-done.21), channel_id=1, source_target_pairs={{96,0},{0,32},{32,64},{64,96},{25,1},{1,9},{9,17},{17,25},{98,2},{... | collective-permute-start | bytes 2359304 | tf_op jit(solution)/shard_map/ppermute | solution.py:48
  132.0 30.4 %collective-permute-start.12 = (bf16[384,1024]{1,0:T(8,128)(2,1)}, bf16[384,1024]{1,0:T(8,128)(2,1)}, u32[]{:S(2)}, u32[]{:S(2)}) collective-permute-start(bf16[384,1024]{1,0:T(8,128)(2,1)} %copy-done.20), channel_id=1, source_target_pairs={{32,0},{64,32},{96,64},{0,96},{9,1},{17,9},{25,17},{1,25},{34,2},{... | collective-permute-start | bytes 2359304 | tf_op jit(solution)/shard_map/ppermute | solution.py:48
  156.1 36.8 %collective-permute-start.10 = (bf16[4,288,1024]{2,1,0:T(8,128)(2,1)}, bf16[4,288,1024]{2,1,0:T(8,128)(2,1)S(1)}, u32[]{:S(2)}, u32[]{:S(2)}) collective-permute-start(bf16[4,288,1024]{2,1,0:T(8,128)(2,1)} %bitcast.10.own), channel_id=1, source_target_pairs={{0,1},{1,0},{2,3},{3,2},{4,5},{5,4},{6,7},{7,6},{8,9},{9,8},{10,11... | collective-permute-start | bytes 7077896 | tf_op jit(solution)/shard_map/ppermute | solution.py:56
  170.2 20.8 %collective-permute-start.13 = (bf16[768,1024]{1,0:T(8,128)(2,1)S(1)}, bf16[768,1024]{1,0:T(8,128)(2,1)S(1)}, u32[]{:S(2)}, u32[]{:S(2)}) collective-permute-start(bf16[768,1024]{1,0:T(8,128)(2,1)S(1)} %get-tuple-element.34), channel_id=1, source_target_pairs={{96,0},{0,32},{32,64},{64,96},{25,1},{1,9},{9,17},{17,25},{98,2},{... | collective-permute-start | bytes 4718600 | tf_op jit(solution)/shard_map/ppermute | solution.py:48
  170.3 20.8 %collective-permute-start.14 = (bf16[768,1024]{1,0:T(8,128)(2,1)S(1)}, bf16[768,1024]{1,0:T(8,128)(2,1)S(1)}, u32[]{:S(2)}, u32[]{:S(2)}) collective-permute-start(bf16[768,1024]{1,0:T(8,128)(2,1)S(1)} %get-tuple-element.35), channel_id=1, source_target_pairs={{32,0},{64,32},{96,64},{0,96},{9,1},{17,9},{25,17},{1,25},{34,2},{... | collective-permute-start | bytes 4718600 | tf_op jit(solution)/shard_map/ppermute | solution.py:48
  191.1 1.8 copy-start.17
  191.1 1.8 copy-start.19
  (9 other events, 10.6 us)

commit v3 on v2

v3 whole, which is shorter than its diff:
```python
import jax
import jax.numpy as jnp
from jax import lax
from jax.experimental import pallas as pl
from jax.experimental.pallas import tpu as pltpu
from jax.sharding import Mesh
from jax.sharding import PartitionSpec as P


AXES = ("y", "x", "z", "c")
BF = jnp.bfloat16
F32 = jnp.float32
SIDE = 4
TOK = 128
BLK = 256
FF = 1024
SLOT = 36
PAIR = 2 * SLOT
PAD = 40
SHARE = SIDE * SLOT
SENT = SIDE * PAIR
BACK = SIDE * PAD
ROWS = SIDE * SHARE
WIDE = SIDE * BLK


def place(y, x, z, c):
    return ((y * SIDE + x) * SIDE + z) * 2 + c


def groups():
    n = range(SIDE)
    feature, copies, spread = [], [], []
    for k in n:
        for z in n:
            feature.append([place(k, x, z, 0) for x in n])
            feature.append([place(y, k, z, 1) for y in n])
            copies.append([place(y, k, z, 0) for y in n])
            copies.append([place(k, x, z, 1) for x in n])
        spread.append([place(k, x, z, 0) for x in n for z in n])
        spread.append([place(y, k, z, 1) for y in n for z in n])
    return feature, copies, spread


FEATURE, COPIES, SPREAD = groups()


def shifted(value, rings, step):
    pairs = [(g[(i + step) % SIDE], g[i]) for g in rings for i in range(SIDE)]
    return lax.ppermute(value, AXES, pairs)


def grouped(value, rings):
    return lax.all_to_all(value, AXES, 0, 0, axis_index_groups=rings, tiled=True)


def other_core(value):
    return lax.ppermute(value, "c", [(0, 1), (1, 0)])


def iota(shape, dim):
    return lax.broadcasted_iota(jnp.int32, shape, dim)


def dot(a, b):
    return jnp.dot(a, b, preferred_element_type=F32)


def dot_nt(a, b):
    return lax.dot_general(a, b, (((1,), (1,)), ((), ())), preferred_element_type=F32)


def near(value):
    return pltpu.with_memory_space_constraint(value, pltpu.VMEM)


def far(value):
    return pltpu.with_memory_space_constraint(value, pltpu.HBM)


def call(body, outs, args, hbm=(), scratch=(), smem=1, limit=16):
    vmem = pl.BlockSpec(memory_space=pltpu.VMEM)
    shapes = [(pltpu.HBM if n in hbm else pltpu.VMEM)(dims, BF) for n, dims in enumerate(outs)]
    return pl.pallas_call(
        body,
        out_shape=shapes,
        in_specs=[pl.BlockSpec(memory_space=pltpu.SMEM)] * smem + [vmem] * (len(args) - smem),
        out_specs=[vmem] * len(outs),
        scratch_shapes=[pltpu.VMEM(dims, BF) for dims in scratch],
        compiler_params=pltpu.CompilerParams(vmem_limit_bytes=limit * 2**20),
    )(*args)


def column(kind, near, group, k):
    turned = (near + k) % SIDE
    return jnp.where(kind == 0, turned * SIDE + group, group * SIDE + turned)


def row_targets(route, kind, block):
    count = route.shape[0]
    hits = (iota((count, 8), 1) == route).astype(F32)
    earlier = (iota((count, count), 1) < iota((count, count), 0)).astype(BF)
    slot = jnp.sum(dot(earlier, hits.astype(BF)) * hits, axis=1, keepdims=True).astype(jnp.int32)
    return jnp.where(route % 2 == kind, (route // 2) * block + slot, -2 * block)


def routes_of(*metas):
    return jnp.concatenate([m[:, 0:1] for m in metas], axis=0).astype(F32).astype(jnp.int32)


def pack_body(pos, meta_a, meta_b, tok_a, tok_b, cot_a, cot_b, out):
    kind, at = pos[0], pos[1]
    target = row_targets(routes_of(meta_a, meta_b), kind, PAIR)
    rows = iota((2 * TOK, SENT), 1)
    pick_x = jnp.transpose((rows == target).astype(F32)).astype(BF)
    pick_y = jnp.transpose((rows == target + SLOT).astype(F32)).astype(BF)
    weight = jnp.concatenate([meta_a[:, 1:2], meta_b[:, 1:2]], axis=0).astype(F32)
    for d in range(SIDE):
        for k in range(SIDE):
            src = pl.ds(pl.multiple_of(column(kind, at, d, k) * BLK, BLK), BLK)
            x = jnp.concatenate([tok_a[:, src], tok_b[:, src]], axis=0)
            y = jnp.concatenate([cot_a[:, src], cot_b[:, src]], axis=0).astype(F32)
            both = dot(pick_x, x) + dot(pick_y, (y * weight).astype(BF))
            out[d, :, k * BLK : (k + 1) * BLK] = both.astype(BF)


def compact(pos, got, first, rows_out):
    q, r = iota((SHARE, SENT), 0), iota((SHARE, SENT), 1)
    take = (r == q + (q // SLOT) * (PAIR - SLOT) + first).astype(BF)
    for k in range(SIDE):
        rows_out[k * SHARE : (k + 1) * SHARE, :] = dot(take, got[(pos[2] + k) % SIDE]).astype(BF)


def expand(pos, rows, back):
    r, q = iota((BACK, SHARE), 0), iota((BACK, SHARE), 1)
    give = (r == q + (q // SLOT) * (PAD - SLOT)).astype(BF)
    for k in range(SIDE):
        back[(pos[2] + k) % SIDE] = dot(give, rows[k * SHARE : (k + 1) * SHARE, :]).astype(BF)


def share_out(total, parts, cols):
    total = total.astype(BF)
    for k, part in enumerate(parts):
        part[:, cols] = total[k * SHARE : (k + 1) * SHARE]


def project_y_body(pos, got, d0, d1, d2, d3, rows, p0, p1, p2, p3):
    compact(pos, got, SLOT, rows)
    for n in range(FF // BLK):
        cols = slice(n * BLK, (n + 1) * BLK)
        total = sum(dot_nt(rows[:, k * BLK : (k + 1) * BLK], w[cols, :]) for k, w in enumerate((d0, d1, d2, d3)))
        share_out(total, (p0, p1, p2, p3), cols)


def project_x_body(pos, got, w0, w1, w2, w3, rows, p0, p1, p2, p3):
    compact(pos, got, 0, rows)
    for n in range(2 * FF // BLK):
        t, cols = divmod(n * BLK, FF)
        total = sum(
            dot(rows[:, k * BLK : (k + 1) * BLK], w[t * BLK : (t + 1) * BLK, cols : cols + BLK])
            for k, w in enumerate((w0, w1, w2, w3))
        )
        share_out(total, (p0, p1, p2, p3), slice(n * BLK, (n + 1) * BLK))


def activate_body(y0, y1, y2, y3, x0, x1, x2, x3, act, grads):
    for n in range(FF // BLK):
        cols = slice(n * BLK, (n + 1) * BLK)
        ups = slice(FF + n * BLK, FF + (n + 1) * BLK)
        gate = sum(p[:, cols].astype(F32) for p in (x0, x1, x2, x3))
        upper = sum(p[:, ups].astype(F32) for p in (x0, x1, x2, x3))
        dact = sum(p[:, cols].astype(F32) for p in (y0, y1, y2, y3))
        sig = jax.nn.sigmoid(gate)
        act[:, cols] = (gate * sig * upper).astype(BF)
        grads[:, cols] = (dact * upper * sig * (1.0 + gate * (1.0 - sig))).astype(BF)
        grads[:, ups] = (dact * gate * sig).astype(BF)


def turn_body(x, y, xt, yt):
    for src, dst in ((x, xt), (y, yt)):
        for k in range(SIDE):
            cols = slice(k * BLK, (k + 1) * BLK)
            dst[cols, :] = jnp.transpose(src[:, cols].astype(F32)).astype(BF)


def result_body(pos, a0, a1, a2, a3, d0, d1, d2, d3, back, acts, res):
    for k, a in enumerate((a0, a1, a2, a3)):
        acts[k * SHARE : (k + 1) * SHARE, :] = a[...]
    for k, w in enumerate((d0, d1, d2, d3)):
        res[:, k * BLK : (k + 1) * BLK] = dot(acts[...], w[...]).astype(BF)
    expand(pos, res, back)


def grads_body(xt, yt, acts, a0, a1, a2, a3, grads, n0, n1, n2, n3):
    for k, a in enumerate((a0, a1, a2, a3)):
        grads[k * SHARE : (k + 1) * SHARE, :] = a[...]
    for k, out in ((2, n2), (1, n1), (3, n3), (0, n0)):
        rows = slice(k * BLK, (k + 1) * BLK)
        out[0:BLK, :] = dot(xt[rows, :], grads[:, 0:FF]).astype(BF)
        out[BLK : 2 * BLK, :] = dot(xt[rows, :], grads[:, FF:]).astype(BF)
        out[2 * BLK :, :] = dot(yt[rows, :], acts[...]).astype(BF)


def slot_body(pos, grads, w0, w1, w2, w3, back, slot):
    for k, w in enumerate((w0, w1, w2, w3)):
        total = dot_nt(grads[:, 0:FF], w[0:BLK, :]) + dot_nt(grads[:, FF:], w[BLK:, :])
        slot[:, k * BLK : (k + 1) * BLK] = total.astype(BF)
    expand(pos, slot, back)


def unpack_body(pos, meta_a, meta_b, own_m, own_s, oth_m, oth_s, mixed, grad):
    kind, at, across = pos[0], pos[1], pos[2]
    mine = row_targets(routes_of(meta_a, meta_b), kind, PAD)[0:TOK]
    theirs = row_targets(routes_of(meta_b, meta_a), 1 - kind, PAD)[TOK:]
    rows = iota((TOK, BACK), 1)
    mine, theirs = (rows == mine).astype(BF), (rows == theirs).astype(BF)
    weight = meta_a[:, 1:2].astype(F32)
    for b in range(SIDE * SIDE):
        major, minor = b // SIDE, b % SIDE
        own_d = jnp.where(kind == 0, minor, major)
        own_k = (jnp.where(kind == 0, major, minor) - at + SIDE) % SIDE
        oth_d = jnp.where(kind == 0, major, minor)
        oth_k = (jnp.where(kind == 0, minor, major) - across + SIDE) % SIDE
        own_c = pl.ds(pl.multiple_of(own_k * BLK, BLK), BLK)
        oth_c = pl.ds(pl.multiple_of(oth_k * BLK, BLK), BLK)
        cols = slice(b * BLK, (b + 1) * BLK)
        total = dot(mine, own_m[own_d, :, own_c]) + dot(theirs, oth_m[oth_d, :, oth_c])
        mixed[:, cols] = (total * weight).astype(BF)
        total = dot(mine, own_s[own_d, :, own_c]) + dot(theirs, oth_s[oth_d, :, oth_c])
        grad[:, cols] = total.astype(BF)


def total_body(n0, n1, n2, n3, gate, upper, down):
    def total(t):
        rows = slice(t * BLK, (t + 1) * BLK)
        return sum(n[rows, :].astype(F32) for n in (n0, n1, n2, n3))

    gate[...] = total(0).astype(BF)
    upper[...] = total(1).astype(BF)
    down[...] = jnp.transpose(total(2)).astype(BF)


def exchanged(value, block):
    rows = value.reshape(SIDE * SIDE, block, WIDE)
    return grouped(rows, SPREAD).reshape(SIDE, SIDE * block, WIDE)


def layer(tokens, probs, routes, w_gate, w_up, w_down, cotangent):
    y, x, c = lax.axis_index("y"), lax.axis_index("x"), lax.axis_index("c")
    pos = jnp.stack([c, jnp.where(c == 0, y, x), jnp.where(c == 0, x, y)]).astype(jnp.int32)
    meta = jnp.concatenate([routes.astype(BF), probs], axis=1)
    meta_b, tok_b, cot_b = other_core(meta), other_core(tokens), other_core(cotangent)
    d0, w0 = w_down[0], jnp.concatenate([w_gate[0], w_up[0]], axis=0)
    d1, d3 = far(shifted(d0, COPIES, 1)), far(shifted(d0, COPIES, -1))
    w1, w3 = far(shifted(w0, COPIES, 1)), far(shifted(w0, COPIES, -1))
    d2, w2 = far(shifted(d1, COPIES, 1)), far(shifted(w3, COPIES, -1))
    ds, ws = [far(d0), d1, d2, d3], [far(w0), w1, w2, w3]
    (sent,) = call(
        pack_body,
        [(SIDE, SENT, WIDE)],
        [pos, meta, meta_b, far(tokens), near(tok_b), far(cotangent), near(cot_b)],
        hbm=(0,),
    )
    got = near(exchanged(sent, PAIR))
    rows_x, *px = call(project_x_body, [(ROWS, WIDE)] + [(SHARE, 2 * FF)] * 4, [pos, got, *ws])
    px = [px[0]] + [near(shifted(px[k], FEATURE, -k)) for k in (1, 2, 3)]
    rows_y, *py = call(project_y_body, [(ROWS, WIDE)] + [(SHARE, FF)] * 4, [pos, got, *ds])
    py = [py[0]] + [near(shifted(py[k], FEATURE, -k)) for k in (1, 2, 3)]
    act, grad = call(activate_body, [(SHARE, FF), (SHARE, 2 * FF)], [*py, *px], smem=0)
    act = [act] + [near(shifted(act, FEATURE, k)) for k in (1, 2, -1)]
    grad = [far(grad)] + [far(shifted(grad, FEATURE, k)) for k in (1, 2, -1)]
    xt, yt = call(turn_body, [(WIDE, ROWS)] * 2, [rows_x, rows_y], smem=0, hbm=(0, 1))
    back_m, acts = call(
        result_body, [(SIDE, BACK, WIDE), (ROWS, FF)], [pos, *act, *ds], hbm=(0, 1), scratch=[(ROWS, WIDE)]
    )
    own_m = exchanged(back_m, PAD)
    grads, *ns = call(
        grads_body,
        [(ROWS, 2 * FF)] + [(3 * BLK, FF)] * 4,
        [far(xt), far(yt), far(acts), *grad],
        smem=0,
        hbm=(1, 2, 3, 4),
        limit=24,
    )
    ns = [far(ns[0])] + [near(shifted(ns[k], COPIES, -k)) for k in (1, 2, 3)]
    (back_s,) = call(slot_body, [(SIDE, BACK, WIDE)], [pos, near(grads), *ws], hbm=(0,), scratch=[(ROWS, WIDE)])
    own_s = exchanged(back_s, PAD)
    oth_m = near(other_core(own_m))
    oth_s = near(other_core(own_s))
    mixed, into = call(
        unpack_body,
        [(TOK, SIDE * WIDE)] * 2,
        [pos, meta, meta_b, far(own_m), far(own_s), oth_m, oth_s],
        hbm=(0, 1),
    )
    gate, upper, down = call(total_body, [(BLK, FF), (BLK, FF), (FF, BLK)], ns, smem=0, hbm=(0, 1, 2))
    return mixed, into, gate[None], upper[None], down[None]


def solution(mesh):
    finer = Mesh(mesh.devices.reshape(SIDE, SIDE, SIDE, 2), AXES)
    rows = P(AXES, None)
    wide = P(("z", "c"), ("y", "x"), None)
    tall = P(("z", "c"), None, ("y", "x"))
    return jax.shard_map(
        layer,
        mesh=finer,
        in_specs=(rows, rows, rows, wide, wide, tall, rows),
        out_specs=(rows, rows, wide, wide, tall),
        check_vma=False,
    )
```

time: 199 us -> 228 us (1.15)
  starting transfers between devices: 36.1 us -> 68.8 us
  blocking collectives: 27.2 us -> 0 us
  waiting for transfers between devices: 83.4 us -> 106 us
  local copies, waits for them, and re-layouts: 15.4 us -> 2.84 us
  Pallas kernels: 34.2 us -> 46.1 us
    ppermute x11 -> x21, waiting for transfers between devices: 57.3 us -> 100 us  [shifted(): return lax.ppermute(value, AXES, pairs)]
    all_to_all x1 -> x0, blocking collectives: 27.2 us -> none  [grouped(): lax.all_to_all(value, AXES, 0, 0, axis_index_groups=rings, tiled=True)]
    all_to_all x2 -> x3, waiting for transfers between devices: 25.3 us -> 4.48 us  [grouped(): lax.all_to_all(value, AXES, 0, 0, axis_index_groups=rings, tiled=True)]
    ppermute x4 -> x5, starting transfers between devices: 8.87 us -> 26.6 us  [other_core(): return lax.ppermute(value, 'c', [(0, 1), (1, 0)])]
    pallas_call x9 -> x10, Pallas kernels: 34.2 us -> 46.1 us  [call(): pl.pallas_call(body, out_shape=shapes, in_specs=[pl.BlockSpec(memory_spac...]
    ppermute x11 -> x21, starting transfers between devices: 13.7 us -> 24.9 us  [shifted(): return lax.ppermute(value, AXES, pairs)]
    unnamed x49 -> x30, local copies, waits for them, and re-layouts: 13.8 us -> 2.71 us
    all_to_all x2 -> x3, starting transfers between devices: 13.5 us -> 17.4 us  [grouped(): lax.all_to_all(value, AXES, 0, 0, axis_index_groups=rings, tiled=True)]
  transfers between devices with their start and end apart: 17 -> 29, of which waited for: 8 -> 14; matrix products, arithmetic and copies ran while one was open for 2% -> 1% of each run, Pallas kernels for 6% -> 14%
where the time goes in v3:
time: 228 us; the launch traced here: 227 us
  waiting for transfers between devices  106 us (46%)
  starting transfers between devices  68.8 us (30%)
  Pallas kernels  46.1 us (20%)
  local copies, waits for them, and re-layouts  2.84 us (1%)
  other arithmetic  2.44 us (1%)
    ppermute x21, waiting for transfers between devices, shifted(): return lax.ppermute(value, AXES, pairs)  100 us
    pallas_call x10, Pallas kernels, call(): pl.pallas_call(body, out_shape=shapes, in_specs=[pl.BlockSpec(memory_spac...  46.1 us
    ppermute x5, starting transfers between devices, other_core(): return lax.ppermute(value, 'c', [(0, 1), (1, 0)])  26.6 us
    ppermute x21, starting transfers between devices, shifted(): return lax.ppermute(value, AXES, pairs)  24.9 us
    all_to_all x3, starting transfers between devices, grouped(): lax.all_to_all(value, AXES, 0, 0, axis_index_groups=rings, tiled=True)  17.4 us
  transfers between devices with their start and end apart: 29, of which 14 were waited for; matrix products, arithmetic and copies ran while one was open for 1% of the time, Pallas kernels for 14%

profile of v3, /device:TPU:1, one launch (start us, length us, event | category | flops | bytes accessed | tf_op | source)
XLA Modules:
  0.0 227.5 jit_solution(1357891912349241858)
XLA Ops:
  4.2 1.9 collective-permute-done.meta_b
  6.1 4.9 %shard_map.110 = bf16[4,288,1024]{2,1,0:T(8,128)(2,1)} custom-call(s32[3]{0:T(128)S(1)} %pad_add_fusion.pos, bf16[128,2]{1,0:T(8,128)(2,1)S(1)} %copy.16.meta_a, bf16[128,2]{1,0:T(8,128)(2,1)S(1)} %collective-permute-done.meta_b, bf16[128,4096]{1,0:T(8,128)(2,1)} %tok_a.1, bf16[128,4096]{1,0:T(8,128)(2,1)S(1)} %collective-permute-done.1.tok_b, ...), custom_call_target="tpu_custom_call" | custom-call | tf_op jit(solution)/shard_map/pallas_call | solution.py:84
  11.1 8.0 %all-to-all-start = ((bf16[16,72,1024]{2,1,0:T(8,128)(2,1)}), bf16[16,72,1024]{2,1,0:T(8,128)(2,1)S(1)}, u32[]{:S(2)}, u32[]{:S(2)}) async-start(bf16[16,72,1024]{2,1,0:T(8,128)(2,1)} %bitcast.17), calls=%async_computation | async-start | bytes 4718592 | tf_op jit(solution)/shard_map/all_to_all | solution.py:54
  24.1 24.2 %collective-permute-done.10.w3 = bf16[512,1024]{1,0:T(8,128)(2,1)} collective-permute-done((bf16[512,1024]{1,0:T(8,128)(2,1)}, bf16[512,1024]{1,0:T(8,128)(2,1)}, u32[]{:S(2)}, u32[]{:S(2)}) %collective-permute-start.10) | collective-permute-done | bytes 1048608 | tf_op jit(solution)/shard_map/ppermute | solution.py:50
  49.3 1.8 collective-permute-start.4
  51.1 17.9 %collective-permute-done.5.d3 = bf16[1024,256]{1,0:T(8,128)(2,1)S(1)} collective-permute-done((bf16[1024,256]{1,0:T(8,128)(2,1)S(1)}, bf16[1024,256]{1,0:T(8,128)(2,1)S(1)}, u32[]{:S(2)}, u32[]{:S(2)}) %collective-permute-start.5) | collective-permute-done | bytes 524320 | tf_op jit(solution)/shard_map/ppermute | solution.py:50
  69.8 3.6 %shard_map.111 = (bf16[576,1024]{1,0:T(8,128)(2,1)S(1)}, bf16[144,1024]{1,0:T(8,128)(2,1)S(1)}, bf16[144,1024]{1,0:T(8,128)(2,1)S(1)}, bf16[144,1024]{1,0:T(8,128)(2,1)S(1)}, bf16[144,1024]{1,0:T(8,128)(2,1)S(1)}) custom-call(s32[3]{0:T(128)S(1)} %pad_add_fusion.pos, bf16[4,288,1024]{2,1,0:T(8,128)(2,1)S(1)} %bitcast.15, bf16[1024,256]{1,0:T(8,128)(2,1)} %bitcast.19, ...), custom_call_target="tpu_custom_call" | custom-call | tf_op jit(solution)/shard_map/pallas_call | solution.py:84
  73.4 1.8 collective-permute-start.6
  75.3 5.4 %shard_map.112 = (bf16[576,1024]{1,0:T(8,128)(2,1)S(1)}, bf16[144,2048]{1,0:T(8,128)(2,1)S(1)}, bf16[144,2048]{1,0:T(8,128)(2,1)S(1)}, bf16[144,2048]{1,0:T(8,128)(2,1)S(1)}, bf16[144,2048]{1,0:T(8,128)(2,1)S(1)}) custom-call(s32[3]{0:T(128)S(1)} %pad_add_fusion.pos, bf16[4,288,1024]{2,1,0:T(8,128)(2,1)S(1)} %bitcast.16, ...), custom_call_target="tpu_custom_call" | custom-call | tf_op jit(solution)/shard_map/pallas_call | solution.py:84
  81.8 2.6 %collective-permute-start.13 = (bf16[144,2048]{1,0:T(8,128)(2,1)S(1)}, bf16[144,2048]{1,0:T(8,128)(2,1)S(1)}, u32[]{:S(2)}, u32[]{:S(2)}) collective-permute-start(bf16[144,2048]{1,0:T(8,128)(2,1)S(1)} %get-tuple-element.37), channel_id=1, source_target_pairs={{16,0},{24,8},{0,16},{8,24},{65,1},{97,33},{1,65},{33,97},{18,2},{... | collective-permute-start | bytes 1769480 | tf_op jit(solution)/shard_map/ppermute | solution.py:50
  84.4 2.0 collective-permute-start.14
  88.3 13.2 %collective-permute-done.7.y2 = bf16[144,1024]{1,0:T(8,128)(2,1)S(1)} collective-permute-done((bf16[144,1024]{1,0:T(8,128)(2,1)S(1)}, bf16[144,1024]{1,0:T(8,128)(2,1)S(1)}, u32[]{:S(2)}, u32[]{:S(2)}) %collective-permute-start.7) | collective-permute-done | bytes 294944 | tf_op jit(solution)/shard_map/ppermute | solution.py:50
  101.4 3.8 %collective-permute-done.8.y3 = bf16[144,1024]{1,0:T(8,128)(2,1)S(1)} collective-permute-done((bf16[144,1024]{1,0:T(8,128)(2,1)S(1)}, bf16[144,1024]{1,0:T(8,128)(2,1)S(1)}, u32[]{:S(2)}, u32[]{:S(2)}) %collective-permute-start.8) | collective-permute-done | bytes 294944 | tf_op jit(solution)/shard_map/ppermute | solution.py:50
  106.0 2.3 collective-permute-start.15
  109.5 5.6 %collective-permute-done.15.a1 = bf16[144,1024]{1,0:T(8,128)(2,1)S(1)} collective-permute-done((bf16[144,1024]{1,0:T(8,128)(2,1)S(1)}, bf16[144,1024]{1,0:T(8,128)(2,1)S(1)}, u32[]{:S(2)}, u32[]{:S(2)}) %collective-permute-start.15) | collective-permute-done | bytes 294944 | tf_op jit(solution)/shard_map/ppermute | solution.py:50
  115.7 3.1 %collective-permute-done.17.a3 = bf16[144,1024]{1,0:T(8,128)(2,1)S(1)} collective-permute-done((bf16[144,1024]{1,0:T(8,128)(2,1)S(1)}, bf16[144,1024]{1,0:T(8,128)(2,1)S(1)}, u32[]{:S(2)}, u32[]{:S(2)}) %collective-permute-start.17) | collective-permute-done | bytes 294944 | tf_op jit(solution)/shard_map/ppermute | solution.py:50
  118.8 4.5 %shard_map.114 = (bf16[4,160,1024]{2,1,0:T(8,128)(2,1)}, bf16[576,1024]{1,0:T(8,128)(2,1)}) custom-call(s32[3]{0:T(128)S(1)} %pad_add_fusion.pos, bf16[144,1024]{1,0:T(8,128)(2,1)S(1)} %get-tuple-element.39.a0, bf16[144,1024]{1,0:T(8,128)(2,1)S(1)} %collective-permute-done.15.a1, bf16[144,1024]{1,0:T(8,128)(2,1)S(1)} %collective-permute-done.16.a2, ...), custom_call_target="tpu_custom_call" | custom-call | tf_op jit(solution)/shard_map/pallas_call | solution.py:84
  123.3 4.5 %all-to-all-start.1 = ((bf16[16,40,1024]{2,1,0:T(8,128)(2,1)}), bf16[16,40,1024]{2,1,0:T(8,128)(2,1)}, u32[]{:S(2)}, u32[]{:S(2)}) async-start(bf16[16,40,1024]{2,1,0:T(8,128)(2,1)} %bitcast.23), calls=%async_computation.1 | async-start | bytes 2621440 | tf_op jit(solution)/shard_map/all_to_all | solution.py:54
  127.9 2.5 %collective-permute-start.18 = (bf16[144,2048]{1,0:T(8,128)(2,1)S(1)}, bf16[144,2048]{1,0:T(8,128)(2,1)S(1)}, u32[]{:S(2)}, u32[]{:S(2)}) collective-permute-start(bf16[144,2048]{1,0:T(8,128)(2,1)S(1)} %get-tuple-element.46.a0), channel_id=1, source_target_pairs={{8,0},{16,8},{24,16},{0,24},{33,1},{65,33},{97,65},{1,97},{10,2},{... | collective-permute-start | bytes 1769480 | tf_op jit(solution)/shard_map/ppermute | solution.py:50
  131.5 2.1 shard_map.115
  133.6 10.4 %collective-permute-done.18.a1 = bf16[144,2048]{1,0:T(8,128)(2,1)S(1)} collective-permute-done((bf16[144,2048]{1,0:T(8,128)(2,1)S(1)}, bf16[144,2048]{1,0:T(8,128)(2,1)S(1)}, u32[]{:S(2)}, u32[]{:S(2)}) %collective-permute-start.18) | collective-permute-done | bytes 589856 | tf_op jit(solution)/shard_map/ppermute | solution.py:50
  145.6 6.0 %collective-permute-done.20.a3 = bf16[144,2048]{1,0:T(8,128)(2,1)S(1)} collective-permute-done((bf16[144,2048]{1,0:T(8,128)(2,1)S(1)}, bf16[144,2048]{1,0:T(8,128)(2,1)S(1)}, u32[]{:S(2)}, u32[]{:S(2)}) %collective-permute-start.20) | collective-permute-done | bytes 589856 | tf_op jit(solution)/shard_map/ppermute | solution.py:50
  152.4 9.4 %shard_map.116 = (bf16[576,2048]{1,0:T(8,128)(2,1)S(1)}, bf16[768,1024]{1,0:T(8,128)(2,1)}, bf16[768,1024]{1,0:T(8,128)(2,1)}, bf16[768,1024]{1,0:T(8,128)(2,1)}, bf16[768,1024]{1,0:T(8,128)(2,1)}) custom-call(bf16[1024,576]{1,0:T(8,128)(2,1)} %get-tuple-element.43.xt, bf16[1024,576]{1,0:T(8,128)(2,1)} %get-tuple-element.44.yt, ...), custom_call_target="tpu_custom_call" | custom-call | tf_op jit(solution)/shard_map/pallas_call | solution.py:84
  161.8 6.2 %shard_map.117 = bf16[4,160,1024]{2,1,0:T(8,128)(2,1)} custom-call(s32[3]{0:T(128)S(1)} %pad_add_fusion.pos, bf16[576,2048]{1,0:T(8,128)(2,1)S(1)} %get-tuple-element.47.grads, bf16[512,1024]{1,0:T(8,128)(2,1)} %pad_maximum_fusion.w0, bf16[512,1024]{1,0:T(8,128)(2,1)} %collective-permute-done.9.w1, bf16[512,1024]{1,0:T(8,128)(2,1)} %collective-permute-done.11.w2, ...), custom_call_target="tpu_custom_call" | custom-call | tf_op jit(solution)/shard_map/pallas_call | solution.py:84
  168.1 4.8 %all-to-all-start.2 = ((bf16[16,40,1024]{2,1,0:T(8,128)(2,1)}), bf16[16,40,1024]{2,1,0:T(8,128)(2,1)}, u32[]{:S(2)}, u32[]{:S(2)}) async-start(bf16[16,40,1024]{2,1,0:T(8,128)(2,1)} %bitcast.18), calls=%async_computation.2 | async-start | bytes 2621440 | tf_op jit(solution)/shard_map/all_to_all | solution.py:54
  173.0 2.5 %collective-permute-start.24 = (bf16[768,1024]{1,0:T(8,128)(2,1)}, bf16[768,1024]{1,0:T(8,128)(2,1)S(1)}, u32[]{:S(2)}, u32[]{:S(2)}) collective-permute-start(bf16[768,1024]{1,0:T(8,128)(2,1)} %get-tuple-element.52), channel_id=1, source_target_pairs={{64,0},{96,32},{0,64},{32,96},{17,1},{25,9},{1,17},{9,25},{66,2},{... | collective-permute-start | bytes 4718600 | tf_op jit(solution)/shard_map/ppermute | solution.py:50
  175.7 5.6 %collective-permute-start.21 = (bf16[4,160,1024]{2,1,0:T(8,128)(2,1)}, bf16[4,160,1024]{2,1,0:T(8,128)(2,1)}, u32[]{:S(2)}, u32[]{:S(2)}) collective-permute-start(bf16[4,160,1024]{2,1,0:T(8,128)(2,1)} %bitcast.9.own_m), channel_id=1, source_target_pairs={{0,1},{1,0},{2,3},{3,2},{4,5},{5,4},{6,7},{7,6},{8,9},{9,8},{10,11... | collective-permute-start | bytes 3932168 | tf_op jit(solution)/shard_map/ppermute | solution.py:58
  181.2 4.5 %all-to-all-done.2 = bf16[16,40,1024]{2,1,0:T(8,128)(2,1)} async-done(((bf16[16,40,1024]{2,1,0:T(8,128)(2,1)}), bf16[16,40,1024]{2,1,0:T(8,128)(2,1)}, u32[]{:S(2)}, u32[]{:S(2)}) %all-to-all-start.2) | async-done | bytes 1310752 | tf_op jit(solution)/shard_map/all_to_all | solution.py:54
  185.7 19.0 %collective-permute-start.22 = (bf16[4,160,1024]{2,1,0:T(8,128)(2,1)}, bf16[4,160,1024]{2,1,0:T(8,128)(2,1)S(1)}, u32[]{:S(2)}, u32[]{:S(2)}) collective-permute-start(bf16[4,160,1024]{2,1,0:T(8,128)(2,1)} %bitcast.11.own_s), channel_id=1, source_target_pairs={{0,1},{1,0},{2,3},{3,2},{4,5},{5,4},{6,7},{7,6},{8,9},{9,8},{10,11... | collective-permute-start | bytes 3932168 | tf_op jit(solution)/shard_map/ppermute | solution.py:58
  204.6 13.2 %collective-permute-done.23.n1 = bf16[768,1024]{1,0:T(8,128)(2,1)S(1)} collective-permute-done((bf16[768,1024]{1,0:T(8,128)(2,1)}, bf16[768,1024]{1,0:T(8,128)(2,1)S(1)}, u32[]{:S(2)}, u32[]{:S(2)}) %collective-permute-start.23) | collective-permute-done | bytes 1572896 | tf_op jit(solution)/shard_map/ppermute | solution.py:50
  218.3 4.0 %shard_map.119 = (bf16[256,1024]{1,0:T(8,128)(2,1)}, bf16[256,1024]{1,0:T(8,128)(2,1)}, bf16[1024,256]{1,0:T(8,128)(2,1)}) custom-call(bf16[768,1024]{1,0:T(8,128)(2,1)} %get-tuple-element.50.n0, bf16[768,1024]{1,0:T(8,128)(2,1)S(1)} %collective-permute-done.23.n1, bf16[768,1024]{1,0:T(8,128)(2,1)S(1)} %collective-permute-done.24.n2, ...), custom_call_target="tpu_custom_call" | custom-call | tf_op jit(solution)/shard_map/pallas_call | solution.py:84
  222.3 5.2 %shard_map.118 = (bf16[128,4096]{1,0:T(8,128)(2,1)}, bf16[128,4096]{1,0:T(8,128)(2,1)}) custom-call(s32[3]{0:T(128)S(1)} %pad_add_fusion.pos, bf16[128,2]{1,0:T(8,128)(2,1)S(1)} %copy-done.4, bf16[128,2]{1,0:T(8,128)(2,1)S(1)} %copy-done.6, bf16[4,160,1024]{2,1,0:T(8,128)(2,1)} %bitcast.9.own_m, bf16[4,160,1024]{2,1,0:T(8,128)(2,1)} %bitcast.11.own_s, ...), custom_call_target="tpu_custom_call" | custom-call | tf_op jit(solution)/shard_map/pallas_call | solution.py:84
  (71 shorter events, 20.0 us)
Async XLA Ops:
  0.6 5.5 %collective-permute-start.1 = (bf16[128,4096]{1,0:T(8,128)(2,1)}, bf16[128,4096]{1,0:T(8,128)(2,1)S(1)}, u32[]{:S(2)}, u32[]{:S(2)}) collective-permute-start(bf16[128,4096]{1,0:T(8,128)(2,1)} %tok_a.1), channel_id=1, source_target_pairs={{0,1},{1,0},{2,3},{3,2},{4,5},{5,4},{6,7},{7,6},{8,9},{9,8},{10,11... | collective-permute-start | bytes 3145736 | tf_op jit(solution)/shard_map/ppermute | solution.py:58
  2.1 4.1 %collective-permute-start.2 = (bf16[128,4096]{1,0:T(8,128)(2,1)}, bf16[128,4096]{1,0:T(8,128)(2,1)S(1)}, u32[]{:S(2)}, u32[]{:S(2)}) collective-permute-start(bf16[128,4096]{1,0:T(8,128)(2,1)} %cot_a.1), channel_id=1, source_target_pairs={{0,1},{1,0},{2,3},{3,2},{4,5},{5,4},{6,7},{7,6},{8,9},{9,8},{10,11... | collective-permute-start | bytes 3145736 | tf_op jit(solution)/shard_map/ppermute | solution.py:58
  3.6 2.5 %collective-permute-start = (bf16[128,2]{1,0:T(8,128)(2,1)S(1)}, bf16[128,2]{1,0:T(8,128)(2,1)S(1)}, u32[]{:S(2)}, u32[]{:S(2)}) collective-permute-start(bf16[128,2]{1,0:T(8,128)(2,1)S(1)} %copy.16.meta_a), channel_id=1, source_target_pairs={{0,1},{1,0},{2,3},{3,2},{4,5},{5,4},{6,7},{7,6},{8,9},{9,8},{10,11... | collective-permute-start | bytes 1544 | tf_op jit(solution)/shard_map/ppermute | solution.py:58
  11.1 58.7 %all-to-all-start = ((bf16[16,72,1024]{2,1,0:T(8,128)(2,1)}), bf16[16,72,1024]{2,1,0:T(8,128)(2,1)S(1)}, u32[]{:S(2)}, u32[]{:S(2)}) async-start(bf16[16,72,1024]{2,1,0:T(8,128)(2,1)} %bitcast.17), calls=%async_computation | async-start | bytes 4718592 | tf_op jit(solution)/shard_map/all_to_all | solution.py:54
  20.2 28.1 %collective-permute-start.10 = (bf16[512,1024]{1,0:T(8,128)(2,1)}, bf16[512,1024]{1,0:T(8,128)(2,1)}, u32[]{:S(2)}, u32[]{:S(2)}) collective-permute-start(bf16[512,1024]{1,0:T(8,128)(2,1)} %pad_maximum_fusion.w0), channel_id=1, source_target_pairs={{96,0},{0,32},{32,64},{64,96},{25,1},{1,9},{9,17},{17,25},{98,2},{... | collective-permute-start | bytes 3145736 | tf_op jit(solution)/shard_map/ppermute | solution.py:50
  21.4 27.9 %collective-permute-start.3 = (bf16[1024,256]{1,0:T(8,128)(2,1)S(1)}, bf16[1024,256]{1,0:T(8,128)(2,1)S(1)}, u32[]{:S(2)}, u32[]{:S(2)}) collective-permute-start(bf16[1024,256]{1,0:T(8,128)(2,1)S(1)} %bitcast.21), channel_id=1, source_target_pairs={{32,0},{64,32},{96,64},{0,96},{9,1},{17,9},{25,17},{1,25},{34,2},{... | collective-permute-start | bytes 1572872 | tf_op jit(solution)/shard_map/ppermute | solution.py:50
  22.9 52.4 %collective-permute-start.9 = (bf16[512,1024]{1,0:T(8,128)(2,1)}, bf16[512,1024]{1,0:T(8,128)(2,1)}, u32[]{:S(2)}, u32[]{:S(2)}) collective-permute-start(bf16[512,1024]{1,0:T(8,128)(2,1)} %pad_maximum_fusion.w0), channel_id=1, source_target_pairs={{32,0},{64,32},{96,64},{0,96},{9,1},{17,9},{25,17},{1,25},{34,2},{... | collective-permute-start | bytes 3145736 | tf_op jit(solution)/shard_map/ppermute | solution.py:50
  48.3 26.9 %collective-permute-start.11 = (bf16[512,1024]{1,0:T(8,128)(2,1)}, bf16[512,1024]{1,0:T(8,128)(2,1)}, u32[]{:S(2)}, u32[]{:S(2)}) collective-permute-start(bf16[512,1024]{1,0:T(8,128)(2,1)} %collective-permute-done.10.w3), channel_id=1, source_target_pairs={{96,0},{0,32},{32,64},{64,96},{25,1},{1,9},{9,17},{17,25},{98,2},{... | collective-permute-start | bytes 3145736 | tf_op jit(solution)/shard_map/ppermute | solution.py:50
  48.3 20.7 %collective-permute-start.5 = (bf16[1024,256]{1,0:T(8,128)(2,1)S(1)}, bf16[1024,256]{1,0:T(8,128)(2,1)S(1)}, u32[]{:S(2)}, u32[]{:S(2)}) collective-permute-start(bf16[1024,256]{1,0:T(8,128)(2,1)S(1)} %bitcast.22), channel_id=1, source_target_pairs={{96,0},{0,32},{32,64},{64,96},{25,1},{1,9},{9,17},{17,25},{98,2},{... | collective-permute-start | bytes 1572872 | tf_op jit(solution)/shard_map/ppermute | solution.py:50
  49.3 19.7 %copy-start.8 = (bf16[1024,256]{1,0:T(8,128)(2,1)}, bf16[1024,256]{1,0:T(8,128)(2,1)S(1)}, u32[]{:S(2)}) copy-start(bf16[1024,256]{1,0:T(8,128)(2,1)S(1)} %collective-permute-done.3.d1) | copy-start | bytes 1572868
  49.3 20.5 %collective-permute-start.4 = (bf16[1024,256]{1,0:T(8,128)(2,1)S(1)}, bf16[1024,256]{1,0:T(8,128)(2,1)}, u32[]{:S(2)}, u32[]{:S(2)}) collective-permute-start(bf16[1024,256]{1,0:T(8,128)(2,1)S(1)} %collective-permute-done.3.d1), channel_id=1, source_target_pairs={{32,0},{64,32},{96,64},{0,96},{9,1},{17,9},{25,17},{1,25},{34,2},{... | collective-permute-start | bytes 1572872 | tf_op jit(solution)/shard_map/ppermute | solution.py:50
  73.4 13.3 %collective-permute-start.6 = (bf16[144,1024]{1,0:T(8,128)(2,1)S(1)}, bf16[144,1024]{1,0:T(8,128)(2,1)S(1)}, u32[]{:S(2)}, u32[]{:S(2)}) collective-permute-start(bf16[144,1024]{1,0:T(8,128)(2,1)S(1)} %get-tuple-element.32), channel_id=1, source_target_pairs={{24,0},{0,8},{8,16},{16,24},{97,1},{1,33},{33,65},{65,97},{26,2},{... | collective-permute-start | bytes 884744 | tf_op jit(solution)/shard_map/ppermute | solution.py:50
  81.7 23.5 %collective-permute-start.12 = (bf16[144,2048]{1,0:T(8,128)(2,1)S(1)}, bf16[144,2048]{1,0:T(8,128)(2,1)S(1)}, u32[]{:S(2)}, u32[]{:S(2)}) collective-permute-start(bf16[144,2048]{1,0:T(8,128)(2,1)S(1)} %get-tuple-element.36), channel_id=1, source_target_pairs={{24,0},{0,8},{8,16},{16,24},{97,1},{1,33},{33,65},{65,97},{26,2},{... | collective-permute-start | bytes 1769480 | tf_op jit(solution)/shard_map/ppermute | solution.py:50
  81.8 23.5 %collective-permute-start.13 = (bf16[144,2048]{1,0:T(8,128)(2,1)S(1)}, bf16[144,2048]{1,0:T(8,128)(2,1)S(1)}, u32[]{:S(2)}, u32[]{:S(2)}) collective-permute-start(bf16[144,2048]{1,0:T(8,128)(2,1)S(1)} %get-tuple-element.37), channel_id=1, source_target_pairs={{16,0},{24,8},{0,16},{8,24},{65,1},{97,33},{1,65},{33,97},{18,2},{... | collective-permute-start | bytes 1769480 | tf_op jit(solution)/shard_map/ppermute | solution.py:50
  84.4 20.9 %collective-permute-start.14 = (bf16[144,2048]{1,0:T(8,128)(2,1)S(1)}, bf16[144,2048]{1,0:T(8,128)(2,1)S(1)}, u32[]{:S(2)}, u32[]{:S(2)}) collective-permute-start(bf16[144,2048]{1,0:T(8,128)(2,1)S(1)} %get-tuple-element.38), channel_id=1, source_target_pairs={{8,0},{16,8},{24,16},{0,24},{33,1},{65,33},{97,65},{1,97},{10,2},{... | collective-permute-start | bytes 1769480 | tf_op jit(solution)/shard_map/ppermute | solution.py:50
  86.4 15.0 %collective-permute-start.7 = (bf16[144,1024]{1,0:T(8,128)(2,1)S(1)}, bf16[144,1024]{1,0:T(8,128)(2,1)S(1)}, u32[]{:S(2)}, u32[]{:S(2)}) collective-permute-start(bf16[144,1024]{1,0:T(8,128)(2,1)S(1)} %get-tuple-element.33), channel_id=1, source_target_pairs={{16,0},{24,8},{0,16},{8,24},{65,1},{97,33},{1,65},{33,97},{18,2},{... | collective-permute-start | bytes 884744 | tf_op jit(solution)/shard_map/ppermute | solution.py:50
  86.8 18.5 %collective-permute-start.8 = (bf16[144,1024]{1,0:T(8,128)(2,1)S(1)}, bf16[144,1024]{1,0:T(8,128)(2,1)S(1)}, u32[]{:S(2)}, u32[]{:S(2)}) collective-permute-start(bf16[144,1024]{1,0:T(8,128)(2,1)S(1)} %get-tuple-element.34), channel_id=1, source_target_pairs={{8,0},{16,8},{24,16},{0,24},{33,1},{65,33},{97,65},{1,97},{10,2},{... | collective-permute-start | bytes 884744 | tf_op jit(solution)/shard_map/ppermute | solution.py:50
  106.0 24.8 %copy-start.2 = (bf16[144,2048]{1,0:T(8,128)(2,1)}, bf16[144,2048]{1,0:T(8,128)(2,1)S(1)}, u32[]{:S(2)}) copy-start(bf16[144,2048]{1,0:T(8,128)(2,1)S(1)} %get-tuple-element.46.a0) | copy-start | bytes 1769476
  106.0 9.1 %collective-permute-start.15 = (bf16[144,1024]{1,0:T(8,128)(2,1)S(1)}, bf16[144,1024]{1,0:T(8,128)(2,1)S(1)}, u32[]{:S(2)}, u32[]{:S(2)}) collective-permute-start(bf16[144,1024]{1,0:T(8,128)(2,1)S(1)} %get-tuple-element.39.a0), channel_id=1, source_target_pairs={{8,0},{16,8},{24,16},{0,24},{33,1},{65,33},{97,65},{1,97},{10,2},{... | collective-permute-start | bytes 884744 | tf_op jit(solution)/shard_map/ppermute | solution.py:50
  108.3 7.4 %collective-permute-start.16 = (bf16[144,1024]{1,0:T(8,128)(2,1)S(1)}, bf16[144,1024]{1,0:T(8,128)(2,1)S(1)}, u32[]{:S(2)}, u32[]{:S(2)}) collective-permute-start(bf16[144,1024]{1,0:T(8,128)(2,1)S(1)} %get-tuple-element.39.a0), channel_id=1, source_target_pairs={{16,0},{24,8},{0,16},{8,24},{65,1},{97,33},{1,65},{33,97},{18,2},{... | collective-permute-start | bytes 884744 | tf_op jit(solution)/shard_map/ppermute | solution.py:50
  109.2 9.7 %collective-permute-start.17 = (bf16[144,1024]{1,0:T(8,128)(2,1)S(1)}, bf16[144,1024]{1,0:T(8,128)(2,1)S(1)}, u32[]{:S(2)}, u32[]{:S(2)}) collective-permute-start(bf16[144,1024]{1,0:T(8,128)(2,1)S(1)} %get-tuple-element.39.a0), channel_id=1, source_target_pairs={{24,0},{0,8},{8,16},{16,24},{97,1},{1,33},{33,65},{65,97},{26,2},{... | collective-permute-start | bytes 884744 | tf_op jit(solution)/shard_map/ppermute | solution.py:50
  123.3 8.2 %copy-start.1 = (bf16[576,1024]{1,0:T(8,128)(2,1)S(1)}, bf16[576,1024]{1,0:T(8,128)(2,1)}, u32[]{:S(2)}) copy-start(bf16[576,1024]{1,0:T(8,128)(2,1)} %copy-done) | copy-start | bytes 3538948
  123.3 44.8 %all-to-all-start.1 = ((bf16[16,40,1024]{2,1,0:T(8,128)(2,1)}), bf16[16,40,1024]{2,1,0:T(8,128)(2,1)}, u32[]{:S(2)}, u32[]{:S(2)}) async-start(bf16[16,40,1024]{2,1,0:T(8,128)(2,1)} %bitcast.23), calls=%async_computation.1 | async-start | bytes 2621440 | tf_op jit(solution)/shard_map/all_to_all | solution.py:54
  127.9 16.2 %collective-permute-start.18 = (bf16[144,2048]{1,0:T(8,128)(2,1)S(1)}, bf16[144,2048]{1,0:T(8,128)(2,1)S(1)}, u32[]{:S(2)}, u32[]{:S(2)}) collective-permute-start(bf16[144,2048]{1,0:T(8,128)(2,1)S(1)} %get-tuple-element.46.a0), channel_id=1, source_target_pairs={{8,0},{16,8},{24,16},{0,24},{33,1},{65,33},{97,65},{1,97},{10,2},{... | collective-permute-start | bytes 1769480 | tf_op jit(solution)/shard_map/ppermute | solution.py:50
  130.3 15.2 %collective-permute-start.19 = (bf16[144,2048]{1,0:T(8,128)(2,1)S(1)}, bf16[144,2048]{1,0:T(8,128)(2,1)S(1)}, u32[]{:S(2)}, u32[]{:S(2)}) collective-permute-start(bf16[144,2048]{1,0:T(8,128)(2,1)S(1)} %get-tuple-element.46.a0), channel_id=1, source_target_pairs={{16,0},{24,8},{0,16},{8,24},{65,1},{97,33},{1,65},{33,97},{18,2},{... | collective-permute-start | bytes 1769480 | tf_op jit(solution)/shard_map/ppermute | solution.py:50
  130.9 20.7 %collective-permute-start.20 = (bf16[144,2048]{1,0:T(8,128)(2,1)S(1)}, bf16[144,2048]{1,0:T(8,128)(2,1)S(1)}, u32[]{:S(2)}, u32[]{:S(2)}) collective-permute-start(bf16[144,2048]{1,0:T(8,128)(2,1)S(1)} %get-tuple-element.46.a0), channel_id=1, source_target_pairs={{24,0},{0,8},{8,16},{16,24},{97,1},{1,33},{33,65},{65,97},{26,2},{... | collective-permute-start | bytes 1769480 | tf_op jit(solution)/shard_map/ppermute | solution.py:50
  168.1 17.6 %all-to-all-start.2 = ((bf16[16,40,1024]{2,1,0:T(8,128)(2,1)}), bf16[16,40,1024]{2,1,0:T(8,128)(2,1)}, u32[]{:S(2)}, u32[]{:S(2)}) async-start(bf16[16,40,1024]{2,1,0:T(8,128)(2,1)} %bitcast.18), calls=%async_computation.2 | async-start | bytes 2621440 | tf_op jit(solution)/shard_map/all_to_all | solution.py:54
  172.9 44.9 %collective-permute-start.23 = (bf16[768,1024]{1,0:T(8,128)(2,1)}, bf16[768,1024]{1,0:T(8,128)(2,1)S(1)}, u32[]{:S(2)}, u32[]{:S(2)}) collective-permute-start(bf16[768,1024]{1,0:T(8,128)(2,1)} %get-tuple-element.51), channel_id=1, source_target_pairs={{96,0},{0,32},{32,64},{64,96},{25,1},{1,9},{9,17},{17,25},{98,2},{... | collective-permute-start | bytes 4718600 | tf_op jit(solution)/shard_map/ppermute | solution.py:50
  173.0 44.8 %collective-permute-start.24 = (bf16[768,1024]{1,0:T(8,128)(2,1)}, bf16[768,1024]{1,0:T(8,128)(2,1)S(1)}, u32[]{:S(2)}, u32[]{:S(2)}) collective-permute-start(bf16[768,1024]{1,0:T(8,128)(2,1)} %get-tuple-element.52), channel_id=1, source_target_pairs={{64,0},{96,32},{0,64},{32,96},{17,1},{25,9},{1,17},{9,25},{66,2},{... | collective-permute-start | bytes 4718600 | tf_op jit(solution)/shard_map/ppermute | solution.py:50
  175.5 42.8 %collective-permute-start.25 = (bf16[768,1024]{1,0:T(8,128)(2,1)}, bf16[768,1024]{1,0:T(8,128)(2,1)}, u32[]{:S(2)}, u32[]{:S(2)}) collective-permute-start(bf16[768,1024]{1,0:T(8,128)(2,1)} %get-tuple-element.53), channel_id=1, source_target_pairs={{32,0},{64,32},{96,64},{0,96},{9,1},{17,9},{25,17},{1,25},{34,2},{... | collective-permute-start | bytes 4718600 | tf_op jit(solution)/shard_map/ppermute | solution.py:50
  175.7 46.6 %collective-permute-start.21 = (bf16[4,160,1024]{2,1,0:T(8,128)(2,1)}, bf16[4,160,1024]{2,1,0:T(8,128)(2,1)}, u32[]{:S(2)}, u32[]{:S(2)}) collective-permute-start(bf16[4,160,1024]{2,1,0:T(8,128)(2,1)} %bitcast.9.own_m), channel_id=1, source_target_pairs={{0,1},{1,0},{2,3},{3,2},{4,5},{5,4},{6,7},{7,6},{8,9},{9,8},{10,11... | collective-permute-start | bytes 3932168 | tf_op jit(solution)/shard_map/ppermute | solution.py:58
  185.7 36.6 %collective-permute-start.22 = (bf16[4,160,1024]{2,1,0:T(8,128)(2,1)}, bf16[4,160,1024]{2,1,0:T(8,128)(2,1)S(1)}, u32[]{:S(2)}, u32[]{:S(2)}) collective-permute-start(bf16[4,160,1024]{2,1,0:T(8,128)(2,1)} %bitcast.11.own_s), channel_id=1, source_target_pairs={{0,1},{1,0},{2,3},{3,2},{4,5},{5,4},{6,7},{7,6},{8,9},{9,8},{10,11... | collective-permute-start | bytes 3932168 | tf_op jit(solution)/shard_map/ppermute | solution.py:58
  (12 other events, 55.0 us)

commit v4 on v3

v4 whole, which is shorter than its diff:
```python
import functools

import jax
import jax.numpy as jnp
from jax import lax
from jax.experimental import pallas as pl
from jax.experimental.pallas import tpu as pltpu
from jax.sharding import Mesh
from jax.sharding import PartitionSpec as P


AXES = ("y", "x", "z", "c")
BF = jnp.bfloat16
F32 = jnp.float32
SIDE = 4
TOK = 128
BLK = 256
FF = 1024
SLOT = 36
PAIR = 2 * SLOT
PART = SLOT // 2
SHARE = SIDE * PART
SENT = SIDE * PAIR
ROWS = SIDE * SHARE
WIDE = SIDE * BLK


def place(y, x, z, c):
    return ((y * SIDE + x) * SIDE + z) * 2 + c


def groups():
    n = range(SIDE)
    feature, copies, spread = [], [], []
    for k in n:
        for z in n:
            feature.append([place(k, x, z, 0) for x in n])
            feature.append([place(y, k, z, 1) for y in n])
            copies.append([place(y, k, z, 0) for y in n])
            copies.append([place(k, x, z, 1) for x in n])
        spread.append([place(k, x, z, 0) for x in n for z in n])
        spread.append([place(y, k, z, 1) for y in n for z in n])
    return feature, copies, spread


FEATURE, COPIES, SPREAD = groups()


def shifted(value, rings, step):
    pairs = [(g[(i + step) % SIDE], g[i]) for g in rings for i in range(SIDE)]
    return lax.ppermute(value, AXES, pairs)


def grouped(value, rings):
    return lax.all_to_all(value, AXES, 0, 0, axis_index_groups=rings, tiled=True)


def other_core(value):
    return lax.ppermute(value, "c", [(0, 1), (1, 0)])


def iota(shape, dim):
    return lax.broadcasted_iota(jnp.int32, shape, dim)


def dot(a, b):
    return jnp.dot(a, b, preferred_element_type=F32)


def dot_nt(a, b):
    return lax.dot_general(a, b, (((1,), (1,)), ((), ())), preferred_element_type=F32)


def near(value):
    return pltpu.with_memory_space_constraint(value, pltpu.VMEM)


def far(value):
    return pltpu.with_memory_space_constraint(value, pltpu.HBM)


def call(body, outs, args, hbm=(), scratch=(), copies=0, smem=1, limit=20):
    vmem, raw = pl.BlockSpec(memory_space=pltpu.VMEM), pl.BlockSpec(memory_space=pl.ANY)
    specs = [pl.BlockSpec(memory_space=pltpu.SMEM)] * smem
    specs += [raw if isinstance(a, tuple) else vmem for a in args[smem:]]
    held = [pltpu.VMEM(dims, BF) for dims in scratch]
    return pl.pallas_call(
        body,
        out_shape=[(pltpu.HBM if n in hbm else pltpu.VMEM)(dims, BF) for n, dims in enumerate(outs)],
        in_specs=specs,
        out_specs=[raw if n in hbm else vmem for n in range(len(outs))],
        scratch_shapes=held + ([pltpu.SemaphoreType.DMA((copies,))] if copies else []),
        compiler_params=pltpu.CompilerParams(vmem_limit_bytes=limit * 2**20),
    )(*[far(a[0]) if isinstance(a, tuple) else a for a in args])


class Copies:
    def __init__(self, sems):
        self.sems, self.count, self.going = sems, 0, []

    def start(self, src, dst):
        copy = pltpu.make_async_copy(src, dst, self.sems.at[self.count])
        copy.start()
        self.count += 1
        return copy

    def send(self, src, dst):
        self.going.append(self.start(src, dst))

    def drain(self):
        for copy in self.going:
            copy.wait()


def column(kind, near, group, k):
    turned = (near + k) % SIDE
    return jnp.where(kind == 0, turned * SIDE + group, group * SIDE + turned)


def slots(route):
    count = route.shape[0]
    hits = (iota((count, 8), 1) == route).astype(F32)
    earlier = (iota((count, count), 1) < iota((count, count), 0)).astype(BF)
    return jnp.sum(dot(earlier, hits.astype(BF)) * hits, axis=1, keepdims=True).astype(jnp.int32)


def routes_of(*metas):
    return jnp.concatenate([m[:, 0:1] for m in metas], axis=0).astype(F32).astype(jnp.int32)


def pack_body(pos, meta_a, meta_b, tok_b, cot_b, tok_far, cot_far, out_far, tok_a, cot_a, out, sems):
    kind, at = pos[0], pos[1]
    copies = Copies(sems)
    loads = [copies.start(tok_far, tok_a), copies.start(cot_far, cot_a)]
    route = routes_of(meta_a, meta_b)
    target = jnp.where(route % 2 == kind, (route // 2) * PAIR + slots(route), -PAIR)
    rows = iota((2 * TOK, SENT), 1)
    pick_x = jnp.transpose((rows == target).astype(F32)).astype(BF)
    pick_y = jnp.transpose((rows == target + SLOT).astype(F32)).astype(BF)
    weight = jnp.concatenate([meta_a[:, 1:2], meta_b[:, 1:2]], axis=0).astype(F32)
    for load in loads:
        load.wait()
    for d in range(SIDE):
        for k in range(SIDE):
            src = pl.ds(pl.multiple_of(column(kind, at, d, k) * BLK, BLK), BLK)
            x = jnp.concatenate([tok_a[:, src], tok_b[:, src]], axis=0)
            y = jnp.concatenate([cot_a[:, src], cot_b[:, src]], axis=0).astype(F32)
            both = dot(pick_x, x) + dot(pick_y, (y * weight).astype(BF))
            out[d, :, k * BLK : (k + 1) * BLK] = both.astype(BF)
        copies.send(out.at[d], out_far.at[d])
    copies.drain()


def project_body(first, loads, pos, got, *refs):
    if loads:
        given, x, y, parts, kept, sems = refs[:13], refs[13], refs[14], refs[15:19], refs[19:27], refs[27]
        copies = Copies(sems)
        d0, d1, low, high, d3 = given[:5]
        halves = (slice(0, FF // 2), slice(FF // 2, FF))
        going = [copies.start(a, kept[k]) for k, a in ((0, d0), (1, d1), (3, d3))]
        going += [copies.start(a, kept[2].at[rows, :]) for a, rows in zip((low, high), halves)]
        first_up = len(going)
        for t in range(2):
            for k in range(SIDE):
                rows = slice(t * BLK, (t + 1) * BLK)
                going.append(copies.start(given[5 + t * SIDE + k], kept[SIDE + k].at[rows, :]))
    else:
        kept, x, y, parts = refs[:8], refs[8], refs[9], refs[10:14]
    ds, ws = kept[:SIDE], kept[SIDE:]
    q, r = iota((SHARE, SENT), 0), iota((SHARE, SENT), 1)
    home = q + (q // PART) * (PAIR - PART) + first
    for rows, take in ((x, (r == home).astype(BF)), (y, (r == home + SLOT).astype(BF))):
        for k in range(SIDE):
            rows[k * SHARE : (k + 1) * SHARE, :] = dot(take, got[(pos[2] + k) % SIDE]).astype(BF)
    for t in (2, 0, 1):
        if loads and t != 1:
            for copy in going[:first_up] if t == 2 else going[first_up:]:
                copy.wait()
        for n in range(FF // BLK):
            cols = slice(n * BLK, (n + 1) * BLK)
            total = 0.0
            for k in range(SIDE):
                block = slice(k * BLK, (k + 1) * BLK)
                if t == 2:
                    total = total + dot_nt(y[:, block], ds[k][cols, :])
                else:
                    total = total + dot(x[:, block], ws[k][t * BLK : (t + 1) * BLK, cols])
            total = total.astype(BF)
            for k, p in enumerate(parts):
                p[:, t * FF + n * BLK : t * FF + (n + 1) * BLK] = total[k * SHARE : (k + 1) * SHARE]


def activate_body(p0, p1, p2, p3, out):
    for n in range(FF // BLK):
        cols = [slice(t * FF + n * BLK, t * FF + (n + 1) * BLK) for t in range(3)]
        gate, upper, dact = [sum(p[:, c].astype(F32) for p in (p0, p1, p2, p3)) for c in cols]
        sig = jax.nn.sigmoid(gate)
        out[:, cols[0]] = (gate * sig * upper).astype(BF)
        out[:, cols[1]] = (dact * upper * sig * (1.0 + gate * (1.0 - sig))).astype(BF)
        out[:, cols[2]] = (dact * gate * sig).astype(BF)


def turn_body(x_a, x_b, y_a, y_b, xt, yt, own_far, sems):
    copies = Copies(sems)
    for n, (a, b, out) in enumerate(((x_a, x_b, xt), (y_a, y_b, yt))):
        for k in range(SIDE):
            cols = slice(k * BLK, (k + 1) * BLK)
            both = [v[m * SHARE : (m + 1) * SHARE, cols].astype(F32) for m in range(SIDE) for v in (a, b)]
            both = jnp.concatenate(both, axis=0)
            out[cols, :] = jnp.transpose(both).astype(BF)
        copies.send(out.at[0:BLK, :], own_far.at[n])
    copies.drain()


def block_grads(out, x, y, acts):
    out[0:BLK, :] = dot(x, acts[:, FF : 2 * FF]).astype(BF)
    out[BLK : 2 * BLK, :] = dot(x, acts[:, 2 * FF :]).astype(BF)
    out[2 * BLK :, :] = dot(y, acts[:, 0:FF]).astype(BF)


def first_grads_body(xt, yt, *refs):
    pieces, acts, out_far, out, sems = refs[: 2 * SIDE], *refs[2 * SIDE :]
    copies = Copies(sems)
    for n, a in enumerate(pieces):
        at = 2 * (n % SIDE) + n // SIDE
        acts[at * SHARE : (at + 1) * SHARE, :] = a[...]
    rows = slice(2 * BLK, 3 * BLK)
    block_grads(out, xt[rows, :], yt[rows, :], acts)
    copies.send(out, out_far)
    copies.drain()


def more_grads_body(xt, yt, acts, acts_far, one_far, three_far, one, three, sems):
    copies = Copies(sems)
    copies.send(acts, acts_far)
    for k, out, out_far in ((1, one, one_far), (3, three, three_far)):
        rows = slice(k * BLK, (k + 1) * BLK)
        block_grads(out, xt[rows, :], yt[rows, :], acts)
        copies.send(out, out_far)
    copies.drain()


def own_grads_body(turned_far, acts_far, out, turned, acts, sems):
    copies = Copies(sems)
    loads = [copies.start(turned_far, turned), copies.start(acts_far, acts)]
    for load in loads:
        load.wait()
    block_grads(out, turned[0], turned[1], acts)


def return_body(pos, acts, *refs):
    weights, back_far, res, slot, back, sems = refs[: 2 * SIDE], *refs[2 * SIDE :]
    copies = Copies(sems)
    for k in range(SIDE):
        d, w, cols = weights[k], weights[SIDE + k], slice(k * BLK, (k + 1) * BLK)
        res[:, cols] = dot(acts[:, 0:FF], d[...]).astype(BF)
        total = dot_nt(acts[:, FF : 2 * FF], w[0:BLK, :]) + dot_nt(acts[:, 2 * FF :], w[BLK:, :])
        slot[:, cols] = total.astype(BF)
    r, q = iota((SENT, 2 * SHARE), 0), iota((SENT, 2 * SHARE), 1)
    step, q = q // SHARE, q % SHARE
    home = q + (q // PART) * (PAIR - PART) + step * PART
    give_m, give_s = (r == home).astype(BF), (r == home + SLOT).astype(BF)
    for k in range(SIDE):
        rows = slice(2 * k * SHARE, 2 * (k + 1) * SHARE)
        back[k] = (dot(give_m, res[rows, :]) + dot(give_s, slot[rows, :])).astype(BF)
        copies.send(back.at[k], back_far.at[(pos[2] + k) % SIDE])
    copies.drain()


def unpack_body(pos, meta_a, meta_b, own, oth, mixed_far, grad_far, mixed, grad, sems):
    kind, at, across = pos[0], pos[1], pos[2]
    copies = Copies(sems)
    rows = iota((TOK, SENT), 1)

    def picks(route, core, mine):
        target = jnp.where(route % 2 == core, (route // 2) * PAIR + slots(route), -PAIR)[mine]
        return (rows == target).astype(BF), (rows == target + SLOT).astype(BF)

    own_m, own_s = picks(routes_of(meta_a, meta_b), kind, slice(0, TOK))
    oth_m, oth_s = picks(routes_of(meta_b, meta_a), 1 - kind, slice(TOK, 2 * TOK))
    weight = meta_a[:, 1:2].astype(F32)
    for b in range(SIDE * SIDE):
        major, minor = b // SIDE, b % SIDE
        own_d = jnp.where(kind == 0, minor, major)
        own_k = (jnp.where(kind == 0, major, minor) - at + SIDE) % SIDE
        oth_d = jnp.where(kind == 0, major, minor)
        oth_k = (jnp.where(kind == 0, minor, major) - across + SIDE) % SIDE
        o = own[own_d, :, pl.ds(pl.multiple_of(own_k * BLK, BLK), BLK)]
        t = oth[oth_d, :, pl.ds(pl.multiple_of(oth_k * BLK, BLK), BLK)]
        cols = slice(b * BLK, (b + 1) * BLK)
        mixed[:, cols] = ((dot(own_m, o) + dot(oth_m, t)) * weight).astype(BF)
        grad[:, cols] = (dot(own_s, o) + dot(oth_s, t)).astype(BF)
        if minor == SIDE - 1:
            done = pl.ds(major * WIDE, WIDE)
            copies.send(mixed.at[:, done], mixed_far.at[:, done])
            copies.send(grad.at[:, done], grad_far.at[:, done])
    copies.drain()


def total_body(n0, n1, n2, n3, gate_far, upper_far, down_far, gate, upper, down, sems):
    copies = Copies(sems)

    def total(t):
        rows = slice(t * BLK, (t + 1) * BLK)
        return sum(n[rows, :].astype(F32) for n in (n0, n1, n2, n3))

    down[...] = jnp.transpose(total(2)).astype(BF)
    copies.send(down, down_far)
    gate[...] = total(0).astype(BF)
    copies.send(gate, gate_far)
    upper[...] = total(1).astype(BF)
    copies.send(upper, upper_far)
    copies.drain()


def exchanged(value):
    rows = value.reshape(SIDE * SIDE, PAIR, WIDE)
    return near(grouped(rows, SPREAD).reshape(SIDE, SENT, WIDE))


def layer(tokens, probs, routes, w_gate, w_up, w_down, cotangent):
    y, x, c = lax.axis_index("y"), lax.axis_index("x"), lax.axis_index("c")
    pos = jnp.stack([c, jnp.where(c == 0, y, x), jnp.where(c == 0, x, y)]).astype(jnp.int32)
    meta = jnp.concatenate([routes.astype(BF), probs], axis=1)
    meta_b, tok_b, cot_b = other_core(meta), other_core(tokens), other_core(cotangent)
    d0, g0, u0 = w_down[0], w_gate[0], w_up[0]
    g1, g3 = shifted(g0, COPIES, 1), shifted(g0, COPIES, -1)
    u1, u3 = shifted(u0, COPIES, 1), shifted(u0, COPIES, -1)
    d1, d3 = shifted(d0, COPIES, 1), shifted(d0, COPIES, -1)
    half = FF // 2
    g2 = near(shifted(g3, COPIES, -1))
    u2 = near(shifted(u1, COPIES, 1))
    low, high = near(shifted(d1[:half], COPIES, 1)), near(shifted(d3[half:], COPIES, -1))
    weights = [(d0,), (d1,), low, high, (d3,), (g0,), (g1,), g2, (g3,), (u0,), (u1,), u2, (u3,)]
    (sent,) = call(
        pack_body,
        [(SIDE, SENT, WIDE)],
        [pos, meta, meta_b, near(tok_b), near(cot_b), (tokens,), (cotangent,)],
        hbm=(0,),
        scratch=[tokens.shape, tokens.shape, (SIDE, SENT, WIDE)],
        copies=2 + SIDE,
    )
    got = exchanged(sent)
    xs, ys, parts, pieces = [], [], [], []
    kept = weights
    for p in (0, 1):
        x, y, *part = call(
            functools.partial(project_body, p * PART, p == 0),
            [(ROWS, WIDE)] * 2 + [(SHARE, 3 * FF)] * SIDE + ([] if p else [(FF, BLK)] * SIDE + [(2 * BLK, FF)] * SIDE),
            [pos, got, *kept],
            copies=0 if p else len(weights),
        )
        if p == 0:
            part, kept = part[:SIDE], part[SIDE:]
        parts.append([part[0]] + [near(shifted(part[k], FEATURE, -k)) for k in (1, 2, 3)])
        xs.append(x)
        ys.append(y)
    for p in (0, 1):
        (act,) = call(activate_body, [(SHARE, 3 * FF)], parts[p], smem=0)
        pieces += [act] + [near(shifted(act, FEATURE, k)) for k in (1, 2, -1)]
    turned = (2, BLK, 2 * ROWS)
    block = (3 * BLK, FF)
    whole = (2 * ROWS, 3 * FF)
    xt, yt, own_t = call(turn_body, [(WIDE, 2 * ROWS)] * 2 + [turned], [*xs, *ys], smem=0, hbm=(2,), copies=2)
    acts, n2 = call(first_grads_body, [whole, block], [xt, yt, *pieces], smem=0, hbm=(1,), scratch=[block], copies=1)
    n2 = near(shifted(n2, COPIES, -2))
    acts_far, n1, n3 = call(
        more_grads_body,
        [whole, block, block],
        [xt, yt, near(acts)],
        smem=0,
        hbm=(0, 1, 2),
        scratch=[block] * 2,
        copies=3,
    )
    n1, n3 = near(shifted(n1, COPIES, -1)), near(shifted(n3, COPIES, 1))
    (back,) = call(
        return_body,
        [(SIDE, SENT, WIDE)],
        [pos, near(acts), *kept],
        hbm=(0,),
        scratch=[(2 * ROWS, WIDE)] * 2 + [(SIDE, SENT, WIDE)],
        copies=SIDE,
    )
    own = exchanged(back)
    (n0,) = call(own_grads_body, [block], [(own_t,), (acts_far,)], smem=0, scratch=[turned, whole], copies=2)
    ns = [n0, n1, n2, n3]
    oth = near(other_core(own))
    mixed, into = call(
        unpack_body,
        [tokens.shape] * 2,
        [pos, meta, meta_b, own, oth],
        hbm=(0, 1),
        scratch=[tokens.shape] * 2,
        copies=2 * SIDE,
    )
    shapes = [(BLK, FF), (BLK, FF), (FF, BLK)]
    gate, upper, down = call(total_body, shapes, ns, smem=0, hbm=(0, 1, 2), scratch=shapes, copies=3)
    return mixed, into, gate[None], upper[None], down[None]


def solution(mesh):
    finer = Mesh(mesh.devices.reshape(SIDE, SIDE, SIDE, 2), AXES)
    rows = P(AXES, None)
    wide = P(("z", "c"), ("y", "x"), None)
    tall = P(("z", "c"), None, ("y", "x"))
    return jax.shard_map(
        layer,
        mesh=finer,
        in_specs=(rows, rows, rows, wide, wide, tall, rows),
        out_specs=(rows, rows, wide, wide, tall),
        check_vma=False,
    )
```

time: 228 us -> 207 us (0.908)
  blocking collectives: 0 us -> 33.3 us
  waiting for transfers between devices: 106 us -> 77.4 us
  starting transfers between devices: 68.8 us -> 51.1 us
  Pallas kernels: 46.1 us -> 38.9 us
    all_to_all x0 -> x1, blocking collectives: none -> 33.3 us  [grouped(): lax.all_to_all(value, AXES, 0, 0, axis_index_groups=rings, tiled=True)]
    ppermute x21 -> x25, waiting for transfers between devices: 100 us -> 75.5 us  [shifted(): return lax.ppermute(value, AXES, pairs)]
    ppermute x5 -> x4, starting transfers between devices: 26.6 us -> 5.37 us  [other_core(): return lax.ppermute(value, 'c', [(0, 1), (1, 0)])]
    ppermute x21 -> x25, starting transfers between devices: 24.9 us -> 37.9 us  [shifted(): return lax.ppermute(value, AXES, pairs)]
    all_to_all x3 -> x1, starting transfers between devices: 17.4 us -> 7.89 us  [grouped(): lax.all_to_all(value, AXES, 0, 0, axis_index_groups=rings, tiled=True)]
    pallas_call x10 -> x12, Pallas kernels: 46.1 us -> 38.9 us  [call(): pl.pallas_call(body, out_shape=[(pltpu.HBM if n in hbm else pltpu.VMEM)(d...]
    all_to_all x3 -> x1, waiting for transfers between devices: 4.48 us -> 0.01 us  [grouped(): lax.all_to_all(value, AXES, 0, 0, axis_index_groups=rings, tiled=True)]
  transfers between devices with their start and end apart: 29 -> 30, of which waited for: 14 -> 15; matrix products, arithmetic and copies ran while one was open for 1% -> 1% of each run, Pallas kernels for 14% -> 8%
where the time goes in v4:
time: 207 us
  waiting for transfers between devices  77.4 us (37%)
  starting transfers between devices  51.1 us (25%)
  Pallas kernels  38.9 us (19%)
  blocking collectives  33.3 us (16%)
  local copies, waits for them, and re-layouts  3.49 us (2%)
    ppermute x25, waiting for transfers between devices, shifted(): return lax.ppermute(value, AXES, pairs)  75.5 us
    pallas_call x12, Pallas kernels, call(): pl.pallas_call(body, out_shape=[(pltpu.HBM if n in hbm else pltpu.VMEM)(d...  38.9 us
    ppermute x25, starting transfers between devices, shifted(): return lax.ppermute(value, AXES, pairs)  37.9 us
    all_to_all x1, blocking collectives, grouped(): lax.all_to_all(value, AXES, 0, 0, axis_index_groups=rings, tiled=True)  33.3 us
    all_to_all x1, starting transfers between devices, grouped(): lax.all_to_all(value, AXES, 0, 0, axis_index_groups=rings, tiled=True)  7.89 us
    ppermute x4, starting transfers between devices, other_core(): return lax.ppermute(value, 'c', [(0, 1), (1, 0)])  5.37 us
  transfers between devices with their start and end apart: 30, of which 15 were waited for; matrix products, arithmetic and copies ran while one was open for 1% of the time, Pallas kernels for 8%

profile of v4, /device:TPU:1, one launch (start us, length us, event | category | flops | bytes accessed | tf_op | source)
XLA Modules:
  0.0 206.7 jit_solution(5129380314945022074)
XLA Ops:
  4.2 1.9 collective-permute-done.meta_b
  6.1 4.5 %shard_map.110 = bf16[4,288,1024]{2,1,0:T(8,128)(2,1)} custom-call(s32[3]{0:T(128)S(1)} %pad_add_fusion.pos, bf16[128,2]{1,0:T(8,128)(2,1)S(1)} %copy.16.meta_a, bf16[128,2]{1,0:T(8,128)(2,1)S(1)} %collective-permute-done.meta_b, bf16[128,4096]{1,0:T(8,128)(2,1)S(1)} %collective-permute-done.1.tok_b, bf16[128,4096]{1,0:T(8,128)(2,1)S(1)} %collective-permute-done.2.cot_b, ...), custom_call_target="tpu_custom_call" | custom-call | tf_op jit(solution)/shard_map/pallas_call | solution.py:87
  10.7 7.9 %all-to-all-start = ((bf16[16,72,1024]{2,1,0:T(8,128)(2,1)}), bf16[16,72,1024]{2,1,0:T(8,128)(2,1)S(1)}, u32[]{:S(2)}, u32[]{:S(2)}) async-start(bf16[16,72,1024]{2,1,0:T(8,128)(2,1)} %bitcast.17), calls=%async_computation | async-start | bytes 4718592 | tf_op jit(solution)/shard_map/all_to_all | solution.py:55
  21.3 2.7 %collective-permute-start.3 = (bf16[1024,256]{1,0:T(8,128)(2,1)}, bf16[1024,256]{1,0:T(8,128)(2,1)S(1)}, u32[]{:S(2)}, u32[]{:S(2)}) collective-permute-start(bf16[1024,256]{1,0:T(8,128)(2,1)} %bitcast.5.refs_0_), channel_id=1, source_target_pairs={{32,0},{64,32},{96,64},{0,96},{9,1},{17,9},{25,17},{1,25},{34,2},{... | collective-permute-start | bytes 1572872 | tf_op jit(solution)/shard_map/ppermute | solution.py:51
  24.1 12.1 %collective-permute-done.8.refs_8_ = bf16[256,1024]{1,0:T(8,128)(2,1)S(1)} collective-permute-done((bf16[256,1024]{1,0:T(8,128)(2,1)}, bf16[256,1024]{1,0:T(8,128)(2,1)S(1)}, u32[]{:S(2)}, u32[]{:S(2)}) %collective-permute-start.8) | collective-permute-done | bytes 524320 | tf_op jit(solution)/shard_map/ppermute | solution.py:51
  36.3 6.2 %collective-permute-start.9 = (bf16[256,1024]{1,0:T(8,128)(2,1)S(1)}, bf16[256,1024]{1,0:T(8,128)(2,1)S(1)}, u32[]{:S(2)}, u32[]{:S(2)}) collective-permute-start(bf16[256,1024]{1,0:T(8,128)(2,1)S(1)} %collective-permute-done.8.refs_8_), channel_id=1, source_target_pairs={{96,0},{0,32},{32,64},{64,96},{25,1},{1,9},{9,17},{17,25},{98,2},{... | collective-permute-start | bytes 1572872 | tf_op jit(solution)/shard_map/ppermute | solution.py:51
  42.5 1.9 collective-permute-done.5.refs_4_
  44.4 3.0 %collective-permute-start.11 = (bf16[256,1024]{1,0:T(8,128)(2,1)S(1)}, bf16[256,1024]{1,0:T(8,128)(2,1)S(1)}, u32[]{:S(2)}, u32[]{:S(2)}) collective-permute-start(bf16[256,1024]{1,0:T(8,128)(2,1)S(1)} %collective-permute-done.10.refs_10_), channel_id=1, source_target_pairs={{32,0},{64,32},{96,64},{0,96},{9,1},{17,9},{25,17},{1,25},{34,2},{... | collective-permute-start | bytes 1572872 | tf_op jit(solution)/shard_map/ppermute | solution.py:51
  49.2 3.3 %collective-permute-done.7.refs_6_ = bf16[256,1024]{1,0:T(8,128)(2,1)S(1)} collective-permute-done((bf16[256,1024]{1,0:T(8,128)(2,1)}, bf16[256,1024]{1,0:T(8,128)(2,1)S(1)}, u32[]{:S(2)}, u32[]{:S(2)}) %collective-permute-start.7) | collective-permute-done | bytes 524320 | tf_op jit(solution)/shard_map/ppermute | solution.py:51
  53.9 6.6 %collective-permute-done.6.refs_3_ = bf16[512,256]{1,0:T(8,128)(2,1)S(1)} collective-permute-done((bf16[512,256]{1,0:T(8,128)(2,1)S(1)}, bf16[512,256]{1,0:T(8,128)(2,1)S(1)}, u32[]{:S(2)}, u32[]{:S(2)}) %collective-permute-start.6) | collective-permute-done | bytes 262176 | tf_op jit(solution)/shard_map/ppermute | solution.py:51
  63.9 4.5 %shard_map.111 = (bf16[288,1024]{1,0:T(8,128)(2,1)S(1)}, bf16[288,1024]{1,0:T(8,128)(2,1)S(1)}, bf16[72,3072]{1,0:T(8,128)(2,1)S(1)}, bf16[72,3072]{1,0:T(8,128)...) custom-call(s32[3]{0:T(128)S(1)} %pad_add_fusion.pos, ...), custom_call_target="tpu_custom_call" | custom-call | tf_op jit(solution)/shard_map/pallas_call | solution.py:87
  69.7 2.4 %collective-permute-start.14 = (bf16[72,3072]{1,0:T(8,128)(2,1)S(1)}, bf16[72,3072]{1,0:T(8,128)(2,1)S(1)}, u32[]{:S(2)}, u32[]{:S(2)}) collective-permute-start(bf16[72,3072]{1,0:T(8,128)(2,1)S(1)} %get-tuple-element.54), channel_id=1, source_target_pairs={{16,0},{24,8},{0,16},{8,24},{65,1},{97,33},{1,65},{33,97},{18,2},{... | collective-permute-start | bytes 1327112 | tf_op jit(solution)/shard_map/ppermute | solution.py:51
  73.3 3.7 %shard_map.112 = (bf16[288,1024]{1,0:T(8,128)(2,1)S(1)}, bf16[288,1024]{1,0:T(8,128)(2,1)S(1)}, bf16[72,3072]{1,0:T(8,128)(2,1)S(1)}, bf16[72,3072]{1,0:T(8,128)...) custom-call(s32[3]{0:T(128)S(1)} %pad_add_fusion.pos, bf16[4,288,1024]{2,1,0:T(8,128)(2,1)S(1)} %bitcast.14, ...), custom_call_target="tpu_custom_call" | custom-call | tf_op jit(solution)/shard_map/pallas_call | solution.py:87
  79.8 3.0 %collective-permute-done.14.p2 = bf16[72,3072]{1,0:T(8,128)(2,1)S(1)} collective-permute-done((bf16[72,3072]{1,0:T(8,128)(2,1)S(1)}, bf16[72,3072]{1,0:T(8,128)(2,1)S(1)}, u32[]{:S(2)}, u32[]{:S(2)}) %collective-permute-start.14) | collective-permute-done | bytes 442400 | tf_op jit(solution)/shard_map/ppermute | solution.py:51
  84.4 2.1 %collective-permute-start.17 = (bf16[72,3072]{1,0:T(8,128)(2,1)S(1)}, bf16[72,3072]{1,0:T(8,128)(2,1)S(1)}, u32[]{:S(2)}, u32[]{:S(2)}) collective-permute-start(bf16[72,3072]{1,0:T(8,128)(2,1)S(1)} %shard_map.114.refs_0_), channel_id=1, source_target_pairs={{16,0},{24,8},{0,16},{8,24},{65,1},{97,33},{1,65},{33,97},{18,2},{... | collective-permute-start | bytes 1327112 | tf_op jit(solution)/shard_map/ppermute | solution.py:51
  87.9 4.5 %collective-permute-done.20.p2 = bf16[72,3072]{1,0:T(8,128)(2,1)S(1)} collective-permute-done((bf16[72,3072]{1,0:T(8,128)(2,1)S(1)}, bf16[72,3072]{1,0:T(8,128)(2,1)S(1)}, u32[]{:S(2)}, u32[]{:S(2)}) %collective-permute-start.20) | collective-permute-done | bytes 442400 | tf_op jit(solution)/shard_map/ppermute | solution.py:51
  93.9 2.1 %collective-permute-start.23 = (bf16[72,3072]{1,0:T(8,128)(2,1)S(1)}, bf16[72,3072]{1,0:T(8,128)(2,1)S(1)}, u32[]{:S(2)}, u32[]{:S(2)}) collective-permute-start(bf16[72,3072]{1,0:T(8,128)(2,1)S(1)} %shard_map.115.refs_4_), channel_id=1, source_target_pairs={{16,0},{24,8},{0,16},{8,24},{65,1},{97,33},{1,65},{33,97},{18,2},{... | collective-permute-start | bytes 1327112 | tf_op jit(solution)/shard_map/ppermute | solution.py:51
  98.9 3.0 %collective-permute-done.17.refs_2_ = bf16[72,3072]{1,0:T(8,128)(2,1)S(1)} collective-permute-done((bf16[72,3072]{1,0:T(8,128)(2,1)S(1)}, bf16[72,3072]{1,0:T(8,128)(2,1)S(1)}, u32[]{:S(2)}, u32[]{:S(2)}) %collective-permute-start.17) | collective-permute-done | bytes 442400 | tf_op jit(solution)/shard_map/ppermute | solution.py:51
  101.9 4.6 %collective-permute-done.24.refs_7_ = bf16[72,3072]{1,0:T(8,128)(2,1)S(1)} collective-permute-done((bf16[72,3072]{1,0:T(8,128)(2,1)S(1)}, bf16[72,3072]{1,0:T(8,128)(2,1)S(1)}, u32[]{:S(2)}, u32[]{:S(2)}) %collective-permute-start.24) | collective-permute-done | bytes 442400 | tf_op jit(solution)/shard_map/ppermute | solution.py:51
  106.5 4.9 %collective-permute-done.23.refs_6_ = bf16[72,3072]{1,0:T(8,128)(2,1)S(1)} collective-permute-done((bf16[72,3072]{1,0:T(8,128)(2,1)S(1)}, bf16[72,3072]{1,0:T(8,128)(2,1)S(1)}, u32[]{:S(2)}, u32[]{:S(2)}) %collective-permute-start.23) | collective-permute-done | bytes 442400 | tf_op jit(solution)/shard_map/ppermute | solution.py:51
  111.4 2.6 %shard_map.116 = (bf16[576,3072]{1,0:T(8,128)(2,1)S(1)}, bf16[768,1024]{1,0:T(8,128)(2,1)}) custom-call(bf16[1024,576]{1,0:T(8,128)(2,1)S(1)} %get-tuple-element.50.xt, bf16[1024,576]{1,0:T(8,128)(2,1)S(1)} %get-tuple-element.51.yt, bf16[72,3072]{1,0:T(8,128)(2,1)S(1)} %shard_map.114.refs_0_, bf16[72,3072]{1,0:T(8,128)(2,1)S(1)} %collective-permute-done.16.refs_1_, ...), custom_call_target="tpu_custom_call" | custom-call | tf_op jit(solution)/shard_map/pallas_call | solution.py:87
  114.0 7.5 %shard_map.117 = bf16[4,288,1024]{2,1,0:T(8,128)(2,1)} custom-call(s32[3]{0:T(128)S(1)} %pad_add_fusion.pos, bf16[576,3072]{1,0:T(8,128)(2,1)S(1)} %get-tuple-element.60.acts, bf16[1024,256]{1,0:T(8,128)(2,1)S(1)} %get-tuple-element.39.refs_0_, bf16[1024,256]{1,0:T(8,128)(2,1)S(1)} %get-tuple-element.40.refs_1_, ...), custom_call_target="tpu_custom_call" | custom-call | tf_op jit(solution)/shard_map/pallas_call | solution.py:87
  121.4 33.3 %all_to_all.10 = bf16[16,72,1024]{2,1,0:T(8,128)(2,1)S(1)} all-to-all(bf16[16,72,1024]{2,1,0:T(8,128)(2,1)} %bitcast.18), channel_id=1, replica_groups={{0,2,4,6,8,10,12,14,16,18,20,22,24,26,28,30},{1,3,5,7,33,35,37,39,65,67..., dimensions={0} | all-to-all | bytes 4718592 | tf_op jit(solution)/shard_map/all_to_all | solution.py:55
  154.7 3.3 %collective-permute-start.25 = (bf16[4,288,1024]{2,1,0:T(8,128)(2,1)S(1)}, bf16[4,288,1024]{2,1,0:T(8,128)(2,1)S(1)}, u32[]{:S(2)}, u32[]{:S(2)}) collective-permute-start(bf16[4,288,1024]{2,1,0:T(8,128)(2,1)S(1)} %bitcast.15), channel_id=1, source_target_pairs={{0,1},{1,0},{2,3},{3,2},{4,5},{5,4},{6,7},{7,6},{8,9},{9,8},{10,11... | collective-permute-start | bytes 7077896 | tf_op jit(solution)/shard_map/ppermute | solution.py:59
  158.1 3.9 %shard_map.119 = (bf16[576,3072]{1,0:T(8,128)(2,1)}, bf16[768,1024]{1,0:T(8,128)(2,1)}, bf16[768,1024]{1,0:T(8,128)(2,1)}) custom-call(bf16[1024,576]{1,0:T(8,128)(2,1)S(1)} %get-tuple-element.50.xt, bf16[1024,576]{1,0:T(8,128)(2,1)S(1)} %get-tuple-element.51.yt, bf16[576,3072]{1,0:T(8,128)(2,1)S(1)} %get-tuple-element.60.acts), custom_call_target="tpu_custom_call" | custom-call | tf_op jit(solution)/shard_map/pallas_call | solution.py:87
  162.0 2.5 %collective-permute-start.27 = (bf16[768,1024]{1,0:T(8,128)(2,1)S(1)}, bf16[768,1024]{1,0:T(8,128)(2,1)S(1)}, u32[]{:S(2)}, u32[]{:S(2)}) collective-permute-start(bf16[768,1024]{1,0:T(8,128)(2,1)S(1)} %copy-done.10), channel_id=1, source_target_pairs={{64,0},{96,32},{0,64},{32,96},{17,1},{25,9},{1,17},{9,25},{66,2},{... | collective-permute-start | bytes 4718600 | tf_op jit(solution)/shard_map/ppermute | solution.py:51
  165.1 2.0 collective-permute-start.28
  167.1 3.6 %shard_map.120.n0 = bf16[768,1024]{1,0:T(8,128)(2,1)S(1)} custom-call(bf16[2,256,576]{2,1,0:T(8,128)(2,1)} %get-tuple-element.63.turned_far, bf16[576,3072]{1,0:T(8,128)(2,1)} %get-tuple-element.64.acts_far), custom_call_target="tpu_custom_call" | custom-call | tf_op jit(solution)/shard_map/pallas_call | solution.py:87
  170.7 12.4 %collective-permute-done.27.n2 = bf16[768,1024]{1,0:T(8,128)(2,1)S(1)} collective-permute-done((bf16[768,1024]{1,0:T(8,128)(2,1)S(1)}, bf16[768,1024]{1,0:T(8,128)(2,1)S(1)}, u32[]{:S(2)}, u32[]{:S(2)}) %collective-permute-start.27) | collective-permute-done | bytes 1572896 | tf_op jit(solution)/shard_map/ppermute | solution.py:51
  183.1 16.8 %collective-permute-done.26.n1 = bf16[768,1024]{1,0:T(8,128)(2,1)S(1)} collective-permute-done((bf16[768,1024]{1,0:T(8,128)(2,1)}, bf16[768,1024]{1,0:T(8,128)(2,1)S(1)}, u32[]{:S(2)}, u32[]{:S(2)}) %collective-permute-start.26) | collective-permute-done | bytes 1572896 | tf_op jit(solution)/shard_map/ppermute | solution.py:51
  200.1 2.1 %shard_map.121 = (bf16[256,1024]{1,0:T(8,128)(2,1)}, bf16[256,1024]{1,0:T(8,128)(2,1)}, bf16[1024,256]{1,0:T(8,128)(2,1)}) custom-call(bf16[768,1024]{1,0:T(8,128)(2,1)S(1)} %shard_map.120.n0, bf16[768,1024]{1,0:T(8,128)(2,1)S(1)} %collective-permute-done.26.n1, bf16[768,1024]{1,0:T(8,128)(2,1)S(1)} %collective-permute-done.27.n2, ...), custom_call_target="tpu_custom_call" | custom-call | tf_op jit(solution)/shard_map/pallas_call | solution.py:87
  202.2 4.2 %shard_map.118 = (bf16[128,4096]{1,0:T(8,128)(2,1)}, bf16[128,4096]{1,0:T(8,128)(2,1)}) custom-call(s32[3]{0:T(128)S(1)} %pad_add_fusion.pos, bf16[128,2]{1,0:T(8,128)(2,1)S(1)} %copy.16.meta_a, bf16[128,2]{1,0:T(8,128)(2,1)S(1)} %collective-permute-done.meta_b, bf16[4,288,1024]{2,1,0:T(8,128)(2,1)S(1)} %bitcast.16, ...), custom_call_target="tpu_custom_call" | custom-call | tf_op jit(solution)/shard_map/pallas_call | solution.py:87
  (69 shorter events, 26.4 us)
Async XLA Ops:
  0.6 5.5 %collective-permute-start.1 = (bf16[128,4096]{1,0:T(8,128)(2,1)}, bf16[128,4096]{1,0:T(8,128)(2,1)S(1)}, u32[]{:S(2)}, u32[]{:S(2)}) collective-permute-start(bf16[128,4096]{1,0:T(8,128)(2,1)} %tok_far.1), channel_id=1, source_target_pairs={{0,1},{1,0},{2,3},{3,2},{4,5},{5,4},{6,7},{7,6},{8,9},{9,8},{10,11... | collective-permute-start | bytes 3145736 | tf_op jit(solution)/shard_map/ppermute | solution.py:59
  2.1 4.0 %collective-permute-start.2 = (bf16[128,4096]{1,0:T(8,128)(2,1)}, bf16[128,4096]{1,0:T(8,128)(2,1)S(1)}, u32[]{:S(2)}, u32[]{:S(2)}) collective-permute-start(bf16[128,4096]{1,0:T(8,128)(2,1)} %cot_far.1), channel_id=1, source_target_pairs={{0,1},{1,0},{2,3},{3,2},{4,5},{5,4},{6,7},{7,6},{8,9},{9,8},{10,11... | collective-permute-start | bytes 3145736 | tf_op jit(solution)/shard_map/ppermute | solution.py:59
  3.6 2.5 %collective-permute-start = (bf16[128,2]{1,0:T(8,128)(2,1)S(1)}, bf16[128,2]{1,0:T(8,128)(2,1)S(1)}, u32[]{:S(2)}, u32[]{:S(2)}) collective-permute-start(bf16[128,2]{1,0:T(8,128)(2,1)S(1)} %copy.16.meta_a), channel_id=1, source_target_pairs={{0,1},{1,0},{2,3},{3,2},{4,5},{5,4},{6,7},{7,6},{8,9},{9,8},{10,11... | collective-permute-start | bytes 1544 | tf_op jit(solution)/shard_map/ppermute | solution.py:59
  10.7 51.3 %all-to-all-start = ((bf16[16,72,1024]{2,1,0:T(8,128)(2,1)}), bf16[16,72,1024]{2,1,0:T(8,128)(2,1)S(1)}, u32[]{:S(2)}, u32[]{:S(2)}) async-start(bf16[16,72,1024]{2,1,0:T(8,128)(2,1)} %bitcast.17), calls=%async_computation | async-start | bytes 4718592 | tf_op jit(solution)/shard_map/all_to_all | solution.py:55
  18.6 17.6 %collective-permute-start.8 = (bf16[256,1024]{1,0:T(8,128)(2,1)}, bf16[256,1024]{1,0:T(8,128)(2,1)S(1)}, u32[]{:S(2)}, u32[]{:S(2)}) collective-permute-start(bf16[256,1024]{1,0:T(8,128)(2,1)} %bitcast.6.refs_5_), channel_id=1, source_target_pairs={{96,0},{0,32},{32,64},{64,96},{25,1},{1,9},{9,17},{17,25},{98,2},{... | collective-permute-start | bytes 1572872 | tf_op jit(solution)/shard_map/ppermute | solution.py:51
  19.8 16.4 %collective-permute-start.10 = (bf16[256,1024]{1,0:T(8,128)(2,1)}, bf16[256,1024]{1,0:T(8,128)(2,1)S(1)}, u32[]{:S(2)}, u32[]{:S(2)}) collective-permute-start(bf16[256,1024]{1,0:T(8,128)(2,1)} %bitcast.7.refs_9_), channel_id=1, source_target_pairs={{32,0},{64,32},{96,64},{0,96},{9,1},{17,9},{25,17},{1,25},{34,2},{... | collective-permute-start | bytes 1572872 | tf_op jit(solution)/shard_map/ppermute | solution.py:51
  21.3 23.1 %collective-permute-start.5 = (bf16[1024,256]{1,0:T(8,128)(2,1)}, bf16[1024,256]{1,0:T(8,128)(2,1)S(1)}, u32[]{:S(2)}, u32[]{:S(2)}) collective-permute-start(bf16[1024,256]{1,0:T(8,128)(2,1)} %bitcast.5.refs_0_), channel_id=1, source_target_pairs={{96,0},{0,32},{32,64},{64,96},{25,1},{1,9},{9,17},{17,25},{98,2},{... | collective-permute-start | bytes 1572872 | tf_op jit(solution)/shard_map/ppermute | solution.py:51
  21.3 26.1 %collective-permute-start.3 = (bf16[1024,256]{1,0:T(8,128)(2,1)}, bf16[1024,256]{1,0:T(8,128)(2,1)S(1)}, u32[]{:S(2)}, u32[]{:S(2)}) collective-permute-start(bf16[1024,256]{1,0:T(8,128)(2,1)} %bitcast.5.refs_0_), channel_id=1, source_target_pairs={{32,0},{64,32},{96,64},{0,96},{9,1},{17,9},{25,17},{1,25},{34,2},{... | collective-permute-start | bytes 1572872 | tf_op jit(solution)/shard_map/ppermute | solution.py:51
  24.0 28.5 %collective-permute-start.7 = (bf16[256,1024]{1,0:T(8,128)(2,1)}, bf16[256,1024]{1,0:T(8,128)(2,1)S(1)}, u32[]{:S(2)}, u32[]{:S(2)}) collective-permute-start(bf16[256,1024]{1,0:T(8,128)(2,1)} %bitcast.6.refs_5_), channel_id=1, source_target_pairs={{32,0},{64,32},{96,64},{0,96},{9,1},{17,9},{25,17},{1,25},{34,2},{... | collective-permute-start | bytes 1572872 | tf_op jit(solution)/shard_map/ppermute | solution.py:51
  36.2 25.7 %copy-start.6 = (bf16[256,1024]{1,0:T(8,128)(2,1)}, bf16[256,1024]{1,0:T(8,128)(2,1)S(1)}, u32[]{:S(2)}) copy-start(bf16[256,1024]{1,0:T(8,128)(2,1)S(1)} %collective-permute-done.8.refs_8_) | copy-start | bytes 1572868
  36.2 17.7 %collective-permute-start.12 = (bf16[256,1024]{1,0:T(8,128)(2,1)}, bf16[256,1024]{1,0:T(8,128)(2,1)S(1)}, u32[]{:S(2)}, u32[]{:S(2)}) collective-permute-start(bf16[256,1024]{1,0:T(8,128)(2,1)} %bitcast.7.refs_9_), channel_id=1, source_target_pairs={{96,0},{0,32},{32,64},{64,96},{25,1},{1,9},{9,17},{17,25},{98,2},{... | collective-permute-start | bytes 1572872 | tf_op jit(solution)/shard_map/ppermute | solution.py:51
  36.3 25.7 %copy-start.7 = (bf16[256,1024]{1,0:T(8,128)(2,1)}, bf16[256,1024]{1,0:T(8,128)(2,1)S(1)}, u32[]{:S(2)}) copy-start(bf16[256,1024]{1,0:T(8,128)(2,1)S(1)} %collective-permute-done.10.refs_10_) | copy-start | bytes 1572868
  36.3 25.6 %collective-permute-start.9 = (bf16[256,1024]{1,0:T(8,128)(2,1)S(1)}, bf16[256,1024]{1,0:T(8,128)(2,1)S(1)}, u32[]{:S(2)}, u32[]{:S(2)}) collective-permute-start(bf16[256,1024]{1,0:T(8,128)(2,1)S(1)} %collective-permute-done.8.refs_8_), channel_id=1, source_target_pairs={{96,0},{0,32},{32,64},{64,96},{25,1},{1,9},{9,17},{17,25},{98,2},{... | collective-permute-start | bytes 1572872 | tf_op jit(solution)/shard_map/ppermute | solution.py:51
  44.4 17.5 %collective-permute-start.11 = (bf16[256,1024]{1,0:T(8,128)(2,1)S(1)}, bf16[256,1024]{1,0:T(8,128)(2,1)S(1)}, u32[]{:S(2)}, u32[]{:S(2)}) collective-permute-start(bf16[256,1024]{1,0:T(8,128)(2,1)S(1)} %collective-permute-done.10.refs_10_), channel_id=1, source_target_pairs={{32,0},{64,32},{96,64},{0,96},{9,1},{17,9},{25,17},{1,25},{34,2},{... | collective-permute-start | bytes 1572872 | tf_op jit(solution)/shard_map/ppermute | solution.py:51
  47.5 13.0 %collective-permute-start.6 = (bf16[512,256]{1,0:T(8,128)(2,1)S(1)}, bf16[512,256]{1,0:T(8,128)(2,1)S(1)}, u32[]{:S(2)}, u32[]{:S(2)}) collective-permute-start(bf16[512,256]{1,0:T(8,128)(2,1)S(1)} %slice.9), channel_id=1, source_target_pairs={{96,0},{0,32},{32,64},{64,96},{25,1},{1,9},{9,17},{17,25},{98,2},{... | collective-permute-start | bytes 786440 | tf_op jit(solution)/shard_map/ppermute | solution.py:51
  52.5 8.8 %collective-permute-start.4 = (bf16[512,256]{1,0:T(8,128)(2,1)S(1)}, bf16[512,256]{1,0:T(8,128)(2,1)S(1)}, u32[]{:S(2)}, u32[]{:S(2)}) collective-permute-start(bf16[512,256]{1,0:T(8,128)(2,1)S(1)} %slice.8), channel_id=1, source_target_pairs={{32,0},{64,32},{96,64},{0,96},{9,1},{17,9},{25,17},{1,25},{34,2},{... | collective-permute-start | bytes 786440 | tf_op jit(solution)/shard_map/ppermute | solution.py:51
  68.4 9.8 %collective-permute-start.13 = (bf16[72,3072]{1,0:T(8,128)(2,1)S(1)}, bf16[72,3072]{1,0:T(8,128)(2,1)S(1)}, u32[]{:S(2)}, u32[]{:S(2)}) collective-permute-start(bf16[72,3072]{1,0:T(8,128)(2,1)S(1)} %get-tuple-element.53), channel_id=1, source_target_pairs={{24,0},{0,8},{8,16},{16,24},{97,1},{1,33},{33,65},{65,97},{26,2},{... | collective-permute-start | bytes 1327112 | tf_op jit(solution)/shard_map/ppermute | solution.py:51
  69.7 13.2 %collective-permute-start.14 = (bf16[72,3072]{1,0:T(8,128)(2,1)S(1)}, bf16[72,3072]{1,0:T(8,128)(2,1)S(1)}, u32[]{:S(2)}, u32[]{:S(2)}) collective-permute-start(bf16[72,3072]{1,0:T(8,128)(2,1)S(1)} %get-tuple-element.54), channel_id=1, source_target_pairs={{16,0},{24,8},{0,16},{8,24},{65,1},{97,33},{1,65},{33,97},{18,2},{... | collective-permute-start | bytes 1327112 | tf_op jit(solution)/shard_map/ppermute | solution.py:51
  72.1 10.8 %collective-permute-start.15 = (bf16[72,3072]{1,0:T(8,128)(2,1)S(1)}, bf16[72,3072]{1,0:T(8,128)(2,1)S(1)}, u32[]{:S(2)}, u32[]{:S(2)}) collective-permute-start(bf16[72,3072]{1,0:T(8,128)(2,1)S(1)} %get-tuple-element.55), channel_id=1, source_target_pairs={{8,0},{16,8},{24,16},{0,24},{33,1},{65,33},{97,65},{1,97},{10,2},{... | collective-permute-start | bytes 1327112 | tf_op jit(solution)/shard_map/ppermute | solution.py:51
  77.0 10.6 %collective-permute-start.19 = (bf16[72,3072]{1,0:T(8,128)(2,1)S(1)}, bf16[72,3072]{1,0:T(8,128)(2,1)S(1)}, u32[]{:S(2)}, u32[]{:S(2)}) collective-permute-start(bf16[72,3072]{1,0:T(8,128)(2,1)S(1)} %get-tuple-element.57), channel_id=1, source_target_pairs={{24,0},{0,8},{8,16},{16,24},{97,1},{1,33},{33,65},{65,97},{26,2},{... | collective-permute-start | bytes 1327112 | tf_op jit(solution)/shard_map/ppermute | solution.py:51
  77.3 15.0 %collective-permute-start.20 = (bf16[72,3072]{1,0:T(8,128)(2,1)S(1)}, bf16[72,3072]{1,0:T(8,128)(2,1)S(1)}, u32[]{:S(2)}, u32[]{:S(2)}) collective-permute-start(bf16[72,3072]{1,0:T(8,128)(2,1)S(1)} %get-tuple-element.58), channel_id=1, source_target_pairs={{16,0},{24,8},{0,16},{8,24},{65,1},{97,33},{1,65},{33,97},{18,2},{... | collective-permute-start | bytes 1327112 | tf_op jit(solution)/shard_map/ppermute | solution.py:51
  78.2 14.1 %collective-permute-start.21 = (bf16[72,3072]{1,0:T(8,128)(2,1)S(1)}, bf16[72,3072]{1,0:T(8,128)(2,1)S(1)}, u32[]{:S(2)}, u32[]{:S(2)}) collective-permute-start(bf16[72,3072]{1,0:T(8,128)(2,1)S(1)} %get-tuple-element.59), channel_id=1, source_target_pairs={{8,0},{16,8},{24,16},{0,24},{33,1},{65,33},{97,65},{1,97},{10,2},{... | collective-permute-start | bytes 1327112 | tf_op jit(solution)/shard_map/ppermute | solution.py:51
  83.2 13.8 %collective-permute-start.18 = (bf16[72,3072]{1,0:T(8,128)(2,1)S(1)}, bf16[72,3072]{1,0:T(8,128)(2,1)S(1)}, u32[]{:S(2)}, u32[]{:S(2)}) collective-permute-start(bf16[72,3072]{1,0:T(8,128)(2,1)S(1)} %shard_map.114.refs_0_), channel_id=1, source_target_pairs={{24,0},{0,8},{8,16},{16,24},{97,1},{1,33},{33,65},{65,97},{26,2},{... | collective-permute-start | bytes 1327112 | tf_op jit(solution)/shard_map/ppermute | solution.py:51
  84.4 17.5 %collective-permute-start.17 = (bf16[72,3072]{1,0:T(8,128)(2,1)S(1)}, bf16[72,3072]{1,0:T(8,128)(2,1)S(1)}, u32[]{:S(2)}, u32[]{:S(2)}) collective-permute-start(bf16[72,3072]{1,0:T(8,128)(2,1)S(1)} %shard_map.114.refs_0_), channel_id=1, source_target_pairs={{16,0},{24,8},{0,16},{8,24},{65,1},{97,33},{1,65},{33,97},{18,2},{... | collective-permute-start | bytes 1327112 | tf_op jit(solution)/shard_map/ppermute | solution.py:51
  87.5 14.3 %collective-permute-start.16 = (bf16[72,3072]{1,0:T(8,128)(2,1)S(1)}, bf16[72,3072]{1,0:T(8,128)(2,1)S(1)}, u32[]{:S(2)}, u32[]{:S(2)}) collective-permute-start(bf16[72,3072]{1,0:T(8,128)(2,1)S(1)} %shard_map.114.refs_0_), channel_id=1, source_target_pairs={{8,0},{16,8},{24,16},{0,24},{33,1},{65,33},{97,65},{1,97},{10,2},{... | collective-permute-start | bytes 1327112 | tf_op jit(solution)/shard_map/ppermute | solution.py:51
  92.7 13.8 %collective-permute-start.24 = (bf16[72,3072]{1,0:T(8,128)(2,1)S(1)}, bf16[72,3072]{1,0:T(8,128)(2,1)S(1)}, u32[]{:S(2)}, u32[]{:S(2)}) collective-permute-start(bf16[72,3072]{1,0:T(8,128)(2,1)S(1)} %shard_map.115.refs_4_), channel_id=1, source_target_pairs={{24,0},{0,8},{8,16},{16,24},{97,1},{1,33},{33,65},{65,97},{26,2},{... | collective-permute-start | bytes 1327112 | tf_op jit(solution)/shard_map/ppermute | solution.py:51
  93.9 17.5 %collective-permute-start.23 = (bf16[72,3072]{1,0:T(8,128)(2,1)S(1)}, bf16[72,3072]{1,0:T(8,128)(2,1)S(1)}, u32[]{:S(2)}, u32[]{:S(2)}) collective-permute-start(bf16[72,3072]{1,0:T(8,128)(2,1)S(1)} %shard_map.115.refs_4_), channel_id=1, source_target_pairs={{16,0},{24,8},{0,16},{8,24},{65,1},{97,33},{1,65},{33,97},{18,2},{... | collective-permute-start | bytes 1327112 | tf_op jit(solution)/shard_map/ppermute | solution.py:51
  97.0 14.3 %collective-permute-start.22 = (bf16[72,3072]{1,0:T(8,128)(2,1)S(1)}, bf16[72,3072]{1,0:T(8,128)(2,1)S(1)}, u32[]{:S(2)}, u32[]{:S(2)}) collective-permute-start(bf16[72,3072]{1,0:T(8,128)(2,1)S(1)} %shard_map.115.refs_4_), channel_id=1, source_target_pairs={{8,0},{16,8},{24,16},{0,24},{33,1},{65,33},{97,65},{1,97},{10,2},{... | collective-permute-start | bytes 1327112 | tf_op jit(solution)/shard_map/ppermute | solution.py:51
  154.7 47.5 %collective-permute-start.25 = (bf16[4,288,1024]{2,1,0:T(8,128)(2,1)S(1)}, bf16[4,288,1024]{2,1,0:T(8,128)(2,1)S(1)}, u32[]{:S(2)}, u32[]{:S(2)}) collective-permute-start(bf16[4,288,1024]{2,1,0:T(8,128)(2,1)S(1)} %bitcast.15), channel_id=1, source_target_pairs={{0,1},{1,0},{2,3},{3,2},{4,5},{5,4},{6,7},{7,6},{8,9},{9,8},{10,11... | collective-permute-start | bytes 7077896 | tf_op jit(solution)/shard_map/ppermute | solution.py:59
  162.0 21.2 %collective-permute-start.27 = (bf16[768,1024]{1,0:T(8,128)(2,1)S(1)}, bf16[768,1024]{1,0:T(8,128)(2,1)S(1)}, u32[]{:S(2)}, u32[]{:S(2)}) collective-permute-start(bf16[768,1024]{1,0:T(8,128)(2,1)S(1)} %copy-done.10), channel_id=1, source_target_pairs={{64,0},{96,32},{0,64},{32,96},{17,1},{25,9},{1,17},{9,25},{66,2},{... | collective-permute-start | bytes 4718600 | tf_op jit(solution)/shard_map/ppermute | solution.py:51
  164.4 35.5 %collective-permute-start.26 = (bf16[768,1024]{1,0:T(8,128)(2,1)}, bf16[768,1024]{1,0:T(8,128)(2,1)S(1)}, u32[]{:S(2)}, u32[]{:S(2)}) collective-permute-start(bf16[768,1024]{1,0:T(8,128)(2,1)} %get-tuple-element.65), channel_id=1, source_target_pairs={{96,0},{0,32},{32,64},{64,96},{25,1},{1,9},{9,17},{17,25},{98,2},{... | collective-permute-start | bytes 4718600 | tf_op jit(solution)/shard_map/ppermute | solution.py:51
  165.1 35.0 %collective-permute-start.28 = (bf16[768,1024]{1,0:T(8,128)(2,1)}, bf16[768,1024]{1,0:T(8,128)(2,1)S(1)}, u32[]{:S(2)}, u32[]{:S(2)}) collective-permute-start(bf16[768,1024]{1,0:T(8,128)(2,1)} %get-tuple-element.67), channel_id=1, source_target_pairs={{32,0},{64,32},{96,64},{0,96},{9,1},{17,9},{25,17},{1,25},{34,2},{... | collective-permute-start | bytes 4718600 | tf_op jit(solution)/shard_map/ppermute | solution.py:51
  (9 other events, 45.6 us)

commit v5 on v4

--- a/solution.py
+++ b/solution.py
@@ -200,15 +200,16 @@
         out[:, cols[2]] = (dact * gate * sig).astype(BF)
 
 
-def turn_body(x_a, x_b, y_a, y_b, xt, yt, own_far, sems):
-    copies = Copies(sems)
-    for n, (a, b, out) in enumerate(((x_a, x_b, xt), (y_a, y_b, yt))):
-        for k in range(SIDE):
+def turn_body(x_a, x_b, y_a, y_b, two, turned_far, turned, sems):
+    copies = Copies(sems)
+    for k in (2, 1, 3, 0):
+        for n, (a, b) in enumerate(((x_a, x_b), (y_a, y_b))):
             cols = slice(k * BLK, (k + 1) * BLK)
             both = [v[m * SHARE : (m + 1) * SHARE, cols].astype(F32) for m in range(SIDE) for v in (a, b)]
-            both = jnp.concatenate(both, axis=0)
-            out[cols, :] = jnp.transpose(both).astype(BF)
-        copies.send(out.at[0:BLK, :], own_far.at[n])
+            out = two.at[n] if k == 2 else turned.at[k, n]
+            out[...] = jnp.transpose(jnp.concatenate(both, axis=0)).astype(BF)
+        if k != 2:
+            copies.send(turned.at[k], turned_far.at[k])
     copies.drain()
 
 
@@ -218,34 +219,32 @@
     out[2 * BLK :, :] = dot(y, acts[:, 0:FF]).astype(BF)
 
 
-def first_grads_body(xt, yt, *refs):
-    pieces, acts, out_far, out, sems = refs[: 2 * SIDE], *refs[2 * SIDE :]
+def first_grads_body(turned, *refs):
+    pieces, acts, acts_far, out_far, out, sems = refs[: 2 * SIDE], *refs[2 * SIDE :]
     copies = Copies(sems)
     for n, a in enumerate(pieces):
         at = 2 * (n % SIDE) + n // SIDE
         acts[at * SHARE : (at + 1) * SHARE, :] = a[...]
-    rows = slice(2 * BLK, 3 * BLK)
-    block_grads(out, xt[rows, :], yt[rows, :], acts)
+    copies.send(acts, acts_far)
+    block_grads(out, turned[0], turned[1], acts)
     copies.send(out, out_far)
     copies.drain()
 
 
-def more_grads_body(xt, yt, acts, acts_far, one_far, three_far, one, three, sems):
-    copies = Copies(sems)
-    copies.send(acts, acts_far)
-    for k, out, out_far in ((1, one, one_far), (3, three, three_far)):
-        rows = slice(k * BLK, (k + 1) * BLK)
-        block_grads(out, xt[rows, :], yt[rows, :], acts)
-        copies.send(out, out_far)
-    copies.drain()
-
-
-def own_grads_body(turned_far, acts_far, out, turned, acts, sems):
-    copies = Copies(sems)
-    loads = [copies.start(turned_far, turned), copies.start(acts_far, acts)]
-    for load in loads:
-        load.wait()
-    block_grads(out, turned[0], turned[1], acts)
+def more_grads_body(blocks, turned_far, acts_far, *refs):
+    n = len(blocks)
+    outs_far, turned, acts, *outs, sems = refs[:n], *refs[n:]
+    copies = Copies(sems)
+    load = copies.start(acts_far, acts)
+    loads = [copies.start(turned_far.at[k], turned.at[i]) for i, k in enumerate(blocks)]
+    load.wait()
+    for i in range(n):
+        loads[i].wait()
+        made = outs[0].at[i] if outs else outs_far[i]
+        block_grads(made, turned[i, 0], turned[i, 1], acts)
+        if outs:
+            copies.send(made, outs_far[i])
+    copies.drain()
 
 
 def return_body(pos, acts, *refs):
@@ -328,10 +327,10 @@
     u1, u3 = shifted(u0, COPIES, 1), shifted(u0, COPIES, -1)
     d1, d3 = shifted(d0, COPIES, 1), shifted(d0, COPIES, -1)
     half = FF // 2
-    g2 = near(shifted(g3, COPIES, -1))
-    u2 = near(shifted(u1, COPIES, 1))
-    low, high = near(shifted(d1[:half], COPIES, 1)), near(shifted(d3[half:], COPIES, -1))
-    weights = [(d0,), (d1,), low, high, (d3,), (g0,), (g1,), g2, (g3,), (u0,), (u1,), u2, (u3,)]
+    g2 = (shifted(g3, COPIES, -1))
+    u2 = (shifted(u1, COPIES, 1))
+    low, high = (shifted(d1[:half], COPIES, 1)), (shifted(d3[half:], COPIES, -1))
+    weights = [(d0,), (d1,), (low,), (high,), (d3,), (g0,), (g1,), (g2,), (g3,), (u0,), (u1,), (u2,), (u3,)]
     (sent,) = call(
         pack_body,
         [(SIDE, SENT, WIDE)],
@@ -358,22 +357,16 @@
     for p in (0, 1):
         (act,) = call(activate_body, [(SHARE, 3 * FF)], parts[p], smem=0)
         pieces += [act] + [near(shifted(act, FEATURE, k)) for k in (1, 2, -1)]
-    turned = (2, BLK, 2 * ROWS)
+    pair = (2, BLK, 2 * ROWS)
     block = (3 * BLK, FF)
     whole = (2 * ROWS, 3 * FF)
-    xt, yt, own_t = call(turn_body, [(WIDE, 2 * ROWS)] * 2 + [turned], [*xs, *ys], smem=0, hbm=(2,), copies=2)
-    acts, n2 = call(first_grads_body, [whole, block], [xt, yt, *pieces], smem=0, hbm=(1,), scratch=[block], copies=1)
+    two, turned = call(
+        turn_body, [pair, (SIDE, *pair)], [*xs, *ys], smem=0, hbm=(1,), scratch=[(SIDE, *pair)], copies=3
+    )
+    acts, acts_far, n2 = call(
+        first_grads_body, [whole, whole, block], [two, *pieces], smem=0, hbm=(1, 2), scratch=[block], copies=2
+    )
     n2 = near(shifted(n2, COPIES, -2))
-    acts_far, n1, n3 = call(
-        more_grads_body,
-        [whole, block, block],
-        [xt, yt, near(acts)],
-        smem=0,
-        hbm=(0, 1, 2),
-        scratch=[block] * 2,
-        copies=3,
-    )
-    n1, n3 = near(shifted(n1, COPIES, -1)), near(shifted(n3, COPIES, 1))
     (back,) = call(
         return_body,
         [(SIDE, SENT, WIDE)],
@@ -383,8 +376,20 @@
         copies=SIDE,
     )
     own = exchanged(back)
-    (n0,) = call(own_grads_body, [block], [(own_t,), (acts_far,)], smem=0, scratch=[turned, whole], copies=2)
-    ns = [n0, n1, n2, n3]
+    ns = {}
+    for blocks in ((1, 3), (0,)):
+        many = len(blocks)
+        done = call(
+            functools.partial(more_grads_body, blocks),
+            [block] * many,
+            [(turned,), (acts_far,)],
+            smem=0,
+            hbm=tuple(range(many)) if many > 1 else (),
+            scratch=[(many, *pair), whole] + [(many, *block)] * (many > 1),
+            copies=1 + 2 * many,
+        )
+        ns.update(zip(blocks, done))
+    n1, n3 = near(shifted(ns[1], COPIES, -1)), near(shifted(ns[3], COPIES, 1))
     oth = near(other_core(own))
     mixed, into = call(
         unpack_body,
@@ -395,7 +400,7 @@
         copies=2 * SIDE,
     )
     shapes = [(BLK, FF), (BLK, FF), (FF, BLK)]
-    gate, upper, down = call(total_body, shapes, ns, smem=0, hbm=(0, 1, 2), scratch=shapes, copies=3)
+    gate, upper, down = call(total_body, shapes, [ns[0], n1, n2, n3], smem=0, hbm=(0, 1, 2), scratch=shapes, copies=3)
     return mixed, into, gate[None], upper[None], down[None]
 
 

time: 207 us -> 210 us (1.014)
  Pallas kernels: 38.9 us -> 43.5 us
    pallas_call x12, Pallas kernels: 38.9 us -> 43.5 us  [call(): pl.pallas_call(body, out_shape=[(pltpu.HBM if n in hbm else pltpu.VMEM)(d...]
  transfers between devices with their start and end apart: 30 -> 30, of which waited for: 15 -> 16; matrix products, arithmetic and copies ran while one was open for 1% -> 1% of each run, Pallas kernels for 8% -> 9%
where the time goes in v5:
time: 210 us
  waiting for transfers between devices  78.7 us (37%)
  starting transfers between devices  50.7 us (24%)
  Pallas kernels  43.5 us (21%)
  blocking collectives  33.3 us (16%)
    ppermute x25, waiting for transfers between devices, shifted(): return lax.ppermute(value, AXES, pairs)  76.7 us
    pallas_call x12, Pallas kernels, call(): pl.pallas_call(body, out_shape=[(pltpu.HBM if n in hbm else pltpu.VMEM)(d...  43.5 us
    ppermute x25, starting transfers between devices, shifted(): return lax.ppermute(value, AXES, pairs)  37.6 us
    all_to_all x1, blocking collectives, grouped(): lax.all_to_all(value, AXES, 0, 0, axis_index_groups=rings, tiled=True)  33.3 us
    all_to_all x1, starting transfers between devices, grouped(): lax.all_to_all(value, AXES, 0, 0, axis_index_groups=rings, tiled=True)  7.89 us
    ppermute x4, starting transfers between devices, other_core(): return lax.ppermute(value, 'c', [(0, 1), (1, 0)])  5.19 us
  transfers between devices with their start and end apart: 30, of which 16 were waited for; matrix products, arithmetic and copies ran while one was open for 1% of the time, Pallas kernels for 9%

profile of v5, /device:TPU:1, one launch (start us, length us, event | category | flops | bytes accessed | tf_op | source)
XLA Modules:
  0.0 210.2 jit_solution(9800357792952459704)
XLA Ops:
  4.2 1.9 collective-permute-done.meta_b
  6.1 4.5 %shard_map.110 = bf16[4,288,1024]{2,1,0:T(8,128)(2,1)} custom-call(s32[3]{0:T(128)S(1)} %pad_add_fusion.pos, bf16[128,2]{1,0:T(8,128)(2,1)S(1)} %copy.16.meta_a, bf16[128,2]{1,0:T(8,128)(2,1)S(1)} %collective-permute-done.meta_b, bf16[128,4096]{1,0:T(8,128)(2,1)S(1)} %collective-permute-done.1.tok_b, bf16[128,4096]{1,0:T(8,128)(2,1)S(1)} %collective-permute-done.2.cot_b, ...), custom_call_target="tpu_custom_call" | custom-call | tf_op jit(solution)/shard_map/pallas_call | solution.py:87
  10.7 7.9 %all-to-all-start = ((bf16[16,72,1024]{2,1,0:T(8,128)(2,1)}), bf16[16,72,1024]{2,1,0:T(8,128)(2,1)S(1)}, u32[]{:S(2)}, u32[]{:S(2)}) async-start(bf16[16,72,1024]{2,1,0:T(8,128)(2,1)} %bitcast.17), calls=%async_computation | async-start | bytes 4718592 | tf_op jit(solution)/shard_map/all_to_all | solution.py:55
  21.3 2.7 %collective-permute-start.3 = (bf16[1024,256]{1,0:T(8,128)(2,1)}, bf16[1024,256]{1,0:T(8,128)(2,1)S(1)}, u32[]{:S(2)}, u32[]{:S(2)}) collective-permute-start(bf16[1024,256]{1,0:T(8,128)(2,1)} %bitcast.5.refs_0_), channel_id=1, source_target_pairs={{32,0},{64,32},{96,64},{0,96},{9,1},{17,9},{25,17},{1,25},{34,2},{... | collective-permute-start | bytes 1572872 | tf_op jit(solution)/shard_map/ppermute | solution.py:51
  24.1 12.1 %collective-permute-done.8.refs_8_ = bf16[256,1024]{1,0:T(8,128)(2,1)S(1)} collective-permute-done((bf16[256,1024]{1,0:T(8,128)(2,1)}, bf16[256,1024]{1,0:T(8,128)(2,1)S(1)}, u32[]{:S(2)}, u32[]{:S(2)}) %collective-permute-start.8) | collective-permute-done | bytes 524320 | tf_op jit(solution)/shard_map/ppermute | solution.py:51
  36.3 6.2 %collective-permute-start.9 = (bf16[256,1024]{1,0:T(8,128)(2,1)S(1)}, bf16[256,1024]{1,0:T(8,128)(2,1)S(1)}, u32[]{:S(2)}, u32[]{:S(2)}) collective-permute-start(bf16[256,1024]{1,0:T(8,128)(2,1)S(1)} %collective-permute-done.8.refs_8_), channel_id=1, source_target_pairs={{96,0},{0,32},{32,64},{64,96},{25,1},{1,9},{9,17},{17,25},{98,2},{... | collective-permute-start | bytes 1572872 | tf_op jit(solution)/shard_map/ppermute | solution.py:51
  42.5 1.9 collective-permute-done.5.refs_4_
  44.4 3.0 %collective-permute-start.11 = (bf16[256,1024]{1,0:T(8,128)(2,1)S(1)}, bf16[256,1024]{1,0:T(8,128)(2,1)}, u32[]{:S(2)}, u32[]{:S(2)}) collective-permute-start(bf16[256,1024]{1,0:T(8,128)(2,1)S(1)} %collective-permute-done.10.refs_10_), channel_id=1, source_target_pairs={{32,0},{64,32},{96,64},{0,96},{9,1},{17,9},{25,17},{1,25},{34,2},{... | collective-permute-start | bytes 1572872 | tf_op jit(solution)/shard_map/ppermute | solution.py:51
  49.2 3.4 %collective-permute-done.7.refs_6_ = bf16[256,1024]{1,0:T(8,128)(2,1)S(1)} collective-permute-done((bf16[256,1024]{1,0:T(8,128)(2,1)}, bf16[256,1024]{1,0:T(8,128)(2,1)S(1)}, u32[]{:S(2)}, u32[]{:S(2)}) %collective-permute-start.7) | collective-permute-done | bytes 524320 | tf_op jit(solution)/shard_map/ppermute | solution.py:51
  53.9 6.6 %collective-permute-done.6.refs_3_ = bf16[512,256]{1,0:T(8,128)(2,1)S(1)} collective-permute-done((bf16[512,256]{1,0:T(8,128)(2,1)S(1)}, bf16[512,256]{1,0:T(8,128)(2,1)S(1)}, u32[]{:S(2)}, u32[]{:S(2)}) %collective-permute-start.6) | collective-permute-done | bytes 262176 | tf_op jit(solution)/shard_map/ppermute | solution.py:51
  62.2 5.8 %shard_map.111 = (bf16[288,1024]{1,0:T(8,128)(2,1)S(1)}, bf16[288,1024]{1,0:T(8,128)(2,1)S(1)}, bf16[72,3072]{1,0:T(8,128)(2,1)S(1)}, bf16[72,3072]{1,0:T(8,128)...) custom-call(s32[3]{0:T(128)S(1)} %pad_add_fusion.pos, ...), custom_call_target="tpu_custom_call" | custom-call | tf_op jit(solution)/shard_map/pallas_call | solution.py:87
  69.2 2.4 %collective-permute-start.14 = (bf16[72,3072]{1,0:T(8,128)(2,1)S(1)}, bf16[72,3072]{1,0:T(8,128)(2,1)S(1)}, u32[]{:S(2)}, u32[]{:S(2)}) collective-permute-start(bf16[72,3072]{1,0:T(8,128)(2,1)S(1)} %get-tuple-element.52), channel_id=1, source_target_pairs={{16,0},{24,8},{0,16},{8,24},{65,1},{97,33},{1,65},{33,97},{18,2},{... | collective-permute-start | bytes 1327112 | tf_op jit(solution)/shard_map/ppermute | solution.py:51
  73.0 3.7 %shard_map.112 = (bf16[288,1024]{1,0:T(8,128)(2,1)S(1)}, bf16[288,1024]{1,0:T(8,128)(2,1)S(1)}, bf16[72,3072]{1,0:T(8,128)(2,1)S(1)}, bf16[72,3072]{1,0:T(8,128)...) custom-call(s32[3]{0:T(128)S(1)} %pad_add_fusion.pos, bf16[4,288,1024]{2,1,0:T(8,128)(2,1)S(1)} %bitcast.14, ...), custom_call_target="tpu_custom_call" | custom-call | tf_op jit(solution)/shard_map/pallas_call | solution.py:87
  79.5 2.9 %collective-permute-done.14.p2 = bf16[72,3072]{1,0:T(8,128)(2,1)S(1)} collective-permute-done((bf16[72,3072]{1,0:T(8,128)(2,1)S(1)}, bf16[72,3072]{1,0:T(8,128)(2,1)S(1)}, u32[]{:S(2)}, u32[]{:S(2)}) %collective-permute-start.14) | collective-permute-done | bytes 442400 | tf_op jit(solution)/shard_map/ppermute | solution.py:51
  83.9 2.1 %collective-permute-start.17 = (bf16[72,3072]{1,0:T(8,128)(2,1)S(1)}, bf16[72,3072]{1,0:T(8,128)(2,1)S(1)}, u32[]{:S(2)}, u32[]{:S(2)}) collective-permute-start(bf16[72,3072]{1,0:T(8,128)(2,1)S(1)} %shard_map.114.refs_0_), channel_id=1, source_target_pairs={{16,0},{24,8},{0,16},{8,24},{65,1},{97,33},{1,65},{33,97},{18,2},{... | collective-permute-start | bytes 1327112 | tf_op jit(solution)/shard_map/ppermute | solution.py:51
  87.4 4.4 %collective-permute-done.20.p2 = bf16[72,3072]{1,0:T(8,128)(2,1)S(1)} collective-permute-done((bf16[72,3072]{1,0:T(8,128)(2,1)S(1)}, bf16[72,3072]{1,0:T(8,128)(2,1)S(1)}, u32[]{:S(2)}, u32[]{:S(2)}) %collective-permute-start.20) | collective-permute-done | bytes 442400 | tf_op jit(solution)/shard_map/ppermute | solution.py:51
  92.3 1.7 collective-permute-start.24
  97.0 1.7 shard_map.113
  98.7 2.7 %collective-permute-done.17.refs_2_ = bf16[72,3072]{1,0:T(8,128)(2,1)S(1)} collective-permute-done((bf16[72,3072]{1,0:T(8,128)(2,1)S(1)}, bf16[72,3072]{1,0:T(8,128)(2,1)S(1)}, u32[]{:S(2)}, u32[]{:S(2)}) %collective-permute-start.17) | collective-permute-done | bytes 442400 | tf_op jit(solution)/shard_map/ppermute | solution.py:51
  101.4 4.6 %collective-permute-done.24.refs_7_ = bf16[72,3072]{1,0:T(8,128)(2,1)S(1)} collective-permute-done((bf16[72,3072]{1,0:T(8,128)(2,1)S(1)}, bf16[72,3072]{1,0:T(8,128)(2,1)S(1)}, u32[]{:S(2)}, u32[]{:S(2)}) %collective-permute-start.24) | collective-permute-done | bytes 442400 | tf_op jit(solution)/shard_map/ppermute | solution.py:51
  106.0 4.8 %collective-permute-done.23.refs_6_ = bf16[72,3072]{1,0:T(8,128)(2,1)S(1)} collective-permute-done((bf16[72,3072]{1,0:T(8,128)(2,1)S(1)}, bf16[72,3072]{1,0:T(8,128)(2,1)S(1)}, u32[]{:S(2)}, u32[]{:S(2)}) %collective-permute-start.23) | collective-permute-done | bytes 442400 | tf_op jit(solution)/shard_map/ppermute | solution.py:51
  110.9 3.4 %shard_map.116 = (bf16[576,3072]{1,0:T(8,128)(2,1)S(1)}, bf16[576,3072]{1,0:T(8,128)(2,1)}, bf16[768,1024]{1,0:T(8,128)(2,1)}) custom-call(bf16[2,256,576]{2,1,0:T(8,128)(2,1)S(1)} %get-tuple-element.49.turned, bf16[72,3072]{1,0:T(8,128)(2,1)S(1)} %shard_map.114.refs_0_, bf16[72,3072]{1,0:T(8,128)(2,1)S(1)} %collective-permute-done.16.refs_1_, ...), custom_call_target="tpu_custom_call" | custom-call | tf_op jit(solution)/shard_map/pallas_call | solution.py:87
  114.3 7.5 %shard_map.117 = bf16[4,288,1024]{2,1,0:T(8,128)(2,1)} custom-call(s32[3]{0:T(128)S(1)} %pad_add_fusion.pos, bf16[576,3072]{1,0:T(8,128)(2,1)S(1)} %get-tuple-element.58.acts, bf16[1024,256]{1,0:T(8,128)(2,1)S(1)} %get-tuple-element.38.refs_0_, bf16[1024,256]{1,0:T(8,128)(2,1)S(1)} %get-tuple-element.39.refs_1_, ...), custom_call_target="tpu_custom_call" | custom-call | tf_op jit(solution)/shard_map/pallas_call | solution.py:87
  121.8 33.3 %all_to_all.10 = bf16[16,72,1024]{2,1,0:T(8,128)(2,1)S(1)} all-to-all(bf16[16,72,1024]{2,1,0:T(8,128)(2,1)} %bitcast.18), channel_id=1, replica_groups={{0,2,4,6,8,10,12,14,16,18,20,22,24,26,28,30},{1,3,5,7,33,35,37,39,65,67..., dimensions={0} | all-to-all | bytes 4718592 | tf_op jit(solution)/shard_map/all_to_all | solution.py:55
  155.0 3.2 %collective-permute-start.25 = (bf16[4,288,1024]{2,1,0:T(8,128)(2,1)S(1)}, bf16[4,288,1024]{2,1,0:T(8,128)(2,1)S(1)}, u32[]{:S(2)}, u32[]{:S(2)}) collective-permute-start(bf16[4,288,1024]{2,1,0:T(8,128)(2,1)S(1)} %bitcast.15), channel_id=1, source_target_pairs={{0,1},{1,0},{2,3},{3,2},{4,5},{5,4},{6,7},{7,6},{8,9},{9,8},{10,11... | collective-permute-start | bytes 7077896 | tf_op jit(solution)/shard_map/ppermute | solution.py:59
  158.2 6.2 %shard_map.120 = (bf16[768,1024]{1,0:T(8,128)(2,1)}, bf16[768,1024]{1,0:T(8,128)(2,1)}) custom-call(bf16[4,2,256,576]{3,2,1,0:T(8,128)(2,1)} %get-tuple-element.61.turned_far, bf16[576,3072]{1,0:T(8,128)(2,1)} %get-tuple-element.62.acts_far), custom_call_target="tpu_custom_call" | custom-call | tf_op jit(solution)/shard_map/pallas_call | solution.py:87
  167.4 1.8 collective-permute-start.27
  169.2 3.6 %shard_map.119.n0 = bf16[768,1024]{1,0:T(8,128)(2,1)S(1)} custom-call(bf16[4,2,256,576]{3,2,1,0:T(8,128)(2,1)} %get-tuple-element.61.turned_far, bf16[576,3072]{1,0:T(8,128)(2,1)} %get-tuple-element.62.acts_far), custom_call_target="tpu_custom_call" | custom-call | tf_op jit(solution)/shard_map/pallas_call | solution.py:87
  172.8 12.9 %collective-permute-done.26.n1 = bf16[768,1024]{1,0:T(8,128)(2,1)S(1)} collective-permute-done((bf16[768,1024]{1,0:T(8,128)(2,1)}, bf16[768,1024]{1,0:T(8,128)(2,1)S(1)}, u32[]{:S(2)}, u32[]{:S(2)}) %collective-permute-start.26) | collective-permute-done | bytes 1572896 | tf_op jit(solution)/shard_map/ppermute | solution.py:51
  185.7 17.9 %collective-permute-done.27.n2 = bf16[768,1024]{1,0:T(8,128)(2,1)S(1)} collective-permute-done((bf16[768,1024]{1,0:T(8,128)(2,1)S(1)}, bf16[768,1024]{1,0:T(8,128)(2,1)S(1)}, u32[]{:S(2)}, u32[]{:S(2)}) %collective-permute-start.27) | collective-permute-done | bytes 1572896 | tf_op jit(solution)/shard_map/ppermute | solution.py:51
  203.7 2.1 shard_map.121
  205.8 4.2 %shard_map.118 = (bf16[128,4096]{1,0:T(8,128)(2,1)}, bf16[128,4096]{1,0:T(8,128)(2,1)}) custom-call(s32[3]{0:T(128)S(1)} %pad_add_fusion.pos, bf16[128,2]{1,0:T(8,128)(2,1)S(1)} %copy.16.meta_a, bf16[128,2]{1,0:T(8,128)(2,1)S(1)} %collective-permute-done.meta_b, bf16[4,288,1024]{2,1,0:T(8,128)(2,1)S(1)} %bitcast.16, ...), custom_call_target="tpu_custom_call" | custom-call | tf_op jit(solution)/shard_map/pallas_call | solution.py:87
  (67 shorter events, 25.9 us)
Async XLA Ops:
  0.6 5.5 %collective-permute-start.1 = (bf16[128,4096]{1,0:T(8,128)(2,1)}, bf16[128,4096]{1,0:T(8,128)(2,1)S(1)}, u32[]{:S(2)}, u32[]{:S(2)}) collective-permute-start(bf16[128,4096]{1,0:T(8,128)(2,1)} %tok_far.1), channel_id=1, source_target_pairs={{0,1},{1,0},{2,3},{3,2},{4,5},{5,4},{6,7},{7,6},{8,9},{9,8},{10,11... | collective-permute-start | bytes 3145736 | tf_op jit(solution)/shard_map/ppermute | solution.py:59
  2.1 4.0 %collective-permute-start.2 = (bf16[128,4096]{1,0:T(8,128)(2,1)}, bf16[128,4096]{1,0:T(8,128)(2,1)S(1)}, u32[]{:S(2)}, u32[]{:S(2)}) collective-permute-start(bf16[128,4096]{1,0:T(8,128)(2,1)} %cot_far.1), channel_id=1, source_target_pairs={{0,1},{1,0},{2,3},{3,2},{4,5},{5,4},{6,7},{7,6},{8,9},{9,8},{10,11... | collective-permute-start | bytes 3145736 | tf_op jit(solution)/shard_map/ppermute | solution.py:59
  3.6 2.5 %collective-permute-start = (bf16[128,2]{1,0:T(8,128)(2,1)S(1)}, bf16[128,2]{1,0:T(8,128)(2,1)S(1)}, u32[]{:S(2)}, u32[]{:S(2)}) collective-permute-start(bf16[128,2]{1,0:T(8,128)(2,1)S(1)} %copy.16.meta_a), channel_id=1, source_target_pairs={{0,1},{1,0},{2,3},{3,2},{4,5},{5,4},{6,7},{7,6},{8,9},{9,8},{10,11... | collective-permute-start | bytes 1544 | tf_op jit(solution)/shard_map/ppermute | solution.py:59
  10.7 51.5 %all-to-all-start = ((bf16[16,72,1024]{2,1,0:T(8,128)(2,1)}), bf16[16,72,1024]{2,1,0:T(8,128)(2,1)S(1)}, u32[]{:S(2)}, u32[]{:S(2)}) async-start(bf16[16,72,1024]{2,1,0:T(8,128)(2,1)} %bitcast.17), calls=%async_computation | async-start | bytes 4718592 | tf_op jit(solution)/shard_map/all_to_all | solution.py:55
  18.6 17.6 %collective-permute-start.8 = (bf16[256,1024]{1,0:T(8,128)(2,1)}, bf16[256,1024]{1,0:T(8,128)(2,1)S(1)}, u32[]{:S(2)}, u32[]{:S(2)}) collective-permute-start(bf16[256,1024]{1,0:T(8,128)(2,1)} %bitcast.6.refs_5_), channel_id=1, source_target_pairs={{96,0},{0,32},{32,64},{64,96},{25,1},{1,9},{9,17},{17,25},{98,2},{... | collective-permute-start | bytes 1572872 | tf_op jit(solution)/shard_map/ppermute | solution.py:51
  19.8 16.4 %collective-permute-start.10 = (bf16[256,1024]{1,0:T(8,128)(2,1)}, bf16[256,1024]{1,0:T(8,128)(2,1)S(1)}, u32[]{:S(2)}, u32[]{:S(2)}) collective-permute-start(bf16[256,1024]{1,0:T(8,128)(2,1)} %bitcast.7.refs_9_), channel_id=1, source_target_pairs={{32,0},{64,32},{96,64},{0,96},{9,1},{17,9},{25,17},{1,25},{34,2},{... | collective-permute-start | bytes 1572872 | tf_op jit(solution)/shard_map/ppermute | solution.py:51
  21.3 23.1 %collective-permute-start.5 = (bf16[1024,256]{1,0:T(8,128)(2,1)}, bf16[1024,256]{1,0:T(8,128)(2,1)S(1)}, u32[]{:S(2)}, u32[]{:S(2)}) collective-permute-start(bf16[1024,256]{1,0:T(8,128)(2,1)} %bitcast.5.refs_0_), channel_id=1, source_target_pairs={{96,0},{0,32},{32,64},{64,96},{25,1},{1,9},{9,17},{17,25},{98,2},{... | collective-permute-start | bytes 1572872 | tf_op jit(solution)/shard_map/ppermute | solution.py:51
  21.3 26.1 %collective-permute-start.3 = (bf16[1024,256]{1,0:T(8,128)(2,1)}, bf16[1024,256]{1,0:T(8,128)(2,1)S(1)}, u32[]{:S(2)}, u32[]{:S(2)}) collective-permute-start(bf16[1024,256]{1,0:T(8,128)(2,1)} %bitcast.5.refs_0_), channel_id=1, source_target_pairs={{32,0},{64,32},{96,64},{0,96},{9,1},{17,9},{25,17},{1,25},{34,2},{... | collective-permute-start | bytes 1572872 | tf_op jit(solution)/shard_map/ppermute | solution.py:51
  24.0 28.6 %collective-permute-start.7 = (bf16[256,1024]{1,0:T(8,128)(2,1)}, bf16[256,1024]{1,0:T(8,128)(2,1)S(1)}, u32[]{:S(2)}, u32[]{:S(2)}) collective-permute-start(bf16[256,1024]{1,0:T(8,128)(2,1)} %bitcast.6.refs_5_), channel_id=1, source_target_pairs={{32,0},{64,32},{96,64},{0,96},{9,1},{17,9},{25,17},{1,25},{34,2},{... | collective-permute-start | bytes 1572872 | tf_op jit(solution)/shard_map/ppermute | solution.py:51
  36.2 24.4 %copy-start.2 = (bf16[256,1024]{1,0:T(8,128)(2,1)}, bf16[256,1024]{1,0:T(8,128)(2,1)S(1)}, u32[]{:S(2)}) copy-start(bf16[256,1024]{1,0:T(8,128)(2,1)S(1)} %collective-permute-done.8.refs_8_) | copy-start | bytes 1572868
  36.2 17.7 %collective-permute-start.12 = (bf16[256,1024]{1,0:T(8,128)(2,1)}, bf16[256,1024]{1,0:T(8,128)(2,1)S(1)}, u32[]{:S(2)}, u32[]{:S(2)}) collective-permute-start(bf16[256,1024]{1,0:T(8,128)(2,1)} %bitcast.7.refs_9_), channel_id=1, source_target_pairs={{96,0},{0,32},{32,64},{64,96},{25,1},{1,9},{9,17},{17,25},{98,2},{... | collective-permute-start | bytes 1572872 | tf_op jit(solution)/shard_map/ppermute | solution.py:51
  36.3 24.3 %copy-start.3 = (bf16[256,1024]{1,0:T(8,128)(2,1)}, bf16[256,1024]{1,0:T(8,128)(2,1)S(1)}, u32[]{:S(2)}) copy-start(bf16[256,1024]{1,0:T(8,128)(2,1)S(1)} %collective-permute-done.10.refs_10_) | copy-start | bytes 1572868
  36.3 24.3 %collective-permute-start.9 = (bf16[256,1024]{1,0:T(8,128)(2,1)S(1)}, bf16[256,1024]{1,0:T(8,128)(2,1)S(1)}, u32[]{:S(2)}, u32[]{:S(2)}) collective-permute-start(bf16[256,1024]{1,0:T(8,128)(2,1)S(1)} %collective-permute-done.8.refs_8_), channel_id=1, source_target_pairs={{96,0},{0,32},{32,64},{64,96},{25,1},{1,9},{9,17},{17,25},{98,2},{... | collective-permute-start | bytes 1572872 | tf_op jit(solution)/shard_map/ppermute | solution.py:51
  44.4 17.7 %collective-permute-start.11 = (bf16[256,1024]{1,0:T(8,128)(2,1)S(1)}, bf16[256,1024]{1,0:T(8,128)(2,1)}, u32[]{:S(2)}, u32[]{:S(2)}) collective-permute-start(bf16[256,1024]{1,0:T(8,128)(2,1)S(1)} %collective-permute-done.10.refs_10_), channel_id=1, source_target_pairs={{32,0},{64,32},{96,64},{0,96},{9,1},{17,9},{25,17},{1,25},{34,2},{... | collective-permute-start | bytes 1572872 | tf_op jit(solution)/shard_map/ppermute | solution.py:51
  47.5 13.1 %collective-permute-start.6 = (bf16[512,256]{1,0:T(8,128)(2,1)S(1)}, bf16[512,256]{1,0:T(8,128)(2,1)S(1)}, u32[]{:S(2)}, u32[]{:S(2)}) collective-permute-start(bf16[512,256]{1,0:T(8,128)(2,1)S(1)} %slice.9), channel_id=1, source_target_pairs={{96,0},{0,32},{32,64},{64,96},{25,1},{1,9},{9,17},{17,25},{98,2},{... | collective-permute-start | bytes 786440 | tf_op jit(solution)/shard_map/ppermute | solution.py:51
  52.6 8.0 %collective-permute-start.4 = (bf16[512,256]{1,0:T(8,128)(2,1)S(1)}, bf16[512,256]{1,0:T(8,128)(2,1)S(1)}, u32[]{:S(2)}, u32[]{:S(2)}) collective-permute-start(bf16[512,256]{1,0:T(8,128)(2,1)S(1)} %slice.8), channel_id=1, source_target_pairs={{32,0},{64,32},{96,64},{0,96},{9,1},{17,9},{25,17},{1,25},{34,2},{... | collective-permute-start | bytes 786440 | tf_op jit(solution)/shard_map/ppermute | solution.py:51
  68.0 10.0 %collective-permute-start.13 = (bf16[72,3072]{1,0:T(8,128)(2,1)S(1)}, bf16[72,3072]{1,0:T(8,128)(2,1)S(1)}, u32[]{:S(2)}, u32[]{:S(2)}) collective-permute-start(bf16[72,3072]{1,0:T(8,128)(2,1)S(1)} %get-tuple-element.51), channel_id=1, source_target_pairs={{24,0},{0,8},{8,16},{16,24},{97,1},{1,33},{33,65},{65,97},{26,2},{... | collective-permute-start | bytes 1327112 | tf_op jit(solution)/shard_map/ppermute | solution.py:51
  69.2 13.1 %collective-permute-start.14 = (bf16[72,3072]{1,0:T(8,128)(2,1)S(1)}, bf16[72,3072]{1,0:T(8,128)(2,1)S(1)}, u32[]{:S(2)}, u32[]{:S(2)}) collective-permute-start(bf16[72,3072]{1,0:T(8,128)(2,1)S(1)} %get-tuple-element.52), channel_id=1, source_target_pairs={{16,0},{24,8},{0,16},{8,24},{65,1},{97,33},{1,65},{33,97},{18,2},{... | collective-permute-start | bytes 1327112 | tf_op jit(solution)/shard_map/ppermute | solution.py:51
  71.6 10.7 %collective-permute-start.15 = (bf16[72,3072]{1,0:T(8,128)(2,1)S(1)}, bf16[72,3072]{1,0:T(8,128)(2,1)S(1)}, u32[]{:S(2)}, u32[]{:S(2)}) collective-permute-start(bf16[72,3072]{1,0:T(8,128)(2,1)S(1)} %get-tuple-element.53), channel_id=1, source_target_pairs={{8,0},{16,8},{24,16},{0,24},{33,1},{65,33},{97,65},{1,97},{10,2},{... | collective-permute-start | bytes 1327112 | tf_op jit(solution)/shard_map/ppermute | solution.py:51
  76.7 10.4 %collective-permute-start.19 = (bf16[72,3072]{1,0:T(8,128)(2,1)S(1)}, bf16[72,3072]{1,0:T(8,128)(2,1)S(1)}, u32[]{:S(2)}, u32[]{:S(2)}) collective-permute-start(bf16[72,3072]{1,0:T(8,128)(2,1)S(1)} %get-tuple-element.55), channel_id=1, source_target_pairs={{24,0},{0,8},{8,16},{16,24},{97,1},{1,33},{33,65},{65,97},{26,2},{... | collective-permute-start | bytes 1327112 | tf_op jit(solution)/shard_map/ppermute | solution.py:51
  76.9 15.0 %collective-permute-start.20 = (bf16[72,3072]{1,0:T(8,128)(2,1)S(1)}, bf16[72,3072]{1,0:T(8,128)(2,1)S(1)}, u32[]{:S(2)}, u32[]{:S(2)}) collective-permute-start(bf16[72,3072]{1,0:T(8,128)(2,1)S(1)} %get-tuple-element.56), channel_id=1, source_target_pairs={{16,0},{24,8},{0,16},{8,24},{65,1},{97,33},{1,65},{33,97},{18,2},{... | collective-permute-start | bytes 1327112 | tf_op jit(solution)/shard_map/ppermute | solution.py:51
  77.9 13.9 %collective-permute-start.21 = (bf16[72,3072]{1,0:T(8,128)(2,1)S(1)}, bf16[72,3072]{1,0:T(8,128)(2,1)S(1)}, u32[]{:S(2)}, u32[]{:S(2)}) collective-permute-start(bf16[72,3072]{1,0:T(8,128)(2,1)S(1)} %get-tuple-element.57), channel_id=1, source_target_pairs={{8,0},{16,8},{24,16},{0,24},{33,1},{65,33},{97,65},{1,97},{10,2},{... | collective-permute-start | bytes 1327112 | tf_op jit(solution)/shard_map/ppermute | solution.py:51
  82.7 13.8 %collective-permute-start.18 = (bf16[72,3072]{1,0:T(8,128)(2,1)S(1)}, bf16[72,3072]{1,0:T(8,128)(2,1)S(1)}, u32[]{:S(2)}, u32[]{:S(2)}) collective-permute-start(bf16[72,3072]{1,0:T(8,128)(2,1)S(1)} %shard_map.114.refs_0_), channel_id=1, source_target_pairs={{24,0},{0,8},{8,16},{16,24},{97,1},{1,33},{33,65},{65,97},{26,2},{... | collective-permute-start | bytes 1327112 | tf_op jit(solution)/shard_map/ppermute | solution.py:51
  83.9 17.5 %collective-permute-start.17 = (bf16[72,3072]{1,0:T(8,128)(2,1)S(1)}, bf16[72,3072]{1,0:T(8,128)(2,1)S(1)}, u32[]{:S(2)}, u32[]{:S(2)}) collective-permute-start(bf16[72,3072]{1,0:T(8,128)(2,1)S(1)} %shard_map.114.refs_0_), channel_id=1, source_target_pairs={{16,0},{24,8},{0,16},{8,24},{65,1},{97,33},{1,65},{33,97},{18,2},{... | collective-permute-start | bytes 1327112 | tf_op jit(solution)/shard_map/ppermute | solution.py:51
  87.1 14.3 %collective-permute-start.16 = (bf16[72,3072]{1,0:T(8,128)(2,1)S(1)}, bf16[72,3072]{1,0:T(8,128)(2,1)S(1)}, u32[]{:S(2)}, u32[]{:S(2)}) collective-permute-start(bf16[72,3072]{1,0:T(8,128)(2,1)S(1)} %shard_map.114.refs_0_), channel_id=1, source_target_pairs={{8,0},{16,8},{24,16},{0,24},{33,1},{65,33},{97,65},{1,97},{10,2},{... | collective-permute-start | bytes 1327112 | tf_op jit(solution)/shard_map/ppermute | solution.py:51
  92.3 13.8 %collective-permute-start.24 = (bf16[72,3072]{1,0:T(8,128)(2,1)S(1)}, bf16[72,3072]{1,0:T(8,128)(2,1)S(1)}, u32[]{:S(2)}, u32[]{:S(2)}) collective-permute-start(bf16[72,3072]{1,0:T(8,128)(2,1)S(1)} %shard_map.115.refs_4_), channel_id=1, source_target_pairs={{24,0},{0,8},{8,16},{16,24},{97,1},{1,33},{33,65},{65,97},{26,2},{... | collective-permute-start | bytes 1327112 | tf_op jit(solution)/shard_map/ppermute | solution.py:51
  93.9 17.0 %collective-permute-start.23 = (bf16[72,3072]{1,0:T(8,128)(2,1)S(1)}, bf16[72,3072]{1,0:T(8,128)(2,1)S(1)}, u32[]{:S(2)}, u32[]{:S(2)}) collective-permute-start(bf16[72,3072]{1,0:T(8,128)(2,1)S(1)} %shard_map.115.refs_4_), channel_id=1, source_target_pairs={{16,0},{24,8},{0,16},{8,24},{65,1},{97,33},{1,65},{33,97},{18,2},{... | collective-permute-start | bytes 1327112 | tf_op jit(solution)/shard_map/ppermute | solution.py:51
  96.6 14.3 %collective-permute-start.22 = (bf16[72,3072]{1,0:T(8,128)(2,1)S(1)}, bf16[72,3072]{1,0:T(8,128)(2,1)S(1)}, u32[]{:S(2)}, u32[]{:S(2)}) collective-permute-start(bf16[72,3072]{1,0:T(8,128)(2,1)S(1)} %shard_map.115.refs_4_), channel_id=1, source_target_pairs={{8,0},{16,8},{24,16},{0,24},{33,1},{65,33},{97,65},{1,97},{10,2},{... | collective-permute-start | bytes 1327112 | tf_op jit(solution)/shard_map/ppermute | solution.py:51
  155.0 50.7 %collective-permute-start.25 = (bf16[4,288,1024]{2,1,0:T(8,128)(2,1)S(1)}, bf16[4,288,1024]{2,1,0:T(8,128)(2,1)S(1)}, u32[]{:S(2)}, u32[]{:S(2)}) collective-permute-start(bf16[4,288,1024]{2,1,0:T(8,128)(2,1)S(1)} %bitcast.15), channel_id=1, source_target_pairs={{0,1},{1,0},{2,3},{3,2},{4,5},{5,4},{6,7},{7,6},{8,9},{9,8},{10,11... | collective-permute-start | bytes 7077896 | tf_op jit(solution)/shard_map/ppermute | solution.py:59
  164.4 21.2 %collective-permute-start.26 = (bf16[768,1024]{1,0:T(8,128)(2,1)}, bf16[768,1024]{1,0:T(8,128)(2,1)S(1)}, u32[]{:S(2)}, u32[]{:S(2)}) collective-permute-start(bf16[768,1024]{1,0:T(8,128)(2,1)} %get-tuple-element.63), channel_id=1, source_target_pairs={{96,0},{0,32},{32,64},{64,96},{25,1},{1,9},{9,17},{17,25},{98,2},{... | collective-permute-start | bytes 4718600 | tf_op jit(solution)/shard_map/ppermute | solution.py:51
  165.9 19.9 %collective-permute-start.28 = (bf16[768,1024]{1,0:T(8,128)(2,1)}, bf16[768,1024]{1,0:T(8,128)(2,1)S(1)}, u32[]{:S(2)}, u32[]{:S(2)}) collective-permute-start(bf16[768,1024]{1,0:T(8,128)(2,1)} %get-tuple-element.65), channel_id=1, source_target_pairs={{32,0},{64,32},{96,64},{0,96},{9,1},{17,9},{25,17},{1,25},{34,2},{... | collective-permute-start | bytes 4718600 | tf_op jit(solution)/shard_map/ppermute | solution.py:51
  167.4 36.3 %collective-permute-start.27 = (bf16[768,1024]{1,0:T(8,128)(2,1)S(1)}, bf16[768,1024]{1,0:T(8,128)(2,1)S(1)}, u32[]{:S(2)}, u32[]{:S(2)}) collective-permute-start(bf16[768,1024]{1,0:T(8,128)(2,1)S(1)} %copy-done.9), channel_id=1, source_target_pairs={{64,0},{96,32},{0,64},{32,96},{17,1},{25,9},{1,17},{9,25},{66,2},{... | collective-permute-start | bytes 4718600 | tf_op jit(solution)/shard_map/ppermute | solution.py:51
  (8 other events, 58.7 us)

commit v6 on v5

--- a/solution.py
+++ b/solution.py
@@ -167,14 +167,17 @@
     else:
         kept, x, y, parts = refs[:8], refs[8], refs[9], refs[10:14]
     ds, ws = kept[:SIDE], kept[SIDE:]
-    q, r = iota((SHARE, SENT), 0), iota((SHARE, SENT), 1)
-    home = q + (q // PART) * (PAIR - PART) + first
-    for rows, take in ((x, (r == home).astype(BF)), (y, (r == home + SLOT).astype(BF))):
-        for k in range(SIDE):
-            rows[k * SHARE : (k + 1) * SHARE, :] = dot(take, got[(pos[2] + k) % SIDE]).astype(BF)
+    q, r = iota((2 * SHARE, SENT), 0), iota((2 * SHARE, SENT), 1)
+    kind, q = q // SHARE, q % SHARE
+    take = (r == q + (q // PART) * (PAIR - PART) + first + kind * SLOT).astype(BF)
+    for k in range(SIDE):
+        both = dot(take, got[(pos[2] + k) % SIDE]).astype(BF)
+        x[k * SHARE : (k + 1) * SHARE, :] = both[0:SHARE]
+        y[k * SHARE : (k + 1) * SHARE, :] = both[SHARE:]
     for t in (2, 0, 1):
-        if loads and t != 1:
-            for copy in going[:first_up] if t == 2 else going[first_up:]:
+        if loads:
+            ends = (first_up, first_up + SIDE, first_up + 2 * SIDE)
+            for copy in going[0:first_up] if t == 2 else going[ends[t] : ends[t + 1]]:
                 copy.wait()
         for n in range(FF // BLK):
             cols = slice(n * BLK, (n + 1) * BLK)
@@ -273,10 +276,10 @@
 
     def picks(route, core, mine):
         target = jnp.where(route % 2 == core, (route // 2) * PAIR + slots(route), -PAIR)[mine]
-        return (rows == target).astype(BF), (rows == target + SLOT).astype(BF)
-
-    own_m, own_s = picks(routes_of(meta_a, meta_b), kind, slice(0, TOK))
-    oth_m, oth_s = picks(routes_of(meta_b, meta_a), 1 - kind, slice(TOK, 2 * TOK))
+        return jnp.concatenate([(rows == target).astype(BF), (rows == target + SLOT).astype(BF)], axis=0)
+
+    own_both = picks(routes_of(meta_a, meta_b), kind, slice(0, TOK))
+    oth_both = picks(routes_of(meta_b, meta_a), 1 - kind, slice(TOK, 2 * TOK))
     weight = meta_a[:, 1:2].astype(F32)
     for b in range(SIDE * SIDE):
         major, minor = b // SIDE, b % SIDE
@@ -287,8 +290,9 @@
         o = own[own_d, :, pl.ds(pl.multiple_of(own_k * BLK, BLK), BLK)]
         t = oth[oth_d, :, pl.ds(pl.multiple_of(oth_k * BLK, BLK), BLK)]
         cols = slice(b * BLK, (b + 1) * BLK)
-        mixed[:, cols] = ((dot(own_m, o) + dot(oth_m, t)) * weight).astype(BF)
-        grad[:, cols] = (dot(own_s, o) + dot(oth_s, t)).astype(BF)
+        both = dot(own_both, o) + dot(oth_both, t)
+        mixed[:, cols] = (both[0:TOK] * weight).astype(BF)
+        grad[:, cols] = both[TOK:].astype(BF)
         if minor == SIDE - 1:
             done = pl.ds(major * WIDE, WIDE)
             copies.send(mixed.at[:, done], mixed_far.at[:, done])

time: 210 us -> 210 us (level)
  transfers between devices with their start and end apart: 30 -> 30, of which waited for: 16 -> 16; matrix products, arithmetic and copies ran while one was open for 1% -> 1% of each run, Pallas kernels for 9% -> 8%
where the time goes in v6:
time: 210 us; the launch traced here: 209 us
  waiting for transfers between devices  79.1 us (38%)
  starting transfers between devices  50.6 us (24%)
  Pallas kernels  42.2 us (20%)
  blocking collectives  33.2 us (16%)
    ppermute x25, waiting for transfers between devices, shifted(): return lax.ppermute(value, AXES, pairs)  77.2 us
    pallas_call x12, Pallas kernels, call(): pl.pallas_call(body, out_shape=[(pltpu.HBM if n in hbm else pltpu.VMEM)(d...  42.2 us
    ppermute x25, starting transfers between devices, shifted(): return lax.ppermute(value, AXES, pairs)  37.5 us
    all_to_all x1, blocking collectives, grouped(): lax.all_to_all(value, AXES, 0, 0, axis_index_groups=rings, tiled=True)  33.2 us
    all_to_all x1, starting transfers between devices, grouped(): lax.all_to_all(value, AXES, 0, 0, axis_index_groups=rings, tiled=True)  7.89 us
    ppermute x4, starting transfers between devices, other_core(): return lax.ppermute(value, 'c', [(0, 1), (1, 0)])  5.18 us
  transfers between devices with their start and end apart: 30, of which 16 were waited for; matrix products, arithmetic and copies ran while one was open for 1% of the time, Pallas kernels for 8%

profile of v6, /device:TPU:1, one launch (start us, length us, event | category | flops | bytes accessed | tf_op | source)
XLA Modules:
  0.0 209.3 jit_solution(16218042649211064402)
XLA Ops:
  4.2 1.9 collective-permute-done.meta_b
  6.1 4.5 %shard_map.110 = bf16[4,288,1024]{2,1,0:T(8,128)(2,1)} custom-call(s32[3]{0:T(128)S(1)} %pad_add_fusion.pos, bf16[128,2]{1,0:T(8,128)(2,1)S(1)} %copy.16.meta_a, bf16[128,2]{1,0:T(8,128)(2,1)S(1)} %collective-permute-done.meta_b, bf16[128,4096]{1,0:T(8,128)(2,1)S(1)} %collective-permute-done.1.tok_b, bf16[128,4096]{1,0:T(8,128)(2,1)S(1)} %collective-permute-done.2.cot_b, ...), custom_call_target="tpu_custom_call" | custom-call | tf_op jit(solution)/shard_map/pallas_call | solution.py:87
  10.7 7.9 %all-to-all-start = ((bf16[16,72,1024]{2,1,0:T(8,128)(2,1)}), bf16[16,72,1024]{2,1,0:T(8,128)(2,1)S(1)}, u32[]{:S(2)}, u32[]{:S(2)}) async-start(bf16[16,72,1024]{2,1,0:T(8,128)(2,1)} %bitcast.17), calls=%async_computation | async-start | bytes 4718592 | tf_op jit(solution)/shard_map/all_to_all | solution.py:55
  21.3 2.7 %collective-permute-start.3 = (bf16[1024,256]{1,0:T(8,128)(2,1)}, bf16[1024,256]{1,0:T(8,128)(2,1)S(1)}, u32[]{:S(2)}, u32[]{:S(2)}) collective-permute-start(bf16[1024,256]{1,0:T(8,128)(2,1)} %bitcast.5.refs_0_), channel_id=1, source_target_pairs={{32,0},{64,32},{96,64},{0,96},{9,1},{17,9},{25,17},{1,25},{34,2},{... | collective-permute-start | bytes 1572872 | tf_op jit(solution)/shard_map/ppermute | solution.py:51
  24.1 12.1 %collective-permute-done.8.refs_8_ = bf16[256,1024]{1,0:T(8,128)(2,1)S(1)} collective-permute-done((bf16[256,1024]{1,0:T(8,128)(2,1)}, bf16[256,1024]{1,0:T(8,128)(2,1)S(1)}, u32[]{:S(2)}, u32[]{:S(2)}) %collective-permute-start.8) | collective-permute-done | bytes 524320 | tf_op jit(solution)/shard_map/ppermute | solution.py:51
  36.3 6.2 %collective-permute-start.9 = (bf16[256,1024]{1,0:T(8,128)(2,1)S(1)}, bf16[256,1024]{1,0:T(8,128)(2,1)S(1)}, u32[]{:S(2)}, u32[]{:S(2)}) collective-permute-start(bf16[256,1024]{1,0:T(8,128)(2,1)S(1)} %collective-permute-done.8.refs_8_), channel_id=1, source_target_pairs={{96,0},{0,32},{32,64},{64,96},{25,1},{1,9},{9,17},{17,25},{98,2},{... | collective-permute-start | bytes 1572872 | tf_op jit(solution)/shard_map/ppermute | solution.py:51
  42.5 1.9 collective-permute-done.5.refs_4_
  44.4 3.0 %collective-permute-start.11 = (bf16[256,1024]{1,0:T(8,128)(2,1)S(1)}, bf16[256,1024]{1,0:T(8,128)(2,1)}, u32[]{:S(2)}, u32[]{:S(2)}) collective-permute-start(bf16[256,1024]{1,0:T(8,128)(2,1)S(1)} %collective-permute-done.10.refs_10_), channel_id=1, source_target_pairs={{32,0},{64,32},{96,64},{0,96},{9,1},{17,9},{25,17},{1,25},{34,2},{... | collective-permute-start | bytes 1572872 | tf_op jit(solution)/shard_map/ppermute | solution.py:51
  47.5 1.7 collective-permute-start.6
  49.2 3.4 %collective-permute-done.7.refs_6_ = bf16[256,1024]{1,0:T(8,128)(2,1)S(1)} collective-permute-done((bf16[256,1024]{1,0:T(8,128)(2,1)}, bf16[256,1024]{1,0:T(8,128)(2,1)S(1)}, u32[]{:S(2)}, u32[]{:S(2)}) %collective-permute-start.7) | collective-permute-done | bytes 524320 | tf_op jit(solution)/shard_map/ppermute | solution.py:51
  53.9 6.6 %collective-permute-done.6.refs_3_ = bf16[512,256]{1,0:T(8,128)(2,1)S(1)} collective-permute-done((bf16[512,256]{1,0:T(8,128)(2,1)S(1)}, bf16[512,256]{1,0:T(8,128)(2,1)S(1)}, u32[]{:S(2)}, u32[]{:S(2)}) %collective-permute-start.6) | collective-permute-done | bytes 262176 | tf_op jit(solution)/shard_map/ppermute | solution.py:51
  62.2 5.0 %shard_map.111 = (bf16[288,1024]{1,0:T(8,128)(2,1)S(1)}, bf16[288,1024]{1,0:T(8,128)(2,1)S(1)}, bf16[72,3072]{1,0:T(8,128)(2,1)S(1)}, bf16[72,3072]{1,0:T(8,128)...) custom-call(s32[3]{0:T(128)S(1)} %pad_add_fusion.pos, ...), custom_call_target="tpu_custom_call" | custom-call | tf_op jit(solution)/shard_map/pallas_call | solution.py:87
  68.4 2.4 %collective-permute-start.14 = (bf16[72,3072]{1,0:T(8,128)(2,1)S(1)}, bf16[72,3072]{1,0:T(8,128)(2,1)S(1)}, u32[]{:S(2)}, u32[]{:S(2)}) collective-permute-start(bf16[72,3072]{1,0:T(8,128)(2,1)S(1)} %get-tuple-element.52), channel_id=1, source_target_pairs={{16,0},{24,8},{0,16},{8,24},{65,1},{97,33},{1,65},{33,97},{18,2},{... | collective-permute-start | bytes 1327112 | tf_op jit(solution)/shard_map/ppermute | solution.py:51
  72.2 3.4 %shard_map.112 = (bf16[288,1024]{1,0:T(8,128)(2,1)S(1)}, bf16[288,1024]{1,0:T(8,128)(2,1)S(1)}, bf16[72,3072]{1,0:T(8,128)(2,1)S(1)}, bf16[72,3072]{1,0:T(8,128)...) custom-call(s32[3]{0:T(128)S(1)} %pad_add_fusion.pos, bf16[4,288,1024]{2,1,0:T(8,128)(2,1)S(1)} %bitcast.14, ...), custom_call_target="tpu_custom_call" | custom-call | tf_op jit(solution)/shard_map/pallas_call | solution.py:87
  78.3 3.3 %collective-permute-done.14.p2 = bf16[72,3072]{1,0:T(8,128)(2,1)S(1)} collective-permute-done((bf16[72,3072]{1,0:T(8,128)(2,1)S(1)}, bf16[72,3072]{1,0:T(8,128)(2,1)S(1)}, u32[]{:S(2)}, u32[]{:S(2)}) %collective-permute-start.14) | collective-permute-done | bytes 442400 | tf_op jit(solution)/shard_map/ppermute | solution.py:51
  83.1 2.1 %collective-permute-start.17 = (bf16[72,3072]{1,0:T(8,128)(2,1)S(1)}, bf16[72,3072]{1,0:T(8,128)(2,1)S(1)}, u32[]{:S(2)}, u32[]{:S(2)}) collective-permute-start(bf16[72,3072]{1,0:T(8,128)(2,1)S(1)} %shard_map.114.refs_0_), channel_id=1, source_target_pairs={{16,0},{24,8},{0,16},{8,24},{65,1},{97,33},{1,65},{33,97},{18,2},{... | collective-permute-start | bytes 1327112 | tf_op jit(solution)/shard_map/ppermute | solution.py:51
  86.6 4.5 %collective-permute-done.20.p2 = bf16[72,3072]{1,0:T(8,128)(2,1)S(1)} collective-permute-done((bf16[72,3072]{1,0:T(8,128)(2,1)S(1)}, bf16[72,3072]{1,0:T(8,128)(2,1)S(1)}, u32[]{:S(2)}, u32[]{:S(2)}) %collective-permute-start.20) | collective-permute-done | bytes 442400 | tf_op jit(solution)/shard_map/ppermute | solution.py:51
  96.2 1.7 shard_map.113
  97.9 2.8 %collective-permute-done.17.refs_2_ = bf16[72,3072]{1,0:T(8,128)(2,1)S(1)} collective-permute-done((bf16[72,3072]{1,0:T(8,128)(2,1)S(1)}, bf16[72,3072]{1,0:T(8,128)(2,1)S(1)}, u32[]{:S(2)}, u32[]{:S(2)}) %collective-permute-start.17) | collective-permute-done | bytes 442400 | tf_op jit(solution)/shard_map/ppermute | solution.py:51
  100.7 4.6 %collective-permute-done.24.refs_7_ = bf16[72,3072]{1,0:T(8,128)(2,1)S(1)} collective-permute-done((bf16[72,3072]{1,0:T(8,128)(2,1)S(1)}, bf16[72,3072]{1,0:T(8,128)(2,1)S(1)}, u32[]{:S(2)}, u32[]{:S(2)}) %collective-permute-start.24) | collective-permute-done | bytes 442400 | tf_op jit(solution)/shard_map/ppermute | solution.py:51
  105.3 4.9 %collective-permute-done.23.refs_6_ = bf16[72,3072]{1,0:T(8,128)(2,1)S(1)} collective-permute-done((bf16[72,3072]{1,0:T(8,128)(2,1)S(1)}, bf16[72,3072]{1,0:T(8,128)(2,1)S(1)}, u32[]{:S(2)}, u32[]{:S(2)}) %collective-permute-start.23) | collective-permute-done | bytes 442400 | tf_op jit(solution)/shard_map/ppermute | solution.py:51
  110.1 3.4 %shard_map.116 = (bf16[576,3072]{1,0:T(8,128)(2,1)S(1)}, bf16[576,3072]{1,0:T(8,128)(2,1)}, bf16[768,1024]{1,0:T(8,128)(2,1)}) custom-call(bf16[2,256,576]{2,1,0:T(8,128)(2,1)S(1)} %get-tuple-element.49.turned, bf16[72,3072]{1,0:T(8,128)(2,1)S(1)} %shard_map.114.refs_0_, bf16[72,3072]{1,0:T(8,128)(2,1)S(1)} %collective-permute-done.16.refs_1_, ...), custom_call_target="tpu_custom_call" | custom-call | tf_op jit(solution)/shard_map/pallas_call | solution.py:87
  113.5 7.5 %shard_map.117 = bf16[4,288,1024]{2,1,0:T(8,128)(2,1)} custom-call(s32[3]{0:T(128)S(1)} %pad_add_fusion.pos, bf16[576,3072]{1,0:T(8,128)(2,1)S(1)} %get-tuple-element.58.acts, bf16[1024,256]{1,0:T(8,128)(2,1)S(1)} %get-tuple-element.38.refs_0_, bf16[1024,256]{1,0:T(8,128)(2,1)S(1)} %get-tuple-element.39.refs_1_, ...), custom_call_target="tpu_custom_call" | custom-call | tf_op jit(solution)/shard_map/pallas_call | solution.py:87
  121.0 33.2 %all_to_all.10 = bf16[16,72,1024]{2,1,0:T(8,128)(2,1)S(1)} all-to-all(bf16[16,72,1024]{2,1,0:T(8,128)(2,1)} %bitcast.18), channel_id=1, replica_groups={{0,2,4,6,8,10,12,14,16,18,20,22,24,26,28,30},{1,3,5,7,33,35,37,39,65,67..., dimensions={0} | all-to-all | bytes 4718592 | tf_op jit(solution)/shard_map/all_to_all | solution.py:55
  154.3 3.1 %collective-permute-start.25 = (bf16[4,288,1024]{2,1,0:T(8,128)(2,1)S(1)}, bf16[4,288,1024]{2,1,0:T(8,128)(2,1)S(1)}, u32[]{:S(2)}, u32[]{:S(2)}) collective-permute-start(bf16[4,288,1024]{2,1,0:T(8,128)(2,1)S(1)} %bitcast.15), channel_id=1, source_target_pairs={{0,1},{1,0},{2,3},{3,2},{4,5},{5,4},{6,7},{7,6},{8,9},{9,8},{10,11... | collective-permute-start | bytes 7077896 | tf_op jit(solution)/shard_map/ppermute | solution.py:59
  157.4 6.2 %shard_map.120 = (bf16[768,1024]{1,0:T(8,128)(2,1)}, bf16[768,1024]{1,0:T(8,128)(2,1)}) custom-call(bf16[4,2,256,576]{3,2,1,0:T(8,128)(2,1)} %get-tuple-element.61.turned_far, bf16[576,3072]{1,0:T(8,128)(2,1)} %get-tuple-element.62.acts_far), custom_call_target="tpu_custom_call" | custom-call | tf_op jit(solution)/shard_map/pallas_call | solution.py:87
  166.6 1.8 collective-permute-start.27
  168.4 3.6 %shard_map.119.n0 = bf16[768,1024]{1,0:T(8,128)(2,1)S(1)} custom-call(bf16[4,2,256,576]{3,2,1,0:T(8,128)(2,1)} %get-tuple-element.61.turned_far, bf16[576,3072]{1,0:T(8,128)(2,1)} %get-tuple-element.62.acts_far), custom_call_target="tpu_custom_call" | custom-call | tf_op jit(solution)/shard_map/pallas_call | solution.py:87
  172.0 12.8 %collective-permute-done.26.n1 = bf16[768,1024]{1,0:T(8,128)(2,1)S(1)} collective-permute-done((bf16[768,1024]{1,0:T(8,128)(2,1)}, bf16[768,1024]{1,0:T(8,128)(2,1)S(1)}, u32[]{:S(2)}, u32[]{:S(2)}) %collective-permute-start.26) | collective-permute-done | bytes 1572896 | tf_op jit(solution)/shard_map/ppermute | solution.py:51
  184.9 17.9 %collective-permute-done.27.n2 = bf16[768,1024]{1,0:T(8,128)(2,1)S(1)} collective-permute-done((bf16[768,1024]{1,0:T(8,128)(2,1)S(1)}, bf16[768,1024]{1,0:T(8,128)(2,1)S(1)}, u32[]{:S(2)}, u32[]{:S(2)}) %collective-permute-start.27) | collective-permute-done | bytes 1572896 | tf_op jit(solution)/shard_map/ppermute | solution.py:51
  202.9 2.1 %shard_map.121 = (bf16[256,1024]{1,0:T(8,128)(2,1)}, bf16[256,1024]{1,0:T(8,128)(2,1)}, bf16[1024,256]{1,0:T(8,128)(2,1)}) custom-call(bf16[768,1024]{1,0:T(8,128)(2,1)S(1)} %shard_map.119.n0, bf16[768,1024]{1,0:T(8,128)(2,1)S(1)} %collective-permute-done.26.n1, bf16[768,1024]{1,0:T(8,128)(2,1)S(1)} %collective-permute-done.27.n2, ...), custom_call_target="tpu_custom_call" | custom-call | tf_op jit(solution)/shard_map/pallas_call | solution.py:87
  205.0 4.1 %shard_map.118 = (bf16[128,4096]{1,0:T(8,128)(2,1)}, bf16[128,4096]{1,0:T(8,128)(2,1)}) custom-call(s32[3]{0:T(128)S(1)} %pad_add_fusion.pos, bf16[128,2]{1,0:T(8,128)(2,1)S(1)} %copy.16.meta_a, bf16[128,2]{1,0:T(8,128)(2,1)S(1)} %collective-permute-done.meta_b, bf16[4,288,1024]{2,1,0:T(8,128)(2,1)S(1)} %bitcast.16, ...), custom_call_target="tpu_custom_call" | custom-call | tf_op jit(solution)/shard_map/pallas_call | solution.py:87
  (67 shorter events, 25.8 us)
Async XLA Ops:
  0.6 5.5 %collective-permute-start.1 = (bf16[128,4096]{1,0:T(8,128)(2,1)}, bf16[128,4096]{1,0:T(8,128)(2,1)S(1)}, u32[]{:S(2)}, u32[]{:S(2)}) collective-permute-start(bf16[128,4096]{1,0:T(8,128)(2,1)} %tok_far.1), channel_id=1, source_target_pairs={{0,1},{1,0},{2,3},{3,2},{4,5},{5,4},{6,7},{7,6},{8,9},{9,8},{10,11... | collective-permute-start | bytes 3145736 | tf_op jit(solution)/shard_map/ppermute | solution.py:59
  2.1 4.0 %collective-permute-start.2 = (bf16[128,4096]{1,0:T(8,128)(2,1)}, bf16[128,4096]{1,0:T(8,128)(2,1)S(1)}, u32[]{:S(2)}, u32[]{:S(2)}) collective-permute-start(bf16[128,4096]{1,0:T(8,128)(2,1)} %cot_far.1), channel_id=1, source_target_pairs={{0,1},{1,0},{2,3},{3,2},{4,5},{5,4},{6,7},{7,6},{8,9},{9,8},{10,11... | collective-permute-start | bytes 3145736 | tf_op jit(solution)/shard_map/ppermute | solution.py:59
  3.6 2.5 %collective-permute-start = (bf16[128,2]{1,0:T(8,128)(2,1)S(1)}, bf16[128,2]{1,0:T(8,128)(2,1)S(1)}, u32[]{:S(2)}, u32[]{:S(2)}) collective-permute-start(bf16[128,2]{1,0:T(8,128)(2,1)S(1)} %copy.16.meta_a), channel_id=1, source_target_pairs={{0,1},{1,0},{2,3},{3,2},{4,5},{5,4},{6,7},{7,6},{8,9},{9,8},{10,11... | collective-permute-start | bytes 1544 | tf_op jit(solution)/shard_map/ppermute | solution.py:59
  10.7 51.5 %all-to-all-start = ((bf16[16,72,1024]{2,1,0:T(8,128)(2,1)}), bf16[16,72,1024]{2,1,0:T(8,128)(2,1)S(1)}, u32[]{:S(2)}, u32[]{:S(2)}) async-start(bf16[16,72,1024]{2,1,0:T(8,128)(2,1)} %bitcast.17), calls=%async_computation | async-start | bytes 4718592 | tf_op jit(solution)/shard_map/all_to_all | solution.py:55
  18.6 17.6 %collective-permute-start.8 = (bf16[256,1024]{1,0:T(8,128)(2,1)}, bf16[256,1024]{1,0:T(8,128)(2,1)S(1)}, u32[]{:S(2)}, u32[]{:S(2)}) collective-permute-start(bf16[256,1024]{1,0:T(8,128)(2,1)} %bitcast.6.refs_5_), channel_id=1, source_target_pairs={{96,0},{0,32},{32,64},{64,96},{25,1},{1,9},{9,17},{17,25},{98,2},{... | collective-permute-start | bytes 1572872 | tf_op jit(solution)/shard_map/ppermute | solution.py:51
  19.8 16.4 %collective-permute-start.10 = (bf16[256,1024]{1,0:T(8,128)(2,1)}, bf16[256,1024]{1,0:T(8,128)(2,1)S(1)}, u32[]{:S(2)}, u32[]{:S(2)}) collective-permute-start(bf16[256,1024]{1,0:T(8,128)(2,1)} %bitcast.7.refs_9_), channel_id=1, source_target_pairs={{32,0},{64,32},{96,64},{0,96},{9,1},{17,9},{25,17},{1,25},{34,2},{... | collective-permute-start | bytes 1572872 | tf_op jit(solution)/shard_map/ppermute | solution.py:51
  21.3 23.1 %collective-permute-start.5 = (bf16[1024,256]{1,0:T(8,128)(2,1)}, bf16[1024,256]{1,0:T(8,128)(2,1)S(1)}, u32[]{:S(2)}, u32[]{:S(2)}) collective-permute-start(bf16[1024,256]{1,0:T(8,128)(2,1)} %bitcast.5.refs_0_), channel_id=1, source_target_pairs={{96,0},{0,32},{32,64},{64,96},{25,1},{1,9},{9,17},{17,25},{98,2},{... | collective-permute-start | bytes 1572872 | tf_op jit(solution)/shard_map/ppermute | solution.py:51
  21.3 26.1 %collective-permute-start.3 = (bf16[1024,256]{1,0:T(8,128)(2,1)}, bf16[1024,256]{1,0:T(8,128)(2,1)S(1)}, u32[]{:S(2)}, u32[]{:S(2)}) collective-permute-start(bf16[1024,256]{1,0:T(8,128)(2,1)} %bitcast.5.refs_0_), channel_id=1, source_target_pairs={{32,0},{64,32},{96,64},{0,96},{9,1},{17,9},{25,17},{1,25},{34,2},{... | collective-permute-start | bytes 1572872 | tf_op jit(solution)/shard_map/ppermute | solution.py:51
  24.0 28.6 %collective-permute-start.7 = (bf16[256,1024]{1,0:T(8,128)(2,1)}, bf16[256,1024]{1,0:T(8,128)(2,1)S(1)}, u32[]{:S(2)}, u32[]{:S(2)}) collective-permute-start(bf16[256,1024]{1,0:T(8,128)(2,1)} %bitcast.6.refs_5_), channel_id=1, source_target_pairs={{32,0},{64,32},{96,64},{0,96},{9,1},{17,9},{25,17},{1,25},{34,2},{... | collective-permute-start | bytes 1572872 | tf_op jit(solution)/shard_map/ppermute | solution.py:51
  36.2 24.4 %copy-start.2 = (bf16[256,1024]{1,0:T(8,128)(2,1)}, bf16[256,1024]{1,0:T(8,128)(2,1)S(1)}, u32[]{:S(2)}) copy-start(bf16[256,1024]{1,0:T(8,128)(2,1)S(1)} %collective-permute-done.8.refs_8_) | copy-start | bytes 1572868
  36.2 17.7 %collective-permute-start.12 = (bf16[256,1024]{1,0:T(8,128)(2,1)}, bf16[256,1024]{1,0:T(8,128)(2,1)S(1)}, u32[]{:S(2)}, u32[]{:S(2)}) collective-permute-start(bf16[256,1024]{1,0:T(8,128)(2,1)} %bitcast.7.refs_9_), channel_id=1, source_target_pairs={{96,0},{0,32},{32,64},{64,96},{25,1},{1,9},{9,17},{17,25},{98,2},{... | collective-permute-start | bytes 1572872 | tf_op jit(solution)/shard_map/ppermute | solution.py:51
  36.3 24.3 %copy-start.3 = (bf16[256,1024]{1,0:T(8,128)(2,1)}, bf16[256,1024]{1,0:T(8,128)(2,1)S(1)}, u32[]{:S(2)}) copy-start(bf16[256,1024]{1,0:T(8,128)(2,1)S(1)} %collective-permute-done.10.refs_10_) | copy-start | bytes 1572868
  36.3 24.3 %collective-permute-start.9 = (bf16[256,1024]{1,0:T(8,128)(2,1)S(1)}, bf16[256,1024]{1,0:T(8,128)(2,1)S(1)}, u32[]{:S(2)}, u32[]{:S(2)}) collective-permute-start(bf16[256,1024]{1,0:T(8,128)(2,1)S(1)} %collective-permute-done.8.refs_8_), channel_id=1, source_target_pairs={{96,0},{0,32},{32,64},{64,96},{25,1},{1,9},{9,17},{17,25},{98,2},{... | collective-permute-start | bytes 1572872 | tf_op jit(solution)/shard_map/ppermute | solution.py:51
  44.4 17.7 %collective-permute-start.11 = (bf16[256,1024]{1,0:T(8,128)(2,1)S(1)}, bf16[256,1024]{1,0:T(8,128)(2,1)}, u32[]{:S(2)}, u32[]{:S(2)}) collective-permute-start(bf16[256,1024]{1,0:T(8,128)(2,1)S(1)} %collective-permute-done.10.refs_10_), channel_id=1, source_target_pairs={{32,0},{64,32},{96,64},{0,96},{9,1},{17,9},{25,17},{1,25},{34,2},{... | collective-permute-start | bytes 1572872 | tf_op jit(solution)/shard_map/ppermute | solution.py:51
  47.5 13.1 %collective-permute-start.6 = (bf16[512,256]{1,0:T(8,128)(2,1)S(1)}, bf16[512,256]{1,0:T(8,128)(2,1)S(1)}, u32[]{:S(2)}, u32[]{:S(2)}) collective-permute-start(bf16[512,256]{1,0:T(8,128)(2,1)S(1)} %slice.9), channel_id=1, source_target_pairs={{96,0},{0,32},{32,64},{64,96},{25,1},{1,9},{9,17},{17,25},{98,2},{... | collective-permute-start | bytes 786440 | tf_op jit(solution)/shard_map/ppermute | solution.py:51
  52.6 8.0 %collective-permute-start.4 = (bf16[512,256]{1,0:T(8,128)(2,1)S(1)}, bf16[512,256]{1,0:T(8,128)(2,1)S(1)}, u32[]{:S(2)}, u32[]{:S(2)}) collective-permute-start(bf16[512,256]{1,0:T(8,128)(2,1)S(1)} %slice.8), channel_id=1, source_target_pairs={{32,0},{64,32},{96,64},{0,96},{9,1},{17,9},{25,17},{1,25},{34,2},{... | collective-permute-start | bytes 786440 | tf_op jit(solution)/shard_map/ppermute | solution.py:51
  67.2 9.6 %collective-permute-start.13 = (bf16[72,3072]{1,0:T(8,128)(2,1)S(1)}, bf16[72,3072]{1,0:T(8,128)(2,1)S(1)}, u32[]{:S(2)}, u32[]{:S(2)}) collective-permute-start(bf16[72,3072]{1,0:T(8,128)(2,1)S(1)} %get-tuple-element.51), channel_id=1, source_target_pairs={{24,0},{0,8},{8,16},{16,24},{97,1},{1,33},{33,65},{65,97},{26,2},{... | collective-permute-start | bytes 1327112 | tf_op jit(solution)/shard_map/ppermute | solution.py:51
  68.4 13.2 %collective-permute-start.14 = (bf16[72,3072]{1,0:T(8,128)(2,1)S(1)}, bf16[72,3072]{1,0:T(8,128)(2,1)S(1)}, u32[]{:S(2)}, u32[]{:S(2)}) collective-permute-start(bf16[72,3072]{1,0:T(8,128)(2,1)S(1)} %get-tuple-element.52), channel_id=1, source_target_pairs={{16,0},{24,8},{0,16},{8,24},{65,1},{97,33},{1,65},{33,97},{18,2},{... | collective-permute-start | bytes 1327112 | tf_op jit(solution)/shard_map/ppermute | solution.py:51
  70.8 10.8 %collective-permute-start.15 = (bf16[72,3072]{1,0:T(8,128)(2,1)S(1)}, bf16[72,3072]{1,0:T(8,128)(2,1)S(1)}, u32[]{:S(2)}, u32[]{:S(2)}) collective-permute-start(bf16[72,3072]{1,0:T(8,128)(2,1)S(1)} %get-tuple-element.53), channel_id=1, source_target_pairs={{8,0},{16,8},{24,16},{0,24},{33,1},{65,33},{97,65},{1,97},{10,2},{... | collective-permute-start | bytes 1327112 | tf_op jit(solution)/shard_map/ppermute | solution.py:51
  75.6 10.7 %collective-permute-start.19 = (bf16[72,3072]{1,0:T(8,128)(2,1)S(1)}, bf16[72,3072]{1,0:T(8,128)(2,1)S(1)}, u32[]{:S(2)}, u32[]{:S(2)}) collective-permute-start(bf16[72,3072]{1,0:T(8,128)(2,1)S(1)} %get-tuple-element.55), channel_id=1, source_target_pairs={{24,0},{0,8},{8,16},{16,24},{97,1},{1,33},{33,65},{65,97},{26,2},{... | collective-permute-start | bytes 1327112 | tf_op jit(solution)/shard_map/ppermute | solution.py:51
  75.7 15.4 %collective-permute-start.20 = (bf16[72,3072]{1,0:T(8,128)(2,1)S(1)}, bf16[72,3072]{1,0:T(8,128)(2,1)S(1)}, u32[]{:S(2)}, u32[]{:S(2)}) collective-permute-start(bf16[72,3072]{1,0:T(8,128)(2,1)S(1)} %get-tuple-element.56), channel_id=1, source_target_pairs={{16,0},{24,8},{0,16},{8,24},{65,1},{97,33},{1,65},{33,97},{18,2},{... | collective-permute-start | bytes 1327112 | tf_op jit(solution)/shard_map/ppermute | solution.py:51
  76.8 14.3 %collective-permute-start.21 = (bf16[72,3072]{1,0:T(8,128)(2,1)S(1)}, bf16[72,3072]{1,0:T(8,128)(2,1)S(1)}, u32[]{:S(2)}, u32[]{:S(2)}) collective-permute-start(bf16[72,3072]{1,0:T(8,128)(2,1)S(1)} %get-tuple-element.57), channel_id=1, source_target_pairs={{8,0},{16,8},{24,16},{0,24},{33,1},{65,33},{97,65},{1,97},{10,2},{... | collective-permute-start | bytes 1327112 | tf_op jit(solution)/shard_map/ppermute | solution.py:51
  82.0 13.8 %collective-permute-start.18 = (bf16[72,3072]{1,0:T(8,128)(2,1)S(1)}, bf16[72,3072]{1,0:T(8,128)(2,1)S(1)}, u32[]{:S(2)}, u32[]{:S(2)}) collective-permute-start(bf16[72,3072]{1,0:T(8,128)(2,1)S(1)} %shard_map.114.refs_0_), channel_id=1, source_target_pairs={{24,0},{0,8},{8,16},{16,24},{97,1},{1,33},{33,65},{65,97},{26,2},{... | collective-permute-start | bytes 1327112 | tf_op jit(solution)/shard_map/ppermute | solution.py:51
  83.1 17.5 %collective-permute-start.17 = (bf16[72,3072]{1,0:T(8,128)(2,1)S(1)}, bf16[72,3072]{1,0:T(8,128)(2,1)S(1)}, u32[]{:S(2)}, u32[]{:S(2)}) collective-permute-start(bf16[72,3072]{1,0:T(8,128)(2,1)S(1)} %shard_map.114.refs_0_), channel_id=1, source_target_pairs={{16,0},{24,8},{0,16},{8,24},{65,1},{97,33},{1,65},{33,97},{18,2},{... | collective-permute-start | bytes 1327112 | tf_op jit(solution)/shard_map/ppermute | solution.py:51
  86.3 14.4 %collective-permute-start.16 = (bf16[72,3072]{1,0:T(8,128)(2,1)S(1)}, bf16[72,3072]{1,0:T(8,128)(2,1)S(1)}, u32[]{:S(2)}, u32[]{:S(2)}) collective-permute-start(bf16[72,3072]{1,0:T(8,128)(2,1)S(1)} %shard_map.114.refs_0_), channel_id=1, source_target_pairs={{8,0},{16,8},{24,16},{0,24},{33,1},{65,33},{97,65},{1,97},{10,2},{... | collective-permute-start | bytes 1327112 | tf_op jit(solution)/shard_map/ppermute | solution.py:51
  91.5 13.8 %collective-permute-start.24 = (bf16[72,3072]{1,0:T(8,128)(2,1)S(1)}, bf16[72,3072]{1,0:T(8,128)(2,1)S(1)}, u32[]{:S(2)}, u32[]{:S(2)}) collective-permute-start(bf16[72,3072]{1,0:T(8,128)(2,1)S(1)} %shard_map.115.refs_4_), channel_id=1, source_target_pairs={{24,0},{0,8},{8,16},{16,24},{97,1},{1,33},{33,65},{65,97},{26,2},{... | collective-permute-start | bytes 1327112 | tf_op jit(solution)/shard_map/ppermute | solution.py:51
  93.1 17.0 %collective-permute-start.23 = (bf16[72,3072]{1,0:T(8,128)(2,1)S(1)}, bf16[72,3072]{1,0:T(8,128)(2,1)S(1)}, u32[]{:S(2)}, u32[]{:S(2)}) collective-permute-start(bf16[72,3072]{1,0:T(8,128)(2,1)S(1)} %shard_map.115.refs_4_), channel_id=1, source_target_pairs={{16,0},{24,8},{0,16},{8,24},{65,1},{97,33},{1,65},{33,97},{18,2},{... | collective-permute-start | bytes 1327112 | tf_op jit(solution)/shard_map/ppermute | solution.py:51
  95.8 14.4 %collective-permute-start.22 = (bf16[72,3072]{1,0:T(8,128)(2,1)S(1)}, bf16[72,3072]{1,0:T(8,128)(2,1)S(1)}, u32[]{:S(2)}, u32[]{:S(2)}) collective-permute-start(bf16[72,3072]{1,0:T(8,128)(2,1)S(1)} %shard_map.115.refs_4_), channel_id=1, source_target_pairs={{8,0},{16,8},{24,16},{0,24},{33,1},{65,33},{97,65},{1,97},{10,2},{... | collective-permute-start | bytes 1327112 | tf_op jit(solution)/shard_map/ppermute | solution.py:51
  154.3 50.7 %collective-permute-start.25 = (bf16[4,288,1024]{2,1,0:T(8,128)(2,1)S(1)}, bf16[4,288,1024]{2,1,0:T(8,128)(2,1)S(1)}, u32[]{:S(2)}, u32[]{:S(2)}) collective-permute-start(bf16[4,288,1024]{2,1,0:T(8,128)(2,1)S(1)} %bitcast.15), channel_id=1, source_target_pairs={{0,1},{1,0},{2,3},{3,2},{4,5},{5,4},{6,7},{7,6},{8,9},{9,8},{10,11... | collective-permute-start | bytes 7077896 | tf_op jit(solution)/shard_map/ppermute | solution.py:59
  163.6 21.2 %collective-permute-start.26 = (bf16[768,1024]{1,0:T(8,128)(2,1)}, bf16[768,1024]{1,0:T(8,128)(2,1)S(1)}, u32[]{:S(2)}, u32[]{:S(2)}) collective-permute-start(bf16[768,1024]{1,0:T(8,128)(2,1)} %get-tuple-element.63), channel_id=1, source_target_pairs={{96,0},{0,32},{32,64},{64,96},{25,1},{1,9},{9,17},{17,25},{98,2},{... | collective-permute-start | bytes 4718600 | tf_op jit(solution)/shard_map/ppermute | solution.py:51
  165.1 19.9 %collective-permute-start.28 = (bf16[768,1024]{1,0:T(8,128)(2,1)}, bf16[768,1024]{1,0:T(8,128)(2,1)S(1)}, u32[]{:S(2)}, u32[]{:S(2)}) collective-permute-start(bf16[768,1024]{1,0:T(8,128)(2,1)} %get-tuple-element.65), channel_id=1, source_target_pairs={{32,0},{64,32},{96,64},{0,96},{9,1},{17,9},{25,17},{1,25},{34,2},{... | collective-permute-start | bytes 4718600 | tf_op jit(solution)/shard_map/ppermute | solution.py:51
  166.6 36.3 %collective-permute-start.27 = (bf16[768,1024]{1,0:T(8,128)(2,1)S(1)}, bf16[768,1024]{1,0:T(8,128)(2,1)S(1)}, u32[]{:S(2)}, u32[]{:S(2)}) collective-permute-start(bf16[768,1024]{1,0:T(8,128)(2,1)S(1)} %copy-done.9), channel_id=1, source_target_pairs={{64,0},{96,32},{0,64},{32,96},{17,1},{25,9},{1,17},{9,25},{66,2},{... | collective-permute-start | bytes 4718600 | tf_op jit(solution)/shard_map/ppermute | solution.py:51
  (8 other events, 58.7 us)
